TPU v7x, 32 devices: a whole 2x2x4 slice. The times are simulated.
32 devices in a mesh: row: 8 (over z, core), col: 4 (over y, x).
Axes of the slice: x: 2, y: 2, z: 4, core: 2. Of those that a mesh axis runs over, the one named last changes fastest.
Arguments:
- patches: bfloat16 [3, 128, 128, 1024], P(None, 'row', 'col'), may hold values from -6 to 6
- registers: bfloat16 [3, 8, 1024], replicated, may hold values from -20 to 20
Outputs:
- patch_out: bfloat16 [128, 128, 1024], P('row', 'col')
- register_out: bfloat16 [8, 1024], replicated
All inputs are finite; a program needn't handle non-finite values.
Results may differ from a plain program's by a relative error of at most 0.004.
Values may be sent and summed in bfloat16 or wider, within the bound.
No kernel may reach another device: no remote copies, remote signals or barrier semaphores. Data moves between devices by JAX's collectives and lax.ppermute only.
A program may use at most 64 MiB of HBM per device.

v0:
```python
import jax
import jax.numpy as jnp
from jax import lax
from jax.sharding import PartitionSpec as P

HEADS = 16
RADIUS = 8


def padded_2(cells, sides, width):
    for axis, dim in sides:
        count = lax.axis_size(axis)
        ends = count - 1
        head = lax.slice_in_dim(cells, 0, width, axis=dim)
        tail = lax.slice_in_dim(cells, cells.shape[dim] - width, cells.shape[dim], axis=dim)
        cells = jnp.concatenate(
            [
                lax.ppermute(tail, axis, [(i, (i + 1) % count) for i in range(ends)]),
                cells,
                lax.ppermute(head, axis, [((i + 1) % count, i) for i in range(ends)]),
            ],
            axis=dim,
        )
    return cells


def local(patches, registers):
    tile_rows = patches.shape[1]
    tile_cols = patches.shape[2]
    channels = patches.shape[3]
    head_size = channels // HEADS
    reg_count = registers.shape[1]
    score_scale = head_size ** (-0.5)
    cells = tile_rows * tile_cols
    own_keys = patches[1].reshape(cells, HEADS, head_size)
    own_values = patches[2].reshape(cells, HEADS, head_size)
    reg_queries = registers[0].reshape(reg_count, HEADS, head_size)
    reg_keys = registers[1].reshape(reg_count, HEADS, head_size)
    reg_values = registers[2].reshape(reg_count, HEADS, head_size)
    partial_scores = (
        jnp.einsum("rhd,qhd->hrq", reg_queries, own_keys, preferred_element_type=jnp.float32)
        * score_scale
    )
    local_high = jnp.max(partial_scores, axis=2)
    partial_weights = jnp.exp(partial_scores - local_high[..., None])
    local_totals = jnp.sum(partial_weights, axis=2)
    local_weighted = jnp.einsum(
        "hrq,qhd->hrd",
        partial_weights.astype(jnp.bfloat16),
        own_values,
        preferred_element_type=jnp.float32,
    )
    global_high = lax.pmax(local_high, ("row", "col"))
    factor = jnp.exp(local_high - global_high)
    global_totals, global_weighted = lax.psum(
        (local_totals * factor, local_weighted * factor[..., None]), ("row", "col")
    )
    self_scores = (
        jnp.einsum("rhd,shd->hrs", reg_queries, reg_keys, preferred_element_type=jnp.float32)
        * score_scale
    )
    highest = jnp.maximum(global_high, jnp.max(self_scores, axis=2))
    rescale = jnp.exp(global_high - highest)
    self_weights = jnp.exp(self_scores - highest[..., None])
    denominator = global_totals * rescale + jnp.sum(self_weights, axis=2)
    numerator = global_weighted * rescale[..., None] + jnp.einsum(
        "hrs,shd->hrd",
        self_weights.astype(jnp.bfloat16),
        reg_values,
        preferred_element_type=jnp.float32,
    )
    register_out = (
        jnp.transpose(numerator / denominator[..., None], (1, 0, 2))
        .reshape(reg_count, channels)
        .astype(jnp.bfloat16)
    )
    keys_values = patches[1:3]
    padded = padded_2(keys_values, (("row", 1), ("col", 2)), RADIUS)
    span_rows = tile_rows + 2 * RADIUS
    span_cols = tile_cols + 2 * RADIUS
    spots = span_rows * span_cols
    grid_rows = tile_rows * lax.axis_size("row")
    grid_cols = tile_cols * lax.axis_size("col")
    query_ids = jnp.arange(cells, dtype=jnp.int32)
    key_ids = jnp.arange(spots, dtype=jnp.int32)
    key_row = key_ids // span_cols
    key_col = key_ids % span_cols
    row_gap = key_row[None, :] - RADIUS - (query_ids // tile_cols)[:, None]
    col_gap = key_col[None, :] - RADIUS - (query_ids % tile_cols)[:, None]
    global_row = lax.axis_index("row") * tile_rows + key_row - RADIUS
    global_col = lax.axis_index("col") * tile_cols + key_col - RADIUS
    in_grid = (
        (global_row >= 0) & (global_row < grid_rows) & (global_col >= 0) & (global_col < grid_cols)
    )
    inside = (jnp.abs(row_gap) <= RADIUS) & (jnp.abs(col_gap) <= RADIUS) & in_grid[None, :]
    flat_queries = patches[0].reshape(cells, channels)
    flat_keys = padded[0].reshape(spots, channels)
    flat_values = padded[1].reshape(spots, channels)

    def one_head(head_index):
        start = head_index * head_size
        head_queries = lax.dynamic_slice_in_dim(flat_queries, start, head_size, 1)
        head_keys = lax.dynamic_slice_in_dim(flat_keys, start, head_size, 1)
        head_values = lax.dynamic_slice_in_dim(flat_values, start, head_size, 1)
        head_reg_keys = lax.dynamic_slice_in_dim(registers[1], start, head_size, 1)
        head_reg_values = lax.dynamic_slice_in_dim(registers[2], start, head_size, 1)
        scores = (
            jnp.einsum("qd,kd->qk", head_queries, head_keys, preferred_element_type=jnp.float32)
            * score_scale
        )
        scores = jnp.where(inside, scores, -jnp.inf)
        reg_scores = (
            jnp.einsum("qd,rd->qr", head_queries, head_reg_keys, preferred_element_type=jnp.float32)
            * score_scale
        )
        top_score = jnp.maximum(jnp.max(scores, axis=1), jnp.max(reg_scores, axis=1))
        weights = jnp.exp(scores - top_score[:, None])
        reg_weights = jnp.exp(reg_scores - top_score[:, None])
        totals = jnp.sum(weights, axis=1) + jnp.sum(reg_weights, axis=1)
        summed = jnp.dot(
            weights.astype(jnp.bfloat16), head_values, preferred_element_type=jnp.float32
        )
        summed = summed + jnp.dot(
            reg_weights.astype(jnp.bfloat16), head_reg_values, preferred_element_type=jnp.float32
        )
        return summed / totals[:, None]

    per_head = lax.map(one_head, jnp.arange(HEADS, dtype=jnp.int32))
    patch_out = (
        jnp.transpose(per_head, (1, 0, 2))
        .reshape(tile_rows, tile_cols, channels)
        .astype(jnp.bfloat16)
    )
    return (patch_out, register_out)


def solution(mesh):
    in_specs = (P(None, "row", "col", None), P())
    out_specs = (P("row", "col", None), P())
    return jax.shard_map(local, mesh=mesh, in_specs=in_specs, out_specs=out_specs, check_vma=False)
```

profile of v0, /device:TPU:19, one launch (start us, length us, event | category | flops | bytes accessed | tf_op | source)
XLA Modules:
  0.0 290.5 jit_solution(16762635928399057182)
XLA Ops:
  0.6 3.3 %fusion.91 = (bf16[2,8,32,1024]{3,2,1,0:T(8,128)(2,1)}, bf16[2,8,32,1024]{3,2,1,0:T(8,128)(2,1)}) fusion(bf16[3,16,32,1024]{3,2,1,0:T(8,128)(2,1)} %param.4), kind=kLoop, calls=%fused_computation.102 | loop fusion | bytes 4194304 | tf_op jit(solution)/shard_map/slice | solution.py:15
  4.0 3.9 %collective-permute-start = (bf16[2,8,32,1024]{3,2,1,0:T(8,128)(2,1)}, bf16[2,8,32,1024]{3,2,1,0:T(8,128)(2,1)S(1)}, u32[]{:S(2)}, u32[]{:S(2)}) collective-permute-start(bf16[2,8,32,1024]{3,2,1,0:T(8,128)(2,1)} %get-tuple-element.119), channel_id=1, source_target_pairs={{0,4},{4,8},{8,12},{12,16},{16,20},{20,24},{24,28},{1,5},{5,9},{9,... | collective-permute-start | bytes 3145736 | tf_op jit(solution)/shard_map/ppermute | solution.py:18
  10.7 3.7 %fusion.90 = (bf16[1,16,32,1024]{3,2,1,0:T(8,128)(2,1)}, bf16[1,16,32,1024]{3,2,1,0:T(8,128)(2,1)}, bf16[1,16,32,1024]{3,2,1,0:T(8,128)(2,1)}) fusion(bf16[3,16,32,1024]{3,2,1,0:T(8,128)(2,1)} %param.4), kind=kLoop, calls=%fused_computation.101 | loop fusion | bytes 6291456 | tf_op jit(solution)/shard_map/slice | solution.py:35
  14.4 4.0 %reshape_squeeze.28 = bf16[512,16,64]{2,1,0:T(8,128)(2,1)} reshape(bf16[1,16,32,1024]{3,2,1,0:T(8,128)(2,1)} %get-tuple-element.116) | data formatting | bytes 2097152 | tf_op jit(solution)/shard_map/reshape;squeeze | solution.py:35
  18.5 4.1 %reshape_squeeze.29 = bf16[512,16,64]{2,1,0:T(8,128)(2,1)} reshape(bf16[1,16,32,1024]{3,2,1,0:T(8,128)(2,1)} %get-tuple-element.118) | data formatting | bytes 2097152 | tf_op jit(solution)/shard_map/reshape;squeeze | solution.py:36
  22.6 2.5 fusion.93
  25.1 39.2 %pmax.7 = f32[16,8]{1,0:T(8,128)S(1)} all-reduce(f32[16,8]{1,0:T(8,128)S(1)} %get-tuple-element.125), channel_id=1, replica_groups=mesh['row'=8,'col'=4] {'row','col'}, use_global_device_ids=true, to_apply=%region_7.8 | all-reduce | flops 128 | bytes 1024 | tf_op jit(solution)/shard_map/pmax | solution.py:53
  65.2 2.7 pad_maximum_fusion.3
  68.0 3.1 %collective-permute-start.2 = (bf16[2,32,8,1024]{3,2,1,0:T(8,128)(2,1)}, bf16[2,32,8,1024]{3,2,1,0:T(8,128)(2,1)}, u32[]{:S(2)}, u32[]{:S(2)}) collective-permute-start(bf16[2,32,8,1024]{3,2,1,0:T(8,128)(2,1)} %get-tuple-element.114), channel_id=1, source_target_pairs={{0,1},{1,2},{2,3},{4,5},{5,6},{6,7},{8,9},{9,10},{10,11},{12,13},{... | collective-permute-start | bytes 3145736 | tf_op jit(solution)/shard_map/ppermute | solution.py:18
  71.1 3.2 %collective-permute-start.3 = (bf16[2,32,8,1024]{3,2,1,0:T(8,128)(2,1)}, bf16[2,32,8,1024]{3,2,1,0:T(8,128)(2,1)}, u32[]{:S(2)}, u32[]{:S(2)}) collective-permute-start(bf16[2,32,8,1024]{3,2,1,0:T(8,128)(2,1)} %get-tuple-element.115), channel_id=1, source_target_pairs={{1,0},{2,1},{3,2},{5,4},{6,5},{7,6},{9,8},{10,9},{11,10},{13,12},{... | collective-permute-start | bytes 3145736 | tf_op jit(solution)/shard_map/ppermute | solution.py:20
  75.8 74.4 %all-reduce = (f32[16,8,64]{2,1,0:T(8,128)S(1)}, f32[16,8]{1,0:T(8,128)S(1)}) all-reduce(f32[16,8,64]{2,1,0:T(8,128)S(1)} %fusion.47, f32[16,8]{1,0:T(8,128)S(1)} %get-tuple-element.104), channel_id=1, replica_groups=mesh['row'=8,'col'=4] {'row','col'}, use_global_device_ids=true, to_apply=%region_8.9 | all-reduce | flops 8320 | bytes 66560 | tf_op jit(solution)/shard_map/psum | solution.py:55
  152.9 4.9 %pad_maximum_fusion = bf16[2,32,48,1024]{3,2,1,0:T(8,128)(2,1)S(1)} fusion(bf16[2,32,8,1024]{3,2,1,0:T(8,128)(2,1)} %collective-permute-done.3, bf16[2,8,32,1024]{3,2,1,0:T(8,128)(2,1)} %collective-permute-done.1, bf16[2,16,32,1024]{3,2,1,0:T(8,128)(2,1)S(1)} %slice.49, bf16[2,8,32,1024]{3,2,1,0:T(8,128)(2,1)S(1)} %collective-permute-done, ...), kind=kLoop, calls=%fused_computation.34 | loop fusion | flops 31457280 | bytes 12582912 | tf_op jit(solution)/shard_map/concatenate | solution.py:16
  157.9 2.7 fusion.89
  160.6 124.6 %while.11 = (s32[]{:T(128)}, bf16[16,512,64]{1,2,0:T(8,128)(2,1)}, s32[16]{0:T(128)S(1)}, bf16[512,1024]{1,0:T(8,128)(2,1)}, bf16[1536,1024]{1,0:T(8,128)(2,1)},...) while((s32[]{:T(128)}, bf16[16,512,64]{1,2,0:T(8,128)(2,1)}, ...), condition=%wide.region_5.0_spmd.clone, body=%wide.region_0.5_spmd.clone.sunk | while | flops 214260736 | bytes 11049175 | solution.py:128
  161.7 3.1 %fusion.112 = (f32[512]{0:T(512)S(1)}, f32[512,1536]{1,0:T(8,128)S(1)}) fusion(bf16[1536,1024]{1,0:T(8,128)(2,1)} %get-tuple-element.254, s32[]{:T(128)S(6)} %select_n.92, bf16[512,1024]{1,0:T(8,128)(2,1)} %get-tuple-element.253, pred[1536]{0:T(1024)(128)(4,1)S(1)} %get-tuple-element.261, s32[512]{0:T(512)S(1)} %get-tuple-element.259, ...), kind=kOutput, calls=%fused_computation.98.clone.1 | convolution fusion | flops 109313536 | bytes 3691008 | tf_op jit(solution)/shard_map/while/body/eval_jaxpr/qd,kd->qk/dot_general | solution.py:108
  169.5 3.1 %fusion.112 = (f32[512]{0:T(512)S(1)}, f32[512,1536]{1,0:T(8,128)S(1)}) fusion(bf16[1536,1024]{1,0:T(8,128)(2,1)} %get-tuple-element.254, s32[]{:T(128)S(6)} %select_n.92, bf16[512,1024]{1,0:T(8,128)(2,1)} %get-tuple-element.253, pred[1536]{0:T(1024)(128)(4,1)S(1)} %get-tuple-element.261, s32[512]{0:T(512)S(1)} %get-tuple-element.259, ...), kind=kOutput, calls=%fused_computation.98.clone.1 | convolution fusion | flops 109313536 | bytes 3691008 | tf_op jit(solution)/shard_map/while/body/eval_jaxpr/qd,kd->qk/dot_general | solution.py:108
  177.3 3.1 %fusion.112 = (f32[512]{0:T(512)S(1)}, f32[512,1536]{1,0:T(8,128)S(1)}) fusion(bf16[1536,1024]{1,0:T(8,128)(2,1)} %get-tuple-element.254, s32[]{:T(128)S(6)} %select_n.92, bf16[512,1024]{1,0:T(8,128)(2,1)} %get-tuple-element.253, pred[1536]{0:T(1024)(128)(4,1)S(1)} %get-tuple-element.261, s32[512]{0:T(512)S(1)} %get-tuple-element.259, ...), kind=kOutput, calls=%fused_computation.98.clone.1 | convolution fusion | flops 109313536 | bytes 3691008 | tf_op jit(solution)/shard_map/while/body/eval_jaxpr/qd,kd->qk/dot_general | solution.py:108
  185.1 3.1 %fusion.112 = (f32[512]{0:T(512)S(1)}, f32[512,1536]{1,0:T(8,128)S(1)}) fusion(bf16[1536,1024]{1,0:T(8,128)(2,1)} %get-tuple-element.254, s32[]{:T(128)S(6)} %select_n.92, bf16[512,1024]{1,0:T(8,128)(2,1)} %get-tuple-element.253, pred[1536]{0:T(1024)(128)(4,1)S(1)} %get-tuple-element.261, s32[512]{0:T(512)S(1)} %get-tuple-element.259, ...), kind=kOutput, calls=%fused_computation.98.clone.1 | convolution fusion | flops 109313536 | bytes 3691008 | tf_op jit(solution)/shard_map/while/body/eval_jaxpr/qd,kd->qk/dot_general | solution.py:108
  192.9 3.1 %fusion.112 = (f32[512]{0:T(512)S(1)}, f32[512,1536]{1,0:T(8,128)S(1)}) fusion(bf16[1536,1024]{1,0:T(8,128)(2,1)} %get-tuple-element.254, s32[]{:T(128)S(6)} %select_n.92, bf16[512,1024]{1,0:T(8,128)(2,1)} %get-tuple-element.253, pred[1536]{0:T(1024)(128)(4,1)S(1)} %get-tuple-element.261, s32[512]{0:T(512)S(1)} %get-tuple-element.259, ...), kind=kOutput, calls=%fused_computation.98.clone.1 | convolution fusion | flops 109313536 | bytes 3691008 | tf_op jit(solution)/shard_map/while/body/eval_jaxpr/qd,kd->qk/dot_general | solution.py:108
  200.7 3.1 %fusion.112 = (f32[512]{0:T(512)S(1)}, f32[512,1536]{1,0:T(8,128)S(1)}) fusion(bf16[1536,1024]{1,0:T(8,128)(2,1)} %get-tuple-element.254, s32[]{:T(128)S(6)} %select_n.92, bf16[512,1024]{1,0:T(8,128)(2,1)} %get-tuple-element.253, pred[1536]{0:T(1024)(128)(4,1)S(1)} %get-tuple-element.261, s32[512]{0:T(512)S(1)} %get-tuple-element.259, ...), kind=kOutput, calls=%fused_computation.98.clone.1 | convolution fusion | flops 109313536 | bytes 3691008 | tf_op jit(solution)/shard_map/while/body/eval_jaxpr/qd,kd->qk/dot_general | solution.py:108
  208.5 3.1 %fusion.112 = (f32[512]{0:T(512)S(1)}, f32[512,1536]{1,0:T(8,128)S(1)}) fusion(bf16[1536,1024]{1,0:T(8,128)(2,1)} %get-tuple-element.254, s32[]{:T(128)S(6)} %select_n.92, bf16[512,1024]{1,0:T(8,128)(2,1)} %get-tuple-element.253, pred[1536]{0:T(1024)(128)(4,1)S(1)} %get-tuple-element.261, s32[512]{0:T(512)S(1)} %get-tuple-element.259, ...), kind=kOutput, calls=%fused_computation.98.clone.1 | convolution fusion | flops 109313536 | bytes 3691008 | tf_op jit(solution)/shard_map/while/body/eval_jaxpr/qd,kd->qk/dot_general | solution.py:108
  216.3 3.1 %fusion.112 = (f32[512]{0:T(512)S(1)}, f32[512,1536]{1,0:T(8,128)S(1)}) fusion(bf16[1536,1024]{1,0:T(8,128)(2,1)} %get-tuple-element.254, s32[]{:T(128)S(6)} %select_n.92, bf16[512,1024]{1,0:T(8,128)(2,1)} %get-tuple-element.253, pred[1536]{0:T(1024)(128)(4,1)S(1)} %get-tuple-element.261, s32[512]{0:T(512)S(1)} %get-tuple-element.259, ...), kind=kOutput, calls=%fused_computation.98.clone.1 | convolution fusion | flops 109313536 | bytes 3691008 | tf_op jit(solution)/shard_map/while/body/eval_jaxpr/qd,kd->qk/dot_general | solution.py:108
  224.1 3.1 %fusion.112 = (f32[512]{0:T(512)S(1)}, f32[512,1536]{1,0:T(8,128)S(1)}) fusion(bf16[1536,1024]{1,0:T(8,128)(2,1)} %get-tuple-element.254, s32[]{:T(128)S(6)} %select_n.92, bf16[512,1024]{1,0:T(8,128)(2,1)} %get-tuple-element.253, pred[1536]{0:T(1024)(128)(4,1)S(1)} %get-tuple-element.261, s32[512]{0:T(512)S(1)} %get-tuple-element.259, ...), kind=kOutput, calls=%fused_computation.98.clone.1 | convolution fusion | flops 109313536 | bytes 3691008 | tf_op jit(solution)/shard_map/while/body/eval_jaxpr/qd,kd->qk/dot_general | solution.py:108
  231.8 3.1 %fusion.112 = (f32[512]{0:T(512)S(1)}, f32[512,1536]{1,0:T(8,128)S(1)}) fusion(bf16[1536,1024]{1,0:T(8,128)(2,1)} %get-tuple-element.254, s32[]{:T(128)S(6)} %select_n.92, bf16[512,1024]{1,0:T(8,128)(2,1)} %get-tuple-element.253, pred[1536]{0:T(1024)(128)(4,1)S(1)} %get-tuple-element.261, s32[512]{0:T(512)S(1)} %get-tuple-element.259, ...), kind=kOutput, calls=%fused_computation.98.clone.1 | convolution fusion | flops 109313536 | bytes 3691008 | tf_op jit(solution)/shard_map/while/body/eval_jaxpr/qd,kd->qk/dot_general | solution.py:108
  239.6 3.1 %fusion.112 = (f32[512]{0:T(512)S(1)}, f32[512,1536]{1,0:T(8,128)S(1)}) fusion(bf16[1536,1024]{1,0:T(8,128)(2,1)} %get-tuple-element.254, s32[]{:T(128)S(6)} %select_n.92, bf16[512,1024]{1,0:T(8,128)(2,1)} %get-tuple-element.253, pred[1536]{0:T(1024)(128)(4,1)S(1)} %get-tuple-element.261, s32[512]{0:T(512)S(1)} %get-tuple-element.259, ...), kind=kOutput, calls=%fused_computation.98.clone.1 | convolution fusion | flops 109313536 | bytes 3691008 | tf_op jit(solution)/shard_map/while/body/eval_jaxpr/qd,kd->qk/dot_general | solution.py:108
  247.4 3.1 %fusion.112 = (f32[512]{0:T(512)S(1)}, f32[512,1536]{1,0:T(8,128)S(1)}) fusion(bf16[1536,1024]{1,0:T(8,128)(2,1)} %get-tuple-element.254, s32[]{:T(128)S(6)} %select_n.92, bf16[512,1024]{1,0:T(8,128)(2,1)} %get-tuple-element.253, pred[1536]{0:T(1024)(128)(4,1)S(1)} %get-tuple-element.261, s32[512]{0:T(512)S(1)} %get-tuple-element.259, ...), kind=kOutput, calls=%fused_computation.98.clone.1 | convolution fusion | flops 109313536 | bytes 3691008 | tf_op jit(solution)/shard_map/while/body/eval_jaxpr/qd,kd->qk/dot_general | solution.py:108
  255.2 3.1 %fusion.112 = (f32[512]{0:T(512)S(1)}, f32[512,1536]{1,0:T(8,128)S(1)}) fusion(bf16[1536,1024]{1,0:T(8,128)(2,1)} %get-tuple-element.254, s32[]{:T(128)S(6)} %select_n.92, bf16[512,1024]{1,0:T(8,128)(2,1)} %get-tuple-element.253, pred[1536]{0:T(1024)(128)(4,1)S(1)} %get-tuple-element.261, s32[512]{0:T(512)S(1)} %get-tuple-element.259, ...), kind=kOutput, calls=%fused_computation.98.clone.1 | convolution fusion | flops 109313536 | bytes 3691008 | tf_op jit(solution)/shard_map/while/body/eval_jaxpr/qd,kd->qk/dot_general | solution.py:108
  263.0 3.1 %fusion.112 = (f32[512]{0:T(512)S(1)}, f32[512,1536]{1,0:T(8,128)S(1)}) fusion(bf16[1536,1024]{1,0:T(8,128)(2,1)} %get-tuple-element.254, s32[]{:T(128)S(6)} %select_n.92, bf16[512,1024]{1,0:T(8,128)(2,1)} %get-tuple-element.253, pred[1536]{0:T(1024)(128)(4,1)S(1)} %get-tuple-element.261, s32[512]{0:T(512)S(1)} %get-tuple-element.259, ...), kind=kOutput, calls=%fused_computation.98.clone.1 | convolution fusion | flops 109313536 | bytes 3691008 | tf_op jit(solution)/shard_map/while/body/eval_jaxpr/qd,kd->qk/dot_general | solution.py:108
  270.8 3.1 %fusion.112 = (f32[512]{0:T(512)S(1)}, f32[512,1536]{1,0:T(8,128)S(1)}) fusion(bf16[1536,1024]{1,0:T(8,128)(2,1)} %get-tuple-element.254, s32[]{:T(128)S(6)} %select_n.92, bf16[512,1024]{1,0:T(8,128)(2,1)} %get-tuple-element.253, pred[1536]{0:T(1024)(128)(4,1)S(1)} %get-tuple-element.261, s32[512]{0:T(512)S(1)} %get-tuple-element.259, ...), kind=kOutput, calls=%fused_computation.98.clone.1 | convolution fusion | flops 109313536 | bytes 3691008 | tf_op jit(solution)/shard_map/while/body/eval_jaxpr/qd,kd->qk/dot_general | solution.py:108
  278.6 3.1 %fusion.112 = (f32[512]{0:T(512)S(1)}, f32[512,1536]{1,0:T(8,128)S(1)}) fusion(bf16[1536,1024]{1,0:T(8,128)(2,1)} %get-tuple-element.254, s32[]{:T(128)S(6)} %select_n.92, bf16[512,1024]{1,0:T(8,128)(2,1)} %get-tuple-element.253, pred[1536]{0:T(1024)(128)(4,1)S(1)} %get-tuple-element.261, s32[512]{0:T(512)S(1)} %get-tuple-element.259, ...), kind=kOutput, calls=%fused_computation.98.clone.1 | convolution fusion | flops 109313536 | bytes 3691008 | tf_op jit(solution)/shard_map/while/body/eval_jaxpr/qd,kd->qk/dot_general | solution.py:108
  285.2 3.0 %copy.8 = bf16[512,16,64]{2,1,0:T(8,128)(2,1)S(1)} copy(bf16[512,16,64]{0,2,1:T(8,128)(2,1)} %bitcast.22) | data formatting | bytes 2097152 | tf_op jit(solution)/shard_map/convert_element_type | solution.py:132
  288.2 2.3 convert_element_type.32
  (174 shorter events, 73.6 us)
Async XLA Ops:
  0.6 9.2 %copy-start = (bf16[3,16,32,1024]{3,2,1,0:T(8,128)(2,1)S(1)}, bf16[3,16,32,1024]{3,2,1,0:T(8,128)(2,1)}, u32[]{:S(2)}) copy-start(bf16[3,16,32,1024]{3,2,1,0:T(8,128)(2,1)} %param.4) | copy-start | bytes 9437188
  4.0 6.0 %copy-start.2 = (bf16[3,8,1024]{2,1,0:T(8,128)(2,1)S(1)}, bf16[3,8,1024]{2,1,0:T(8,128)(2,1)}, u32[]{:S(2)}) copy-start(bf16[3,8,1024]{2,1,0:T(8,128)(2,1)} %param.5) | copy-start | bytes 147460
  4.0 61.3 %collective-permute-start = (bf16[2,8,32,1024]{3,2,1,0:T(8,128)(2,1)}, bf16[2,8,32,1024]{3,2,1,0:T(8,128)(2,1)S(1)}, u32[]{:S(2)}, u32[]{:S(2)}) collective-permute-start(bf16[2,8,32,1024]{3,2,1,0:T(8,128)(2,1)} %get-tuple-element.119), channel_id=1, source_target_pairs={{0,4},{4,8},{8,12},{12,16},{16,20},{20,24},{24,28},{1,5},{5,9},{9,... | collective-permute-start | bytes 3145736 | tf_op jit(solution)/shard_map/ppermute | solution.py:18
  7.9 57.4 %collective-permute-start.1 = (bf16[2,8,32,1024]{3,2,1,0:T(8,128)(2,1)}, bf16[2,8,32,1024]{3,2,1,0:T(8,128)(2,1)}, u32[]{:S(2)}, u32[]{:S(2)}) collective-permute-start(bf16[2,8,32,1024]{3,2,1,0:T(8,128)(2,1)} %get-tuple-element.120), channel_id=1, source_target_pairs={{4,0},{8,4},{12,8},{16,12},{20,16},{24,20},{28,24},{5,1},{9,5},{13... | collective-permute-start | bytes 3145736 | tf_op jit(solution)/shard_map/ppermute | solution.py:20
  65.2 9.0 %copy-start.1 = (bf16[512,16,64]{2,1,0:T(8,128)(2,1)S(1)}, bf16[512,16,64]{2,1,0:T(8,128)(2,1)}, u32[]{:S(2)}) copy-start(bf16[512,16,64]{2,1,0:T(8,128)(2,1)} %reshape_squeeze.29) | copy-start | bytes 3145732
  68.0 84.9 %collective-permute-start.2 = (bf16[2,32,8,1024]{3,2,1,0:T(8,128)(2,1)}, bf16[2,32,8,1024]{3,2,1,0:T(8,128)(2,1)}, u32[]{:S(2)}, u32[]{:S(2)}) collective-permute-start(bf16[2,32,8,1024]{3,2,1,0:T(8,128)(2,1)} %get-tuple-element.114), channel_id=1, source_target_pairs={{0,1},{1,2},{2,3},{4,5},{5,6},{6,7},{8,9},{9,10},{10,11},{12,13},{... | collective-permute-start | bytes 3145736 | tf_op jit(solution)/shard_map/ppermute | solution.py:18
  71.1 81.8 %collective-permute-start.3 = (bf16[2,32,8,1024]{3,2,1,0:T(8,128)(2,1)}, bf16[2,32,8,1024]{3,2,1,0:T(8,128)(2,1)}, u32[]{:S(2)}, u32[]{:S(2)}) collective-permute-start(bf16[2,32,8,1024]{3,2,1,0:T(8,128)(2,1)} %get-tuple-element.115), channel_id=1, source_target_pairs={{1,0},{2,1},{3,2},{5,4},{6,5},{7,6},{9,8},{10,9},{11,10},{13,12},{... | collective-permute-start | bytes 3145736 | tf_op jit(solution)/shard_map/ppermute | solution.py:20
where the time goes:
time: 294 us; the launch traced here: 291 us
  blocking collectives  114 us (39%)
  matrix products  102 us (35%)
  local copies, waits for them, and re-layouts  34.5 us (12%)
  other arithmetic  18.4 us (6%)
  starting transfers between devices  12 us (4%)
  loops' own time  9.43 us (3%)
    psum x1, blocking collectives, local(): lax.psum((local_totals * factor, local_weighted * factor[..., None]), ('r...  74.4 us
    dot_general x16, matrix products, one_head(): jnp.einsum('qd,kd->qk', head_queries, head_keys, preferred_element_type=j...  49.7 us
    pmax x1, blocking collectives, local(): global_high = lax.pmax(local_high, ('row', 'col'))  39.2 us
    dot_general x16, matrix products, one_head(): jnp.dot(weights.astype(jnp.bfloat16), head_values, preferred_element_type...  24.3 us
    dot_general x16, matrix products, one_head(): jnp.einsum('qd,rd->qr', head_queries, head_reg_keys, preferred_element_ty...  18.3 us
    reduce_sum x32, other arithmetic, one_head(): totals = jnp.sum(weights, axis=1) + jnp.sum(reg_weights, axis=1)  9.47 us
    another operation x1, loops' own time, local(): per_head = lax.map(one_head, jnp.arange(HEADS, dtype=jnp.int32))  9.43 us
    dynamic_slice x16, local copies, waits for them, and re-layouts, local(): per_head = lax.map(one_head, jnp.arange(HEADS, dtype=jnp.int32))  8.79 us
  transfers between devices with their start and end apart: 4, of which 0 were waited for; matrix products, arithmetic and copies ran while one was open for 7% of the time, Pallas kernels for 0%

commit v1 on v0

v1 whole, which is shorter than its diff:
```python
import functools

import jax
import jax.numpy as jnp
from jax import lax
from jax.experimental import pallas as pl
from jax.experimental.pallas import tpu as pltpu
from jax.sharding import PartitionSpec as P

HEADS = 16
RADIUS = 8
FAR = -30000.0
F32 = jnp.float32
BF16 = jnp.bfloat16
NT = (((1,), (1,)), ((), ()))
NN = (((1,), (0,)), ((), ()))
TN = (((0,), (0,)), ((), ()))


def dot(a, b, dims):
    return lax.dot_general(a, b, dims, preferred_element_type=F32)


def shift(x, axis, step):
    n = lax.axis_size(axis)
    return lax.ppermute(x, axis, [(i, i + step) for i in range(n) if 0 <= i + step < n])


def key_features(rows, cols, grid_ok, tile_rows, tile_cols):
    lane = jnp.arange(128, dtype=jnp.int32)[None, :]
    far_col = (lane < tile_cols) & (jnp.abs(cols[:, None] - lane) > RADIUS)
    row_lane = lane - tile_cols
    is_row = (row_lane >= 0) & (row_lane < tile_rows)
    far_row = is_row & (jnp.abs(rows[:, None] - row_lane) > RADIUS)
    off = (lane == tile_cols + tile_rows) & ~grid_ok[:, None]
    return jnp.where(far_col | far_row | off, FAR, 0.0).astype(BF16)


def query_features(rows, cols, tile_rows, tile_cols):
    lane = jnp.arange(128, dtype=jnp.int32)[None, :]
    hit = (lane == cols[:, None]) | (lane == tile_cols + rows[:, None])
    return (hit | (lane == tile_cols + tile_rows)).astype(BF16)


def register_kernel(scale, flag_ref, reg_ref, k_ref, v_ref, out_ref):
    count = reg_ref.shape[1]
    width = reg_ref.shape[2]
    head = width // HEADS
    keys = k_ref[...].reshape(-1, width)
    values = v_ref[...].reshape(-1, width)
    lane_head = lax.broadcasted_iota(jnp.int32, (HEADS, count, width), 2) // head
    own = lane_head == lax.broadcasted_iota(jnp.int32, (HEADS, count, width), 0)
    q = reg_ref[0].astype(F32) * scale
    q = jnp.where(own, q[None], 0.0).reshape(HEADS * count, width).astype(BF16)
    scores = dot(keys, q, NT)
    self_scores = dot(reg_ref[1], q, NT) + flag_ref[0]
    high = jnp.maximum(
        jnp.max(scores, axis=0, keepdims=True), jnp.max(self_scores, axis=0, keepdims=True)
    )
    w = jnp.exp(scores - high)
    self_w = jnp.exp(self_scores - high)
    total = jnp.sum(w, axis=0, keepdims=True) + jnp.sum(self_w, axis=0, keepdims=True)
    acc = dot(jnp.transpose(w).astype(BF16), values, NN)
    acc = acc + dot(jnp.transpose(self_w).astype(BF16), reg_ref[2], NN)
    acc = jnp.sum(jnp.where(own, acc.reshape(HEADS, count, width), 0.0), axis=0)
    n = HEADS * count

    def spread(row):
        col = jnp.transpose(jnp.broadcast_to(row, (128, n))).reshape(HEADS, count, 128)
        low = lax.broadcasted_iota(jnp.int32, (count, 128), 1) < head
        return jnp.concatenate(
            [jnp.where(low, col[2 * p], col[2 * p + 1]) for p in range(HEADS // 2)], axis=1
        )

    out_ref[0] = acc
    out_ref[1] = spread(high)
    out_ref[2] = spread(total)


def register_partial(patches, registers, flag, scale):
    _, tr, tc, width = patches.shape
    count = registers.shape[1]
    return pl.pallas_call(
        functools.partial(register_kernel, scale),
        grid=(1,),
        in_specs=[
            pl.BlockSpec(memory_space=pltpu.SMEM),
            pl.BlockSpec((3, count, width), lambda i: (0, 0, 0)),
            pl.BlockSpec((None, tr, tc, width), lambda i: (1, 0, 0, 0)),
            pl.BlockSpec((None, tr, tc, width), lambda i: (2, 0, 0, 0)),
        ],
        out_specs=pl.BlockSpec((3, count, width), lambda i: (0, 0, 0)),
        out_shape=jax.ShapeDtypeStruct((3, count, width), F32),
        cost_estimate=pl.CostEstimate(flops=300_000_000, bytes_accessed=2_200_000, transcendentals=70_000),
        name="register_part",
    )(flag, registers, patches, patches)


def merge(a, b):
    high = jnp.maximum(a[1], b[1])
    fa = jnp.exp(a[1] - high)
    fb = jnp.exp(b[1] - high)
    return jnp.stack([a[0] * fa + b[0] * fb, high, a[2] * fa + b[2] * fb])


def merge_over(part, axis):
    n = lax.axis_size(axis)
    if n & (n - 1):
        every = lax.all_gather(part, axis)
        return functools.reduce(merge, [every[i] for i in range(n)])
    step = 1
    while step < n:
        part = merge(part, lax.ppermute(part, axis, [(i, i ^ step) for i in range(n)]))
        step *= 2
    return part


def by_column_group(x, groups):
    r, c, d = x.shape
    g = c // groups
    return jnp.concatenate(
        [x[:, i * g : (i + 1) * g].reshape(r * g, d) for i in range(groups)], axis=0
    )


def centre_kernel(scale, q_ref, k_ref, v_ref, up_ref, down_ref, reg_ref, qf_ref, kf_ref, out_ref, st_ref):
    tr, tc, d = q_ref.shape
    half_rows = tr // 2
    head = d // 2
    nq = half_rows * tc
    edge = half_rows * RADIUS
    groups = tc // RADIUS
    low_q = lax.broadcasted_iota(jnp.int32, (nq, d), 1) < head
    k_own = k_ref[...].reshape(tr * tc, d)
    v_own = v_ref[...].reshape(tr * tc, d)
    reg_k = jnp.concatenate([reg_ref[1], jnp.zeros_like(reg_ref[1])], axis=0)
    reg_v = jnp.concatenate([reg_ref[2], jnp.zeros_like(reg_ref[2])], axis=0)
    nr = reg_k.shape[0]
    last = lax.broadcasted_iota(jnp.int32, (nr, 128), 1) == tr + tc
    pad_row = lax.broadcasted_iota(jnp.int32, (nr, 128), 0) >= nr // 2
    reg_f = jnp.where(last & pad_row, FAR, 0.0).astype(BF16)
    for half in range(2):
        if half == 0:
            k = [up_ref[0].reshape(-1, d), k_own]
            v = [up_ref[1].reshape(-1, d), v_own]
            f0 = 0
        else:
            k = [k_own, down_ref[0].reshape(-1, d)]
            v = [v_own, down_ref[1].reshape(-1, d)]
            f0 = RADIUS * tc
        k = jnp.concatenate(k + [reg_k], axis=0)
        v = jnp.concatenate(v + [reg_v], axis=0)
        f = jnp.concatenate([kf_ref[f0 : f0 + (tr + RADIUS) * tc], reg_f], axis=0)
        kc = jnp.concatenate([k, f], axis=1)
        q = q_ref[half * half_rows : (half + 1) * half_rows].astype(F32) * scale
        q = by_column_group(q, groups)
        qf = qf_ref[half * nq : (half + 1) * nq]
        low_v = lax.broadcasted_iota(jnp.int32, v.shape, 1) < head
        one = jnp.ones_like(v)
        outs, highs = [], []
        for side in range(2):
            mine = low_q if side == 0 else ~low_q
            qc = jnp.concatenate([jnp.where(mine, q, 0.0).astype(BF16), qf], axis=1)
            s = dot(kc, qc, NT)
            high = jnp.max(s, axis=0, keepdims=True)
            w = jnp.exp(s - high).astype(BF16)
            va = jnp.where(low_v, v, one) if side == 0 else jnp.where(low_v, one, v)
            outs.append(dot(va, w, TN))
            highs.append(high)
        oa, ob = outs
        o = jnp.concatenate([oa[:head] / oa[head:], ob[head:] / ob[:head]], axis=0)
        o = jnp.transpose(o).reshape(groups, half_rows, RADIUS, d)
        o = jnp.concatenate([o[g] for g in range(groups)], axis=1)
        out_ref[half * half_rows : (half + 1) * half_rows] = o.astype(BF16)
        for side in range(2):
            c0 = 0 if side == 0 else nq - edge
            cut = lambda a, b: jnp.concatenate([a[:, c0 : c0 + edge], b[:, c0 : c0 + edge]], axis=1)
            st_ref[half, side, :d] = cut(oa, ob)
            high = cut(highs[0], highs[1])
            total = cut(oa[head : head + 1], ob[0:1])
            st_ref[half, side, d : d + 8] = jnp.concatenate(
                [high, total, jnp.zeros((6, 2 * edge), F32)], axis=0
            )


def centre(patches, up, down, registers, qf, kf, scale):
    _, tr, tc, width = patches.shape
    pairs = HEADS // 2
    d = width // pairs
    count = registers.shape[1]
    edge = tr // 2 * RADIUS
    part = lambda j: pl.BlockSpec((None, tr, tc, d), lambda p, j=j: (j, 0, 0, p))
    keys = (tr + RADIUS) * tc + 2 * count
    halo = pl.BlockSpec((2, RADIUS, tc, d), lambda p: (0, 0, 0, p))
    return pl.pallas_call(
        functools.partial(centre_kernel, scale),
        grid=(pairs,),
        in_specs=[
            part(0),
            part(1),
            part(2),
            halo,
            halo,
            pl.BlockSpec((3, count, d), lambda p: (0, 0, p)),
            pl.BlockSpec(qf.shape, lambda p: (0, 0)),
            pl.BlockSpec(kf.shape, lambda p: (0, 0)),
        ],
        out_specs=[
            pl.BlockSpec((tr, tc, d), lambda p: (0, 0, p)),
            pl.BlockSpec((None, 2, 2, d + 8, 2 * edge), lambda p: (p, 0, 0, 0, 0)),
        ],
        out_shape=[
            jax.ShapeDtypeStruct((tr, tc, width), BF16),
            jax.ShapeDtypeStruct((pairs, 2, 2, d + 8, 2 * edge), F32),
        ],
        cost_estimate=pl.CostEstimate(
            flops=HEADS * keys * tr * tc * 2 * 384,
            bytes_accessed=8_000_000,
            transcendentals=HEADS * keys * tr * tc,
        ),
        name="centre",
    )(patches, patches, patches, up, down, registers, qf, kf)


def edge_kernel(scale, q_ref, l_ref, r_ref, cu_ref, cd_ref, qf_ref, kf_ref, st_ref, prev_ref, out_ref):
    tr, tc, d = q_ref.shape
    half_rows = tr // 2
    head = d // 2
    edge = half_rows * RADIUS
    nq = half_rows * tc
    low = lax.broadcasted_iota(jnp.int32, (edge, d), 1) < head
    span = (tr + RADIUS) * RADIUS
    for half in range(2):
        rows = slice(half * half_rows, (half + 1) * half_rows)
        q_rows = q_ref[rows].astype(F32) * scale
        done = []
        for side in range(2):
            halo = l_ref if side == 0 else r_ref
            corner = cu_ref if half == 0 else cd_ref
            c0 = 0 if side == 0 else RADIUS

            def keys(j):
                own = halo[j].astype(F32).reshape(tr * RADIUS, d)
                cor = corner[j].astype(F32)[:, c0 : c0 + RADIUS].reshape(RADIUS * RADIUS, d)
                both = [cor, own] if half == 0 else [own, cor]
                return jnp.concatenate(both, axis=0).astype(BF16)

            f0 = side * (tr + 2 * RADIUS) * RADIUS + half * RADIUS * RADIUS
            kc = jnp.concatenate([keys(0), kf_ref[f0 : f0 + span]], axis=1)
            v = keys(1)
            x0 = 0 if side == 0 else tc - RADIUS
            q = q_rows[:, x0 : x0 + RADIUS].reshape(edge, d)
            q2 = jnp.concatenate([jnp.where(low, q, 0.0), jnp.where(low, 0.0, q)], axis=0)
            g0 = half * nq + (0 if side == 0 else nq - edge)
            qf = qf_ref[g0 : g0 + edge]
            qc = jnp.concatenate([q2.astype(BF16), jnp.concatenate([qf, qf], axis=0)], axis=1)
            s = dot(kc, qc, NT)
            high1 = st_ref[half, side, d : d + 1]
            total1 = st_ref[half, side, d + 1 : d + 2]
            high = jnp.maximum(high1, jnp.max(s, axis=0, keepdims=True))
            fade = jnp.exp(high1 - high)
            w = jnp.exp(s - high)
            total = total1 * fade + jnp.sum(w, axis=0, keepdims=True)
            acc = st_ref[half, side, :d] * fade + dot(v, w.astype(BF16), TN)
            o = jnp.transpose(acc / total)
            o = jnp.where(low, o[:edge], o[edge:])
            done.append(o.reshape(half_rows, RADIUS, d))
        mid = prev_ref[rows].astype(F32)[:, RADIUS : tc - RADIUS]
        out_ref[rows] = jnp.concatenate([done[0], mid, done[1]], axis=1).astype(BF16)


def edges(patches, left, right, corner_up, corner_down, qf, kf, state, prev, scale):
    _, tr, tc, width = patches.shape
    pairs = HEADS // 2
    d = width // pairs
    side = pl.BlockSpec((2, tr, RADIUS, d), lambda p: (0, 0, 0, p))
    corner = pl.BlockSpec((2, RADIUS, 2 * RADIUS, d), lambda p: (0, 0, 0, p))
    tile = pl.BlockSpec((tr, tc, d), lambda p: (0, 0, p))
    return pl.pallas_call(
        functools.partial(edge_kernel, scale),
        grid=(pairs,),
        in_specs=[
            pl.BlockSpec((None, tr, tc, d), lambda p: (0, 0, 0, p)),
            side,
            side,
            corner,
            corner,
            pl.BlockSpec(qf.shape, lambda p: (0, 0)),
            pl.BlockSpec(kf.shape, lambda p: (0, 0)),
            pl.BlockSpec((None,) + state.shape[1:], lambda p: (p, 0, 0, 0, 0)),
            tile,
        ],
        out_specs=tile,
        out_shape=jax.ShapeDtypeStruct((tr, tc, width), BF16),
        input_output_aliases={8: 0},
        cost_estimate=pl.CostEstimate(flops=500_000_000, bytes_accessed=6_000_000, transcendentals=800_000),
        name="edges",
    )(patches, left, right, corner_up, corner_down, qf, kf, state, prev)


def local(patches, registers):
    _, tr, tc, width = patches.shape
    scale = (width // HEADS) ** (-0.5)
    row_at, row_n = lax.axis_index("row"), lax.axis_size("row")
    col_at, col_n = lax.axis_index("col"), lax.axis_size("col")
    kv = patches[1:3]

    left = shift(kv[:, :, tc - RADIUS :], "col", 1)
    right = shift(kv[:, :, :RADIUS], "col", -1)
    up = shift(kv[:, tr - RADIUS :], "row", 1)
    down = shift(kv[:, :RADIUS], "row", -1)

    flag = jnp.where((row_at == 0) & (col_at == 0), 0.0, -1e30).astype(F32).reshape(1)
    part = register_partial(patches, registers, flag, scale)
    part = merge_over(merge_over(part, "row"), "col")
    register_out = (part[0] / part[2]).astype(BF16)

    key_rows = jnp.arange(-RADIUS, tr + RADIUS, dtype=jnp.int32)
    row_ok = ((key_rows >= 0) | (row_at > 0)) & ((key_rows < tr) | (row_at < row_n - 1))

    def features(cols, col_ok):
        n = cols.shape[0]
        rows = jnp.repeat(key_rows, n)
        ok = jnp.repeat(row_ok, n) & col_ok
        return key_features(rows, jnp.tile(cols, tr + 2 * RADIUS), ok, tr, tc)

    arange = lambda a, b: jnp.arange(a, b, dtype=jnp.int32)
    kf = features(arange(0, tc), True)
    kf_side = jnp.concatenate(
        [
            features(arange(-RADIUS, 0), col_at > 0),
            features(arange(tc, tc + RADIUS), col_at < col_n - 1),
        ]
    )
    q_id = arange(0, tr * tc).reshape(2, tc // RADIUS, tr // 2, RADIUS)
    at = lambda i: lax.broadcasted_iota(jnp.int32, q_id.shape, i)
    q_rows = (at(0) * (tr // 2) + at(2)).reshape(-1)
    q_cols = (at(1) * RADIUS + at(3)).reshape(-1)
    qf = query_features(q_rows, q_cols, tr, tc)

    out, state = centre(patches, up, down, registers, qf, kf, scale)
    halo = jnp.concatenate([left, right], axis=2)
    corner_up = shift(halo[:, tr - RADIUS :], "row", 1)
    corner_down = shift(halo[:, :RADIUS], "row", -1)
    out = edges(patches, left, right, corner_up, corner_down, qf, kf_side, state, out, scale)
    return (out, register_out)


def solution(mesh):
    in_specs = (P(None, "row", "col", None), P())
    out_specs = (P("row", "col", None), P())
    return jax.shard_map(local, mesh=mesh, in_specs=in_specs, out_specs=out_specs, check_vma=False)
```

time: 294 us -> 85.3 us (0.29); the launches traced: 291 us -> 84.8 us
  blocking collectives: 114 us -> 0 us
  matrix products: 102 us -> 0 us
  Pallas kernels: 0 us -> 36.3 us
  local copies, waits for them, and re-layouts: 34.5 us -> 5.96 us
  waiting for transfers between devices: 0.01 us -> 15 us
  other arithmetic: 18.4 us -> 4.33 us
  starting transfers between devices: 12 us -> 22.2 us
  loops' own time: 9.43 us -> 0 us
    dot_general x68 -> x0, matrix products: 102 us -> none  [the longest x16 49.7 us: one_head(): jnp.einsum('qd,kd->qk', head_queries, head_keys, preferred_element_type=j...]
    psum x1 -> x0, blocking collectives: 74.4 us -> none  [local(): lax.psum((local_totals * factor, local_weighted * factor[..., None]), ('r...]
    pmax x1 -> x0, blocking collectives: 39.2 us -> none  [local(): global_high = lax.pmax(local_high, ('row', 'col'))]
    pallas_call x0 -> x3, Pallas kernels: none -> 36.3 us  [the longest x1 21.7 us: centre(): pl.pallas_call(functools.partial(centre_kernel, scale), grid=(pairs,), in...]
    ppermute x4 -> x11, waiting for transfers between devices: 0.01 us -> 15 us  [the longest x5 15 us: merge_over(): lax.ppermute(part, axis, [(i, i ^ step) for i in range(n)])]
    reduce_sum x34 -> x0, other arithmetic: 10.5 us -> none  [the longest x32 9.47 us: one_head(): totals = jnp.sum(weights, axis=1) + jnp.sum(reg_weights, axis=1)]
    ppermute x4 -> x11, starting transfers between devices: 12 us -> 22.2 us  [the longest x6 17.3 us: shift(): lax.ppermute(x, axis, [(i, i + step) for i in range(n) if 0 <= i + step <...]
    another operation x1 -> x0, loops' own time: 9.43 us -> none  [local(): per_head = lax.map(one_head, jnp.arange(HEADS, dtype=jnp.int32))]
  transfers between devices with their start and end apart: 4 -> 11, of which waited for: 0 -> 3; matrix products, arithmetic and copies ran while one was open for 7% -> 11% of each run, Pallas kernels for 0% -> 26%
where the time goes in v1:
time: 85.3 us; the launch traced here: 84.8 us
  Pallas kernels  36.3 us (43%)
  starting transfers between devices  22.2 us (26%)
  waiting for transfers between devices  15 us (18%)
  local copies, waits for them, and re-layouts  5.96 us (7%)
  other arithmetic  4.33 us (5%)
  between operations  1.01 us (1%)
    pallas_call x1, Pallas kernels, centre(): pl.pallas_call(functools.partial(centre_kernel, scale), grid=(pairs,), in...  21.7 us
    ppermute x6, starting transfers between devices, shift(): lax.ppermute(x, axis, [(i, i + step) for i in range(n) if 0 <= i + step <...  17.3 us
    ppermute x5, waiting for transfers between devices, merge_over(): lax.ppermute(part, axis, [(i, i ^ step) for i in range(n)])  15 us
    pallas_call x1, Pallas kernels, edges(): pl.pallas_call(functools.partial(edge_kernel, scale), grid=(pairs,), in_s...  10.9 us
    ppermute x5, starting transfers between devices, merge_over(): lax.ppermute(part, axis, [(i, i ^ step) for i in range(n)])  4.96 us
    pallas_call x1, Pallas kernels, register_partial(): pl.pallas_call(functools.partial(register_kernel, scale), grid=(1,), in_s...  3.67 us
    convert_element_type x2, other arithmetic, key_features(): return jnp.where(far_col | far_row | off, FAR, 0.0).astype(BF16)  1.73 us
  transfers between devices with their start and end apart: 11, of which 3 were waited for; matrix products, arithmetic and copies ran while one was open for 11% of the time, Pallas kernels for 26%

profile of v1, /device:TPU:19, one launch (start us, length us, event | category | flops | bytes accessed | tf_op | source)
XLA Modules:
  0.0 84.8 jit_solution(3009465467134790421)
XLA Ops:
  0.7 3.7 %register_part.1 = f32[3,8,1024]{2,1,0:T(8,128)} custom-call(f32[1]{0:T(128)} %bitcast.flag_ref, bf16[3,8,1024]{2,1,0:T(8,128)(2,1)} %reg_ref.3, bf16[3,16,32,1024]{3,2,1,0:T(8,128)(2,1)} %v_ref.3, bf16[3,16,32,1024]{3,2,1,0:T(8,128)(2,1)} %v_ref.3), custom_call_target="tpu_custom_call" | custom-call | flops 300000000 | bytes 2200000 | tf_op jit(solution)/shard_map/register_part/pallas_call | solution.py:83
  4.3 0.7 collective-permute-start.6
  5.0 1.6 %fusion.52 = (bf16[2,8,32,1024]{3,2,1,0:T(8,128)(2,1)}, bf16[2,8,32,1024]{3,2,1,0:T(8,128)(2,1)}) fusion(bf16[3,16,32,1024]{3,2,1,0:T(8,128)(2,1)S(1)} %copy-done), kind=kLoop, calls=%fused_computation.125 | loop fusion | bytes 4194304 | tf_op jit(solution)/shard_map/slice | solution.py:311
  6.6 3.1 %collective-permute-start.4 = (bf16[2,8,32,1024]{3,2,1,0:T(8,128)(2,1)}, bf16[2,8,32,1024]{3,2,1,0:T(8,128)(2,1)}, u32[]{:S(2)}, u32[]{:S(2)}) collective-permute-start(bf16[2,8,32,1024]{3,2,1,0:T(8,128)(2,1)} %get-tuple-element.13), channel_id=1, source_target_pairs={{0,4},{4,8},{8,12},{12,16},{16,20},{20,24},{24,28},{1,5},{5,9},{9,... | collective-permute-start | bytes 3145736 | tf_op jit(solution)/shard_map/ppermute | solution.py:26
  9.7 1.9 %collective-permute-start.5 = (bf16[2,8,32,1024]{3,2,1,0:T(8,128)(2,1)}, bf16[2,8,32,1024]{3,2,1,0:T(8,128)(2,1)}, u32[]{:S(2)}, u32[]{:S(2)}) collective-permute-start(bf16[2,8,32,1024]{3,2,1,0:T(8,128)(2,1)} %get-tuple-element.12), channel_id=1, source_target_pairs={{4,0},{8,4},{12,8},{16,12},{20,16},{24,20},{28,24},{5,1},{9,5},{13... | collective-permute-start | bytes 3145736 | tf_op jit(solution)/shard_map/ppermute | solution.py:26
  11.6 1.0 %fusion.53 = (bf16[2,16,8,1024]{3,2,1,0:T(8,128)(2,1)}, bf16[2,16,8,1024]{3,2,1,0:T(8,128)(2,1)}) fusion(bf16[3,16,32,1024]{3,2,1,0:T(8,128)(2,1)S(1)} %copy-done), kind=kLoop, calls=%fused_computation.126 | loop fusion | bytes 2097152 | tf_op jit(solution)/shard_map/slice | solution.py:309
  12.6 3.1 %collective-permute-start = (bf16[2,16,8,1024]{3,2,1,0:T(8,128)(2,1)}, bf16[2,16,8,1024]{3,2,1,0:T(8,128)(2,1)S(1)}, u32[]{:S(2)}, u32[]{:S(2)}) collective-permute-start(bf16[2,16,8,1024]{3,2,1,0:T(8,128)(2,1)} %get-tuple-element.15), channel_id=1, source_target_pairs={{0,1},{1,2},{2,3},{4,5},{5,6},{6,7},{8,9},{9,10},{10,11},{12,13},{... | collective-permute-start | bytes 1572872 | tf_op jit(solution)/shard_map/ppermute | solution.py:26
  15.8 2.2 %collective-permute-start.1 = (bf16[2,16,8,1024]{3,2,1,0:T(8,128)(2,1)}, bf16[2,16,8,1024]{3,2,1,0:T(8,128)(2,1)S(1)}, u32[]{:S(2)}, u32[]{:S(2)}) collective-permute-start(bf16[2,16,8,1024]{3,2,1,0:T(8,128)(2,1)} %get-tuple-element.14), channel_id=1, source_target_pairs={{1,0},{2,1},{3,2},{5,4},{6,5},{7,6},{9,8},{10,9},{11,10},{13,12},{... | collective-permute-start | bytes 1572872 | tf_op jit(solution)/shard_map/ppermute | solution.py:26
  18.2 0.1 not.37
  18.3 0.1 not.39
  18.5 0.1 sub.190
  18.9 0.1 not.41
  19.3 1.5 %select_convert_fusion.kf_ref = bf16[1024,128]{1,0:T(8,128)(2,1)} fusion(s32[128]{0:T(128)S(1)} %iota_add_fusion.3, s32[1024]{0:T(1024)S(1)} %sub.202, s32[1024]{0:T(1024)S(1)} %sub.198, pred[128]{0:T(512)(128)(4,1)S(1)} %iota_compare_fusion.3, pred[128]{0:T(512)(128)(4,1)S(1)} %get-tuple-element.25, pred[128]{0:T(512)(128)(4,1)S(1)} %get-tuple-element.26, ...), kind=kLoop, calls=%fused_computation | loop fusion | flops 1703936 | bytes 272256 | tf_op jit(solution)/shard_map/convert_element_type | solution.py:36
  20.8 0.2 select_convert_fusion.2
  21.1 1.6 %collective-permute-start.7 = (f32[3,8,1024]{2,1,0:T(8,128)S(1)}, f32[3,8,1024]{2,1,0:T(8,128)S(1)}, u32[]{:S(2)}, u32[]{:S(2)}) collective-permute-start(f32[3,8,1024]{2,1,0:T(8,128)S(1)} %pad_maximum_fusion.1), channel_id=1, source_target_pairs={{0,8},{4,12},{8,0},{12,4},{16,24},{20,28},{24,16},{28,20},{1,9},{5... | collective-permute-start | bytes 294920 | tf_op jit(solution)/shard_map/ppermute | solution.py:113
  22.8 0.1 add.147
  22.9 0.1 add.151
  23.0 3.1 %collective-permute-done.7 = f32[3,8,1024]{2,1,0:T(8,128)S(1)} collective-permute-done((f32[3,8,1024]{2,1,0:T(8,128)S(1)}, f32[3,8,1024]{2,1,0:T(8,128)S(1)}, u32[]{:S(2)}, u32[]{:S(2)}) %collective-permute-start.7) | collective-permute-done | bytes 98336 | tf_op jit(solution)/shard_map/ppermute | solution.py:113
  26.2 0.3 collective-permute-start.8
  26.4 0.9 %fusion.6.qf_ref = bf16[512,128]{1,0:T(8,128)(2,1)} fusion(s32[512]{0:T(512)S(1)} %add.151, s32[512]{0:T(512)S(1)} %add.147, pred[128]{0:T(512)(128)(4,1)S(1)} %iota_compare_fusion.3), kind=kLoop, calls=%fused_computation.11 | loop fusion | flops 327680 | bytes 135296 | tf_op jit(solution)/shard_map/convert_element_type | solution.py:42
  27.3 3.6 %collective-permute-done.8 = f32[3,8,1024]{2,1,0:T(8,128)S(1)} collective-permute-done((f32[3,8,1024]{2,1,0:T(8,128)S(1)}, f32[3,8,1024]{2,1,0:T(8,128)S(1)}, u32[]{:S(2)}, u32[]{:S(2)}) %collective-permute-start.8) | collective-permute-done | bytes 98336 | tf_op jit(solution)/shard_map/ppermute | solution.py:113
  31.1 0.7 pad_maximum_fusion.kf_ref
  31.7 8.3 %collective-permute-done.9 = f32[3,8,1024]{2,1,0:T(8,128)S(1)} collective-permute-done((f32[3,8,1024]{2,1,0:T(8,128)S(1)}, f32[3,8,1024]{2,1,0:T(8,128)S(1)}, u32[]{:S(2)}, u32[]{:S(2)}) %collective-permute-start.9) | collective-permute-done | bytes 98336 | tf_op jit(solution)/shard_map/ppermute | solution.py:113
  40.1 2.3 %collective-permute-start.10 = (f32[3,8,1024]{2,1,0:T(8,128)S(1)}, f32[3,8,1024]{2,1,0:T(8,128)S(1)}, u32[]{:S(2)}, u32[]{:S(2)}) collective-permute-start(f32[3,8,1024]{2,1,0:T(8,128)S(1)} %pad_maximum_fusion.4), channel_id=1, source_target_pairs={{0,2},{1,3},{2,0},{3,1},{4,6},{5,7},{6,4},{7,5},{8,10},{9,11},{10,... | collective-permute-start | bytes 294920 | tf_op jit(solution)/shard_map/ppermute | solution.py:113
  42.5 1.0 %fusion.54 = (bf16[2,8,16,1024]{3,2,1,0:T(8,128)(2,1)S(1)}, bf16[2,8,16,1024]{3,2,1,0:T(8,128)(2,1)}) fusion(bf16[2,16,16,1024]{3,2,1,0:T(8,128)(2,1)S(1)} %constant_dynamic-update-slice_fusion), kind=kLoop, calls=%fused_computation.127 | loop fusion | bytes 2097152 | tf_op jit(solution)/shard_map/slice | solution.py:344
  43.5 5.0 %collective-permute-start.2 = (bf16[2,8,16,1024]{3,2,1,0:T(8,128)(2,1)}, bf16[2,8,16,1024]{3,2,1,0:T(8,128)(2,1)S(1)}, u32[]{:S(2)}, u32[]{:S(2)}) collective-permute-start(bf16[2,8,16,1024]{3,2,1,0:T(8,128)(2,1)} %get-tuple-element.17), channel_id=1, source_target_pairs={{0,4},{4,8},{8,12},{12,16},{16,20},{20,24},{24,28},{1,5},{5,9},{9,... | collective-permute-start | bytes 1572872 | tf_op jit(solution)/shard_map/ppermute | solution.py:26
  48.6 1.9 %collective-permute-start.3 = (bf16[2,8,16,1024]{3,2,1,0:T(8,128)(2,1)S(1)}, bf16[2,8,16,1024]{3,2,1,0:T(8,128)(2,1)S(1)}, u32[]{:S(2)}, u32[]{:S(2)}) collective-permute-start(bf16[2,8,16,1024]{3,2,1,0:T(8,128)(2,1)S(1)} %get-tuple-element.16), channel_id=1, source_target_pairs={{4,0},{8,4},{12,8},{16,12},{20,16},{24,20},{28,24},{5,1},{9,5},{13... | collective-permute-start | bytes 1572872 | tf_op jit(solution)/shard_map/ppermute | solution.py:26
  50.5 0.7 fusion.50
  51.2 21.7 %centre.1 = (bf16[16,32,1024]{2,1,0:T(8,128)(2,1)}, f32[8,2,2,136,128]{4,3,2,1,0:T(8,128)}) custom-call(bf16[3,16,32,1024]{3,2,1,0:T(8,128)(2,1)} %v_ref.3, bf16[3,16,32,1024]{3,2,1,0:T(8,128)(2,1)} %v_ref.3, bf16[3,16,32,1024]{3,2,1,0:T(8,128)(2,1)} %v_ref.3, bf16[2,8,32,1024]{3,2,1,0:T(8,128)(2,1)} %collective-permute-done.4.up_ref, ...), custom_call_target="tpu_custom_call" | custom-call | flops 4932501504 | bytes 8000000 | tf_op jit(solution)/shard_map/centre/pallas_call | solution.py:195
  72.9 0.8 copy-done.4
  73.7 0.2 copy-done.5
  73.9 10.9 %edges.1 = bf16[16,32,1024]{2,1,0:T(8,128)(2,1)} custom-call(bf16[3,16,32,1024]{3,2,1,0:T(8,128)(2,1)} %v_ref.3, bf16[2,16,8,1024]{3,2,1,0:T(8,128)(2,1)} %copy-done.1, bf16[2,16,8,1024]{3,2,1,0:T(8,128)(2,1)} %copy-done.2, bf16[2,8,16,1024]{3,2,1,0:T(8,128)(2,1)} %copy-done.4, bf16[2,8,16,1024]{3,2,1,0:T(8,128)(2,1)} %copy-done.5, ...), custom_call_target="tpu_custom_call", output_to_operand_aliasing={{}: (8, {})} | custom-call | flops 500000000 | bytes 6000000 | tf_op jit(solution)/shard_map/edges/pallas_call | solution.py:279
  (56 shorter events, 1.3 us)
Async XLA Ops:
  0.6 4.4 %copy-start = (bf16[3,16,32,1024]{3,2,1,0:T(8,128)(2,1)S(1)}, bf16[3,16,32,1024]{3,2,1,0:T(8,128)(2,1)}, u32[]{:S(2)}) copy-start(bf16[3,16,32,1024]{3,2,1,0:T(8,128)(2,1)} %v_ref.3) | copy-start | bytes 9437188
  4.3 16.7 %copy-start.3 = (f32[3,8,1024]{2,1,0:T(8,128)S(1)}, f32[3,8,1024]{2,1,0:T(8,128)}, u32[]{:S(2)}) copy-start(f32[3,8,1024]{2,1,0:T(8,128)} %register_part.1) | copy-start | bytes 294916
  4.3 16.7 %collective-permute-start.6 = (f32[3,8,1024]{2,1,0:T(8,128)}, f32[3,8,1024]{2,1,0:T(8,128)S(1)}, u32[]{:S(2)}, u32[]{:S(2)}) collective-permute-start(f32[3,8,1024]{2,1,0:T(8,128)} %register_part.1), channel_id=1, source_target_pairs={{0,4},{4,0},{8,12},{12,8},{16,20},{20,16},{24,28},{28,24},{1,5},{5... | collective-permute-start | bytes 294920 | tf_op jit(solution)/shard_map/ppermute | solution.py:113
  6.6 44.6 %collective-permute-start.4 = (bf16[2,8,32,1024]{3,2,1,0:T(8,128)(2,1)}, bf16[2,8,32,1024]{3,2,1,0:T(8,128)(2,1)}, u32[]{:S(2)}, u32[]{:S(2)}) collective-permute-start(bf16[2,8,32,1024]{3,2,1,0:T(8,128)(2,1)} %get-tuple-element.13), channel_id=1, source_target_pairs={{0,4},{4,8},{8,12},{12,16},{16,20},{20,24},{24,28},{1,5},{5,9},{9,... | collective-permute-start | bytes 3145736 | tf_op jit(solution)/shard_map/ppermute | solution.py:26
  9.7 41.5 %collective-permute-start.5 = (bf16[2,8,32,1024]{3,2,1,0:T(8,128)(2,1)}, bf16[2,8,32,1024]{3,2,1,0:T(8,128)(2,1)}, u32[]{:S(2)}, u32[]{:S(2)}) collective-permute-start(bf16[2,8,32,1024]{3,2,1,0:T(8,128)(2,1)} %get-tuple-element.12), channel_id=1, source_target_pairs={{4,0},{8,4},{12,8},{16,12},{20,16},{24,20},{28,24},{5,1},{9,5},{13... | collective-permute-start | bytes 3145736 | tf_op jit(solution)/shard_map/ppermute | solution.py:26
  12.6 29.7 %collective-permute-start = (bf16[2,16,8,1024]{3,2,1,0:T(8,128)(2,1)}, bf16[2,16,8,1024]{3,2,1,0:T(8,128)(2,1)S(1)}, u32[]{:S(2)}, u32[]{:S(2)}) collective-permute-start(bf16[2,16,8,1024]{3,2,1,0:T(8,128)(2,1)} %get-tuple-element.15), channel_id=1, source_target_pairs={{0,1},{1,2},{2,3},{4,5},{5,6},{6,7},{8,9},{9,10},{10,11},{12,13},{... | collective-permute-start | bytes 1572872 | tf_op jit(solution)/shard_map/ppermute | solution.py:26
  15.8 26.6 %collective-permute-start.1 = (bf16[2,16,8,1024]{3,2,1,0:T(8,128)(2,1)}, bf16[2,16,8,1024]{3,2,1,0:T(8,128)(2,1)S(1)}, u32[]{:S(2)}, u32[]{:S(2)}) collective-permute-start(bf16[2,16,8,1024]{3,2,1,0:T(8,128)(2,1)} %get-tuple-element.14), channel_id=1, source_target_pairs={{1,0},{2,1},{3,2},{5,4},{6,5},{7,6},{9,8},{10,9},{11,10},{13,12},{... | collective-permute-start | bytes 1572872 | tf_op jit(solution)/shard_map/ppermute | solution.py:26
  21.1 5.0 %collective-permute-start.7 = (f32[3,8,1024]{2,1,0:T(8,128)S(1)}, f32[3,8,1024]{2,1,0:T(8,128)S(1)}, u32[]{:S(2)}, u32[]{:S(2)}) collective-permute-start(f32[3,8,1024]{2,1,0:T(8,128)S(1)} %pad_maximum_fusion.1), channel_id=1, source_target_pairs={{0,8},{4,12},{8,0},{12,4},{16,24},{20,28},{24,16},{28,20},{1,9},{5... | collective-permute-start | bytes 294920 | tf_op jit(solution)/shard_map/ppermute | solution.py:113
  26.2 4.8 %collective-permute-start.8 = (f32[3,8,1024]{2,1,0:T(8,128)S(1)}, f32[3,8,1024]{2,1,0:T(8,128)S(1)}, u32[]{:S(2)}, u32[]{:S(2)}) collective-permute-start(f32[3,8,1024]{2,1,0:T(8,128)S(1)} %pad_maximum_fusion.2), channel_id=1, source_target_pairs={{0,16},{4,20},{8,24},{12,28},{16,0},{20,4},{24,8},{28,12},{1,17},{... | collective-permute-start | bytes 294920 | tf_op jit(solution)/shard_map/ppermute | solution.py:113
  31.0 9.0 %collective-permute-start.9 = (f32[3,8,1024]{2,1,0:T(8,128)S(1)}, f32[3,8,1024]{2,1,0:T(8,128)S(1)}, u32[]{:S(2)}, u32[]{:S(2)}) collective-permute-start(f32[3,8,1024]{2,1,0:T(8,128)S(1)} %pad_maximum_fusion.3), channel_id=1, source_target_pairs={{0,1},{1,0},{2,3},{3,2},{4,5},{5,4},{6,7},{7,6},{8,9},{9,8},{10,11... | collective-permute-start | bytes 294920 | tf_op jit(solution)/shard_map/ppermute | solution.py:113
  40.1 10.4 %collective-permute-start.10 = (f32[3,8,1024]{2,1,0:T(8,128)S(1)}, f32[3,8,1024]{2,1,0:T(8,128)S(1)}, u32[]{:S(2)}, u32[]{:S(2)}) collective-permute-start(f32[3,8,1024]{2,1,0:T(8,128)S(1)} %pad_maximum_fusion.4), channel_id=1, source_target_pairs={{0,2},{1,3},{2,0},{3,1},{4,6},{5,7},{6,4},{7,5},{8,10},{9,11},{10,... | collective-permute-start | bytes 294920 | tf_op jit(solution)/shard_map/ppermute | solution.py:113
  42.3 30.5 %copy-start.1 = (bf16[2,16,8,1024]{3,2,1,0:T(8,128)(2,1)}, bf16[2,16,8,1024]{3,2,1,0:T(8,128)(2,1)S(1)}, u32[]{:S(2)}) copy-start(bf16[2,16,8,1024]{3,2,1,0:T(8,128)(2,1)S(1)} %collective-permute-done.l_ref) | copy-start | bytes 1572868
  42.4 30.5 %copy-start.2 = (bf16[2,16,8,1024]{3,2,1,0:T(8,128)(2,1)}, bf16[2,16,8,1024]{3,2,1,0:T(8,128)(2,1)S(1)}, u32[]{:S(2)}) copy-start(bf16[2,16,8,1024]{3,2,1,0:T(8,128)(2,1)S(1)} %collective-permute-done.1.r_ref) | copy-start | bytes 1572868
  43.5 29.4 %collective-permute-start.2 = (bf16[2,8,16,1024]{3,2,1,0:T(8,128)(2,1)}, bf16[2,8,16,1024]{3,2,1,0:T(8,128)(2,1)S(1)}, u32[]{:S(2)}, u32[]{:S(2)}) collective-permute-start(bf16[2,8,16,1024]{3,2,1,0:T(8,128)(2,1)} %get-tuple-element.17), channel_id=1, source_target_pairs={{0,4},{4,8},{8,12},{12,16},{16,20},{20,24},{24,28},{1,5},{5,9},{9,... | collective-permute-start | bytes 1572872 | tf_op jit(solution)/shard_map/ppermute | solution.py:26
  48.6 24.4 %collective-permute-start.3 = (bf16[2,8,16,1024]{3,2,1,0:T(8,128)(2,1)S(1)}, bf16[2,8,16,1024]{3,2,1,0:T(8,128)(2,1)S(1)}, u32[]{:S(2)}, u32[]{:S(2)}) collective-permute-start(bf16[2,8,16,1024]{3,2,1,0:T(8,128)(2,1)S(1)} %get-tuple-element.16), channel_id=1, source_target_pairs={{4,0},{8,4},{12,8},{16,12},{20,16},{24,20},{28,24},{5,1},{9,5},{13... | collective-permute-start | bytes 1572872 | tf_op jit(solution)/shard_map/ppermute | solution.py:26
  72.9 0.8 copy-start.4
  72.9 1.0 %copy-start.5 = (bf16[2,8,16,1024]{3,2,1,0:T(8,128)(2,1)}, bf16[2,8,16,1024]{3,2,1,0:T(8,128)(2,1)S(1)}, u32[]{:S(2)}) copy-start(bf16[2,8,16,1024]{3,2,1,0:T(8,128)(2,1)S(1)} %collective-permute-done.3.cd_ref) | copy-start | bytes 1572868

commit v2 on v0

v2 whole, which is shorter than its diff:
```python
import functools

import jax
import jax.numpy as jnp
import numpy as np
from jax import lax
from jax.experimental import pallas as pl
from jax.experimental.pallas import tpu as pltpu
from jax.sharding import PartitionSpec as P

HEADS = 16
RADIUS = 8
FAR = -30000.0
LANES = 128
F32 = jnp.float32
BF16 = jnp.bfloat16
NT = (((1,), (1,)), ((), ()))
NN = (((1,), (0,)), ((), ()))
TN = (((0,), (0,)), ((), ()))
VMEM = pl.BlockSpec(memory_space=pltpu.VMEM)
HBM = pl.BlockSpec(memory_space=pltpu.HBM)
SMEM = pl.BlockSpec(memory_space=pltpu.SMEM)
PARAMS = pltpu.CompilerParams(vmem_limit_bytes=24 * 1024 * 1024)


def dot(a, b, dims):
    return lax.dot_general(a, b, dims, preferred_element_type=F32)


def shift(x, axis, step):
    n = lax.axis_size(axis)
    return lax.ppermute(x, axis, [(i, i + step) for i in range(n) if 0 <= i + step < n])


def key_features(rows, cols, tr, tc):
    lane = np.arange(LANES)
    far_col = (lane < tc) & (np.abs(cols[..., None] - lane) > RADIUS)
    far_row = (lane >= tc) & (lane < tc + tr) & (np.abs(rows[..., None] - (lane - tc)) > RADIUS)
    return np.where(far_col | far_row, FAR, 0.0).astype(np.float32)


def query_features(rows, cols, tr, tc):
    lane = np.arange(LANES)
    hit = (lane == cols[..., None]) | (lane - tc == rows[..., None]) | (lane == tc + tr)
    return hit.astype(np.float32)


def with_grid_edge(const, off):
    lane = lax.broadcasted_iota(jnp.int32, const.shape, const.ndim - 1)
    return jnp.where((lane == off[1]) & off[0], FAR, jnp.asarray(const)).astype(BF16)


def copy_all(copies, sems):
    started = []
    for i, (src, dst) in enumerate(copies):
        c = pltpu.make_async_copy(src, dst, sems.at[i])
        c.start()
        started.append(c)
    return started


def pack_kernel(p_ref, right_ref, left_ref, down_ref, up_ref, sems):
    _, tr, tc, _ = p_ref.shape
    groups = tc // RADIUS
    copies = []
    for j in range(2):
        copies.append((p_ref.at[1 + j, :, pl.ds(tc - RADIUS, RADIUS)], right_ref.at[j]))
        copies.append((p_ref.at[1 + j, :, pl.ds(0, RADIUS)], left_ref.at[j]))
    for j in range(2):
        for g in range(groups):
            cols = pl.ds(g * RADIUS, RADIUS)
            copies.append((p_ref.at[1 + j, pl.ds(tr - RADIUS, RADIUS), cols], down_ref.at[j, g]))
            copies.append((p_ref.at[1 + j, pl.ds(0, RADIUS), cols], up_ref.at[j, g]))
    for c in copy_all(copies, sems):
        c.wait()


def pack(patches):
    _, tr, tc, width = patches.shape
    groups = tc // RADIUS
    side = pltpu.VMEM((2, tr, RADIUS, width), BF16)
    rows = pltpu.VMEM((2, groups, RADIUS, RADIUS, width), BF16)
    return pl.pallas_call(
        pack_kernel,
        in_specs=[HBM],
        out_specs=[VMEM] * 4,
        out_shape=[side, side, rows, rows],
        scratch_shapes=[pltpu.SemaphoreType.DMA((4 + 4 * groups,))],
        compiler_params=PARAMS,
        name="pack",
    )(patches)


def prep_kernel(scale, flag_ref, reg_ref, p_ref, out_ref, part_ref, sems):
    _, tr, tc, width = p_ref.shape
    groups = tc // RADIUS
    count = reg_ref.shape[1]
    head = width // HEADS
    copies = [
        (p_ref.at[j, :, pl.ds(g * RADIUS, RADIUS)], out_ref.at[j, g])
        for j in (1, 2, 0)
        for g in range(groups)
    ]
    started = copy_all(copies, sems)
    lane_head = lax.broadcasted_iota(jnp.int32, (HEADS, count, width), 2) // head
    own = lane_head == lax.broadcasted_iota(jnp.int32, (HEADS, count, width), 0)
    q = reg_ref[0].astype(F32) * scale
    q = jnp.where(own, q[None], 0.0).reshape(HEADS * count, width).astype(BF16)
    self_scores = dot(reg_ref[1], q, NT) + flag_ref[0]
    for c in started[:groups]:
        c.wait()
    scores = dot(out_ref[1].reshape(tr * tc, width), q, NT)
    high = jnp.maximum(
        jnp.max(scores, axis=0, keepdims=True), jnp.max(self_scores, axis=0, keepdims=True)
    )
    w = jnp.exp(scores - high)
    self_w = jnp.exp(self_scores - high)
    total = jnp.sum(w, axis=0, keepdims=True) + jnp.sum(self_w, axis=0, keepdims=True)
    wt = jnp.transpose(w).astype(BF16)
    for c in started[groups:]:
        c.wait()
    acc = dot(wt, out_ref[2].reshape(tr * tc, width), NN)
    acc = acc + dot(jnp.transpose(self_w).astype(BF16), reg_ref[2], NN)
    acc = jnp.sum(jnp.where(own, acc.reshape(HEADS, count, width), 0.0), axis=0)
    n = HEADS * count

    def spread(row):
        col = jnp.transpose(jnp.broadcast_to(row, (LANES, n))).reshape(HEADS, count, LANES)
        low = lax.broadcasted_iota(jnp.int32, (count, LANES), 1) < head
        return jnp.concatenate(
            [jnp.where(low, col[2 * p], col[2 * p + 1]) for p in range(HEADS // 2)], axis=1
        )

    part_ref[0] = acc
    part_ref[1] = spread(high)
    part_ref[2] = spread(total)


def prep(patches, registers, flag, scale):
    _, tr, tc, width = patches.shape
    groups = tc // RADIUS
    count = registers.shape[1]
    return pl.pallas_call(
        functools.partial(prep_kernel, scale),
        in_specs=[SMEM, VMEM, HBM],
        out_specs=[VMEM, VMEM],
        out_shape=[
            pltpu.VMEM((3, groups, tr, RADIUS, width), BF16),
            pltpu.VMEM((3, count, width), F32),
        ],
        scratch_shapes=[pltpu.SemaphoreType.DMA((3 * groups,))],
        cost_estimate=pl.CostEstimate(
            flops=300_000_000, bytes_accessed=4_000_000, transcendentals=70_000
        ),
        compiler_params=PARAMS,
        name="prep",
    )(flag, registers, patches)


def merge(a, b):
    high = jnp.maximum(a[1], b[1])
    fa = jnp.exp(a[1] - high)
    fb = jnp.exp(b[1] - high)
    return jnp.stack([a[0] * fa + b[0] * fb, high, a[2] * fa + b[2] * fb])


def merge_over(part, axis):
    n = lax.axis_size(axis)
    if n & (n - 1):
        every = lax.all_gather(part, axis)
        return functools.reduce(merge, [every[i] for i in range(n)])
    step = 1
    while step < n:
        part = merge(part, lax.ppermute(part, axis, [(i, i ^ step) for i in range(n)]))
        step *= 2
    return part


def centre_kernel(scale, first, p_ref, up_ref, down_ref, reg_ref, qf_ref, kf_ref, in_ref, st_ref):
    _, groups, cells, width = p_ref.shape
    d = LANES
    head = width // HEADS
    edge = RADIUS * RADIUS
    low = lax.broadcasted_iota(jnp.int32, (edge, d), 1) < head
    pad = lax.broadcasted_iota(jnp.int32, (2 * RADIUS, d), 0) >= RADIUS
    off = lax.broadcasted_iota(jnp.int32, (2 * RADIUS, d), 1) == d - 1
    reg_f = jnp.where(pad & off, FAR, 0.0).astype(BF16)
    zero = jnp.zeros((RADIUS, d), BF16)

    @pl.loop(0, st_ref.shape[0])
    def _(i):
        lanes = pl.ds(pl.multiple_of((i + first) * d, d), d)
        lanes_out = pl.ds(pl.multiple_of(i * d, d), d)
        reg_k = jnp.concatenate([reg_ref[1, :, lanes], zero], axis=0)
        reg_v = jnp.concatenate([reg_ref[2, :, lanes], zero], axis=0)
        for half in range(2):
            for part in range(2):
                near = range(part, part + 3)

                def piece(j, g):
                    own = p_ref[1 + j, g, :, lanes]
                    if half == 0:
                        return [up_ref[j, g, :, lanes], own]
                    return [own, down_ref[j, g, :, lanes]]

                span = cells + edge
                k = jnp.concatenate(sum([piece(0, g) for g in near], []) + [reg_k], axis=0)
                v = jnp.concatenate(sum([piece(1, g) for g in near], []) + [reg_v], axis=0)
                f = jnp.concatenate(
                    [kf_ref[g, half * edge : half * edge + span] for g in near] + [reg_f], axis=0
                )
                kc = jnp.concatenate([k, f], axis=1)
                qs = []
                for g in (0, 1) if part == 0 else (3, 2):
                    rows = slice(half * edge, (half + 1) * edge)
                    q = p_ref[0, g, rows, lanes].astype(F32) * scale
                    qf = qf_ref[g, rows]
                    for x in (jnp.where(low, q, 0.0), jnp.where(low, 0.0, q)):
                        qs.append(jnp.concatenate([x.astype(BF16), qf], axis=1))
                s = dot(kc, jnp.concatenate(qs, axis=0), NT)
                high = jnp.max(s, axis=0, keepdims=True)
                w = jnp.exp(s - high)
                total = jnp.sum(w, axis=0, keepdims=True)
                o = dot(v, w.astype(BF16), TN)
                st_ref[i, half, part, :d] = o[:, :d]
                st_ref[i, half, part, d : d + 8] = jnp.concatenate(
                    [high[:, :d], total[:, :d], jnp.zeros((6, d), F32)], axis=0
                )
                t = jnp.transpose(o[:, d:] / total[:, d:])
                t = jnp.where(low, t[:edge], t[edge:])
                in_ref[part, half * edge : (half + 1) * edge, lanes_out] = t.astype(BF16)


def centre(pg, up, down, registers, qf, kf, scale, first, pairs):
    _, groups, cells, width = pg.shape
    edge = RADIUS * RADIUS
    d = LANES
    keys = 3 * (cells + edge) + 2 * RADIUS
    work = pairs * 4 * keys * 4 * edge
    return pl.pallas_call(
        functools.partial(centre_kernel, scale, first),
        in_specs=[VMEM] * 6,
        out_specs=[VMEM, VMEM],
        out_shape=[
            pltpu.VMEM((2, cells, pairs * d), BF16),
            pltpu.VMEM((pairs, 2, 2, d + 8, d), F32),
        ],
        cost_estimate=pl.CostEstimate(
            flops=work * 2 * 384, bytes_accessed=4_000_000, transcendentals=work
        ),
        compiler_params=PARAMS,
        name="centre",
    )(pg, up, down, registers, qf, kf)


def edge_kernel(
    scale, parts, p_ref, l_ref, r_ref, cu_ref, cd_ref, qf_ref, kf_ref, *refs
):
    inner, states = refs[:parts], refs[parts : 2 * parts]
    out_ref, edge_ref, sems = refs[2 * parts :]
    _, groups, cells, width = p_ref.shape
    d = LANES
    head = width // HEADS
    edge = RADIUS * RADIUS
    span = cells + edge
    low = lax.broadcasted_iota(jnp.int32, (edge, d), 1) < head
    per = states[0].shape[0]
    copies = []
    for n in range(parts):
        for part in range(2):
            g = 1 if part == 0 else groups - 2
            copies.append(
                (
                    inner[n].at[part],
                    out_ref.at[:, pl.ds(g * RADIUS, RADIUS), pl.ds(n * per * d, per * d)],
                )
            )
    started = copy_all(copies, sems)
    for n in range(parts):

        @pl.loop(0, per)
        def _(i):
            lanes = pl.ds(pl.multiple_of((i + n * per) * d, d), d)
            for half in range(2):
                cells_of = slice(half * edge, (half + 1) * edge)
                for side in range(2):
                    halo = l_ref if side == 0 else r_ref
                    corner = cu_ref if half == 0 else cd_ref

                    def keys(j):
                        own = halo[j, :, lanes]
                        far = corner[j, side, :, lanes]
                        return jnp.concatenate([far, own] if half == 0 else [own, far], axis=0)

                    f = kf_ref[side, half * edge : half * edge + span]
                    kc = jnp.concatenate([keys(0), f], axis=1)
                    g = 0 if side == 0 else groups - 1
                    q = p_ref[0, g, cells_of, lanes].astype(F32) * scale
                    qf = qf_ref[g, cells_of]
                    qc = jnp.concatenate(
                        [
                            jnp.concatenate([x.astype(BF16), qf], axis=1)
                            for x in (jnp.where(low, q, 0.0), jnp.where(low, 0.0, q))
                        ],
                        axis=0,
                    )
                    s = dot(kc, qc, NT)
                    st = states[n]
                    high1 = st[i, half, side, d : d + 1]
                    total1 = st[i, half, side, d + 1 : d + 2]
                    high = jnp.maximum(high1, jnp.max(s, axis=0, keepdims=True))
                    fade = jnp.exp(high1 - high)
                    w = jnp.exp(s - high)
                    total = total1 * fade + jnp.sum(w, axis=0, keepdims=True)
                    acc = st[i, half, side, :d] * fade + dot(keys(1), w.astype(BF16), TN)
                    t = jnp.transpose(acc / total)
                    t = jnp.where(low, t[:edge], t[edge:])
                    rows_of = slice(half * RADIUS, (half + 1) * RADIUS)
                    edge_ref[side, rows_of, :, lanes] = t.reshape(RADIUS, RADIUS, d).astype(BF16)

    copies = []
    for side in range(2):
        g = 0 if side == 0 else groups - 1
        copies.append(
            (edge_ref.at[side], out_ref.at[:, pl.ds(g * RADIUS, RADIUS)])
        )
    started += copy_all(copies, sems.at[pl.ds(2 * parts, 2)])
    for c in started:
        c.wait()


def edges(pg, left, right, corner_up, corner_down, qf, kf, inner, states, scale, tr, tc):
    _, groups, cells, width = pg.shape
    parts = len(states)
    return pl.pallas_call(
        functools.partial(edge_kernel, scale, parts),
        in_specs=[VMEM] * (7 + 2 * parts),
        out_specs=HBM,
        out_shape=jax.ShapeDtypeStruct((tr, tc, width), BF16),
        scratch_shapes=[
            pltpu.VMEM((2, tr, RADIUS, width), BF16),
            pltpu.SemaphoreType.DMA((2 * parts + 2,)),
        ],
        cost_estimate=pl.CostEstimate(
            flops=500_000_000, bytes_accessed=3_000_000, transcendentals=800_000
        ),
        compiler_params=PARAMS,
        name="edges",
    )(pg, left, right, corner_up, corner_down, qf, kf, *inner, *states)


def local(patches, registers):
    _, tr, tc, width = patches.shape
    groups = tc // RADIUS
    cells = tr * RADIUS
    edge = RADIUS * RADIUS
    assert tr == 2 * RADIUS and groups == 4 and 2 * width == HEADS * LANES
    scale = (width // HEADS) ** (-0.5)
    row_at, row_n = lax.axis_index("row"), lax.axis_size("row")
    col_at, col_n = lax.axis_index("col"), lax.axis_size("col")

    to_right, to_left, to_down, to_up = pack(patches)
    left = shift(to_right, "col", 1).reshape(2, cells, width)
    right = shift(to_left, "col", -1).reshape(2, cells, width)
    up = shift(to_down, "row", 1).reshape(2, groups, edge, width)
    down = shift(to_up, "row", -1).reshape(2, groups, edge, width)

    flag = jnp.where((row_at == 0) & (col_at == 0), 0.0, -1e30).astype(F32).reshape(1)
    pg, part = prep(patches, registers, flag, scale)
    pg = pg.reshape(3, groups, cells, width)
    part = merge_over(merge_over(part, "row"), "col")
    register_out = (part[0] / part[2]).astype(BF16)

    key_rows = np.repeat(np.arange(-RADIUS, tr + RADIUS), RADIUS)
    key_cols = np.tile(np.arange(RADIUS), tr + 2 * RADIUS)
    stack = lambda cols: np.stack([key_features(key_rows, key_cols + c, tr, tc) for c in cols])
    row = jnp.arange((tr + 2 * RADIUS) * RADIUS, dtype=jnp.int32)[None, :, None]
    off_rows = ((row < edge) & (row_at == 0)) | ((row >= edge + cells) & (row_at == row_n - 1))
    side = jnp.arange(2, dtype=jnp.int32)[:, None, None]
    off_cols = ((side == 0) & (col_at == 0)) | ((side == 1) & (col_at == col_n - 1))
    off_lane = LANES - 1
    kf = with_grid_edge(stack([g * RADIUS for g in range(groups)]), (off_rows, off_lane))
    kf_side = with_grid_edge(stack([-RADIUS, tc]), (off_rows | off_cols, off_lane))
    q_rows = np.repeat(np.arange(tr), RADIUS)
    q_cols = np.tile(np.arange(RADIUS), tr)
    qf = np.stack([query_features(q_rows, q_cols + g * RADIUS, tr, tc) for g in range(groups)])
    qf[..., off_lane] = 1.0
    qf = jnp.asarray(qf.astype(BF16))

    pairs = HEADS // 2
    parts = 2
    per = pairs // parts
    done = [centre(pg, up, down, registers, qf, kf, scale, n * per, per) for n in range(parts)]
    corner_up = shift(jnp.stack([left[:, -edge:], right[:, -edge:]], axis=1), "row", 1)
    corner_down = shift(jnp.stack([left[:, :edge], right[:, :edge]], axis=1), "row", -1)
    inner = [x[0].reshape(2, tr, RADIUS, per * LANES) for x in done]
    out = edges(
        pg, left, right, corner_up, corner_down, qf, kf_side, inner, [x[1] for x in done], scale, tr, tc
    )
    return (out, register_out)


def solution(mesh):
    in_specs = (P(None, "row", "col", None), P())
    out_specs = (P("row", "col", None), P())
    return jax.shard_map(local, mesh=mesh, in_specs=in_specs, out_specs=out_specs, check_vma=False)
```

time: 294 us -> 84.3 us (0.29)
  blocking collectives: 114 us -> 0 us
  matrix products: 102 us -> 0 us
  Pallas kernels: 0 us -> 34.7 us
  local copies, waits for them, and re-layouts: 34.5 us -> 4.9 us
  waiting for transfers between devices: 0.01 us -> 22.2 us
  other arithmetic: 18.4 us -> 2.29 us
  loops' own time: 9.43 us -> 0 us
  starting transfers between devices: 12 us -> 18.2 us
    dot_general x68 -> x0, matrix products: 102 us -> none  [the longest x16 49.7 us: one_head(): jnp.einsum('qd,kd->qk', head_queries, head_keys, preferred_element_type=j...]
    psum x1 -> x0, blocking collectives: 74.4 us -> none  [local(): lax.psum((local_totals * factor, local_weighted * factor[..., None]), ('r...]
    pmax x1 -> x0, blocking collectives: 39.2 us -> none  [local(): global_high = lax.pmax(local_high, ('row', 'col'))]
    pallas_call x0 -> x5, Pallas kernels: none -> 34.7 us  [the longest x2 20.1 us: centre(): pl.pallas_call(functools.partial(centre_kernel, scale, first), in_specs=[...]
    ppermute x4 -> x11, waiting for transfers between devices: 0.01 us -> 22.2 us  [the longest x5 14.4 us: merge_over(): lax.ppermute(part, axis, [(i, i ^ step) for i in range(n)])]
    slice x21 -> x0, local copies, waits for them, and re-layouts: 10.6 us -> none  [the longest x1 3.71 us: local(): own_keys = patches[1].reshape(cells, HEADS, head_size)]
    reduce_sum x34 -> x0, other arithmetic: 10.5 us -> none  [the longest x32 9.47 us: one_head(): totals = jnp.sum(weights, axis=1) + jnp.sum(reg_weights, axis=1)]
    another operation x1 -> x0, loops' own time: 9.43 us -> none  [local(): per_head = lax.map(one_head, jnp.arange(HEADS, dtype=jnp.int32))]
  transfers between devices with their start and end apart: 4 -> 11, of which waited for: 0 -> 5; matrix products, arithmetic and copies ran while one was open for 7% -> 5% of each run, Pallas kernels for 0% -> 27%
where the time goes in v2:
time: 84.3 us; the launch traced here: 83.2 us
  Pallas kernels  34.7 us (41%)
  waiting for transfers between devices  22.2 us (26%)
  starting transfers between devices  18.2 us (22%)
  local copies, waits for them, and re-layouts  4.9 us (6%)
  other arithmetic  2.29 us (3%)
  between operations  0.96 us (1%)
    pallas_call x2, Pallas kernels, centre(): pl.pallas_call(functools.partial(centre_kernel, scale, first), in_specs=[...  20.1 us
    ppermute x6, starting transfers between devices, shift(): lax.ppermute(x, axis, [(i, i + step) for i in range(n) if 0 <= i + step <...  17 us
    ppermute x5, waiting for transfers between devices, merge_over(): lax.ppermute(part, axis, [(i, i ^ step) for i in range(n)])  14.4 us
    pallas_call x1, Pallas kernels, edges(): pl.pallas_call(functools.partial(edge_kernel, scale, parts), in_specs=[VM...  10.2 us
    ppermute x6, waiting for transfers between devices, shift(): lax.ppermute(x, axis, [(i, i + step) for i in range(n) if 0 <= i + step <...  7.8 us
    unnamed x12, local copies, waits for them, and re-layouts  2.7 us
    pallas_call x1, Pallas kernels, pack(): pl.pallas_call(pack_kernel, in_specs=[HBM], out_specs=[VMEM] * 4, out_sha...  2.34 us
    another operation x2, local copies, waits for them, and re-layouts, local(): jnp.stack([left[:, :edge], right[:, :edge]], axis=1)  2.17 us
  transfers between devices with their start and end apart: 11, of which 5 were waited for; matrix products, arithmetic and copies ran while one was open for 5% of the time, Pallas kernels for 27%

profile of v2, /device:TPU:19, one launch (start us, length us, event | category | flops | bytes accessed | tf_op | source)
XLA Modules:
  0.0 83.2 jit_solution(2366444215694375558)
XLA Ops:
  0.7 1.9 %copy-done = bf16[3,16,32,1024]{3,2,1,0:T(8,128)(2,1)S(1)} copy-done((bf16[3,16,32,1024]{3,2,1,0:T(8,128)(2,1)S(1)}, bf16[3,16,32,1024]{3,2,1,0:T(8,128)(2,1)}, u32[]{:S(2)}) %copy-start) | copy-done | bytes 3145752
  2.5 0.8 copy-done.3
  3.3 2.0 %prep.1 = (bf16[3,4,16,8,1024]{4,3,2,1,0:T(8,128)(2,1)S(1)}, f32[3,8,1024]{2,1,0:T(8,128)S(1)}) custom-call(f32[1]{0:T(128)} %bitcast.flag_ref, bf16[3,8,1024]{2,1,0:T(8,128)(2,1)S(1)} %copy-done.3, bf16[3,16,32,1024]{3,2,1,0:T(8,128)(2,1)S(1)} %copy-done), custom_call_target="tpu_custom_call" | custom-call | flops 300000000 | bytes 4000000 | tf_op jit(solution)/shard_map/prep/pallas_call | solution.py:143
  5.3 0.0 copy-start.5
  5.3 0.7 collective-permute-start.6
  6.1 2.3 %pack.1 = (bf16[2,16,8,1024]{3,2,1,0:T(8,128)(2,1)}, bf16[2,16,8,1024]{3,2,1,0:T(8,128)(2,1)}, bf16[2,4,8,8,1024]{4,3,2,1,0:T(8,128)(2,1)}, bf16[2,4,8,8,1024]{4,3,2,1,0:T(8,128)(2,1)}) custom-call(bf16[3,16,32,1024]{3,2,1,0:T(8,128)(2,1)S(1)} %copy-done.1), custom_call_target="tpu_custom_call" | custom-call | tf_op jit(solution)/shard_map/pack/pallas_call | solution.py:83
  8.4 1.9 %collective-permute-start.5 = (bf16[2,4,8,8,1024]{4,3,2,1,0:T(8,128)(2,1)}, bf16[2,4,8,8,1024]{4,3,2,1,0:T(8,128)(2,1)}, u32[]{:S(2)}, u32[]{:S(2)}) collective-permute-start(bf16[2,4,8,8,1024]{4,3,2,1,0:T(8,128)(2,1)} %get-tuple-element.16), channel_id=1, source_target_pairs={{4,0},{8,4},{12,8},{16,12},{20,16},{24,20},{28,24},{5,1},{9,5},{13... | collective-permute-start | bytes 3145736 | tf_op jit(solution)/shard_map/ppermute | solution.py:32
  10.4 3.6 %collective-permute-start.4 = (bf16[2,4,8,8,1024]{4,3,2,1,0:T(8,128)(2,1)}, bf16[2,4,8,8,1024]{4,3,2,1,0:T(8,128)(2,1)}, u32[]{:S(2)}, u32[]{:S(2)}) collective-permute-start(bf16[2,4,8,8,1024]{4,3,2,1,0:T(8,128)(2,1)} %get-tuple-element.15), channel_id=1, source_target_pairs={{0,4},{4,8},{8,12},{12,16},{16,20},{20,24},{24,28},{1,5},{5,9},{9,... | collective-permute-start | bytes 3145736 | tf_op jit(solution)/shard_map/ppermute | solution.py:32
  14.0 3.1 %collective-permute-start = (bf16[2,16,8,1024]{3,2,1,0:T(8,128)(2,1)}, bf16[2,16,8,1024]{3,2,1,0:T(8,128)(2,1)}, u32[]{:S(2)}, u32[]{:S(2)}) collective-permute-start(bf16[2,16,8,1024]{3,2,1,0:T(8,128)(2,1)} %get-tuple-element.13), channel_id=1, source_target_pairs={{0,1},{1,2},{2,3},{4,5},{5,6},{6,7},{8,9},{9,10},{10,11},{12,13},{... | collective-permute-start | bytes 1572872 | tf_op jit(solution)/shard_map/ppermute | solution.py:32
  17.1 3.0 %collective-permute-start.1 = (bf16[2,16,8,1024]{3,2,1,0:T(8,128)(2,1)}, bf16[2,16,8,1024]{3,2,1,0:T(8,128)(2,1)}, u32[]{:S(2)}, u32[]{:S(2)}) collective-permute-start(bf16[2,16,8,1024]{3,2,1,0:T(8,128)(2,1)} %get-tuple-element.14), channel_id=1, source_target_pairs={{1,0},{2,1},{3,2},{5,4},{6,5},{7,6},{9,8},{10,9},{11,10},{13,12},{... | collective-permute-start | bytes 1572872 | tf_op jit(solution)/shard_map/ppermute | solution.py:32
  20.1 1.1 %select_convert_fusion.kf_ref = bf16[4,256,128]{2,1,0:T(8,128)(2,1)S(1)} fusion(bf16[4,256,128]{2,1,0:T(8,128)(2,1)} %constant.137, pred[128]{0:T(512)(128)(4,1)S(1)} %iota_compare_fusion, pred[256]{0:T(512)(128)(4,1)S(1)} %and_or_fusion.1), kind=kLoop, calls=%fused_computation.2 | loop fusion | flops 262144 | bytes 524672 | tf_op jit(solution)/shard_map/convert_element_type | solution.py:50
  21.3 0.1 collective-permute-start.7
  21.4 0.1 broadcast_or_fusion
  21.5 6.6 %collective-permute-done.7 = f32[3,8,1024]{2,1,0:T(8,128)S(1)} collective-permute-done((f32[3,8,1024]{2,1,0:T(8,128)S(1)}, f32[3,8,1024]{2,1,0:T(8,128)S(1)}, u32[]{:S(2)}, u32[]{:S(2)}) %collective-permute-start.7) | collective-permute-done | bytes 98336 | tf_op jit(solution)/shard_map/ppermute | solution.py:174
  28.1 0.1 collective-permute-start.8
  28.2 0.1 select_convert_fusion.1.kf_ref
  28.4 5.6 %collective-permute-done.8 = f32[3,8,1024]{2,1,0:T(8,128)S(1)} collective-permute-done((f32[3,8,1024]{2,1,0:T(8,128)S(1)}, f32[3,8,1024]{2,1,0:T(8,128)S(1)}, u32[]{:S(2)}, u32[]{:S(2)}) %collective-permute-start.8) | collective-permute-done | bytes 98336 | tf_op jit(solution)/shard_map/ppermute | solution.py:174
  34.1 0.1 collective-permute-start.9
  34.2 1.1 %slice_bitcast_fusion.1 = (bf16[2,1,64,1024]{3,2,1,0:T(8,128)(2,1)S(1)}, bf16[2,1,64,1024]{3,2,0,1:T(8,128)(2,1)S(1)}) fusion(bf16[2,128,1024]{2,1,0:T(8,128)(2,1)} %bitcast.2.l_ref), kind=kLoop, calls=%fused_computation.4 | loop fusion | bytes 1048576 | tf_op jit(solution)/shard_map/stack | solution.py:395
  35.3 6.7 %collective-permute-done.1 = bf16[2,16,8,1024]{3,2,1,0:T(8,128)(2,1)} collective-permute-done((bf16[2,16,8,1024]{3,2,1,0:T(8,128)(2,1)}, bf16[2,16,8,1024]{3,2,1,0:T(8,128)(2,1)}, u32[]{:S(2)}, u32[]{:S(2)}) %collective-permute-start.1) | collective-permute-done | bytes 524320 | tf_op jit(solution)/shard_map/ppermute | solution.py:32
  42.1 1.1 %slice_bitcast_fusion = (bf16[2,1,64,1024]{3,2,1,0:T(8,128)(2,1)S(1)}, bf16[2,1,64,1024]{3,2,0,1:T(8,128)(2,1)S(1)}) fusion(bf16[2,128,1024]{2,1,0:T(8,128)(2,1)} %bitcast.3.r_ref), kind=kLoop, calls=%fused_computation.3 | loop fusion | bytes 1048576 | tf_op jit(solution)/shard_map/stack | solution.py:395
  43.1 0.1 pad_maximum_fusion
  43.2 3.5 %collective-permute-start.2 = (bf16[2,2,64,1024]{3,2,0,1:T(8,128)(2,1)S(1)}, bf16[2,2,64,1024]{3,2,0,1:T(8,128)(2,1)S(1)}, u32[]{:S(2)}, u32[]{:S(2)}) collective-permute-start(bf16[2,2,64,1024]{3,2,0,1:T(8,128)(2,1)S(1)} %pad_maximum_fusion), channel_id=1, source_target_pairs={{0,4},{4,8},{8,12},{12,16},{16,20},{20,24},{24,28},{1,5},{5,9},{9,... | collective-permute-start | bytes 1572872 | tf_op jit(solution)/shard_map/ppermute | solution.py:32
  46.7 0.1 collective-permute-start.10
  46.8 0.1 pad_maximum_fusion.1
  46.9 1.9 %collective-permute-start.3 = (bf16[2,2,64,1024]{3,2,1,0:T(8,128)(2,1)S(1)}, bf16[2,2,64,1024]{3,2,1,0:T(8,128)(2,1)S(1)}, u32[]{:S(2)}, u32[]{:S(2)}) collective-permute-start(bf16[2,2,64,1024]{3,2,1,0:T(8,128)(2,1)S(1)} %pad_maximum_fusion.1), channel_id=1, source_target_pairs={{4,0},{8,4},{12,8},{16,12},{20,16},{24,20},{28,24},{5,1},{9,5},{13... | collective-permute-start | bytes 1572872 | tf_op jit(solution)/shard_map/ppermute | solution.py:32
  48.8 2.2 %collective-permute-done.10 = f32[3,8,1024]{2,1,0:T(8,128)S(1)} collective-permute-done((f32[3,8,1024]{2,1,0:T(8,128)S(1)}, f32[3,8,1024]{2,1,0:T(8,128)S(1)}, u32[]{:S(2)}, u32[]{:S(2)}) %collective-permute-start.10) | collective-permute-done | bytes 98336 | tf_op jit(solution)/shard_map/ppermute | solution.py:174
  51.0 0.7 fusion.36
  51.7 1.1 %collective-permute-done.2 = bf16[2,2,64,1024]{3,2,0,1:T(8,128)(2,1)S(1)} collective-permute-done((bf16[2,2,64,1024]{3,2,0,1:T(8,128)(2,1)S(1)}, bf16[2,2,64,1024]{3,2,0,1:T(8,128)(2,1)S(1)}, u32[]{:S(2)}, u32[]{:S(2)}) %collective-permute-start.2) | collective-permute-done | bytes 524320 | tf_op jit(solution)/shard_map/ppermute | solution.py:32
  52.8 10.0 %centre.2 = (bf16[2,128,512]{2,1,0:T(8,128)(2,1)S(1)}, f32[4,2,2,136,128]{4,3,2,1,0:T(8,128)S(1)}) custom-call(bf16[3,4,128,1024]{3,2,1,0:T(8,128)(2,1)S(1)} %bitcast.216, bf16[2,4,64,1024]{3,2,1,0:T(8,128)(2,1)} %bitcast.9.up_ref, bf16[2,4,64,1024]{3,2,1,0:T(8,128)(2,1)} %bitcast.10.down_ref, bf16[3,8,1024]{2,1,0:T(8,128)(2,1)S(1)} %copy-done.4, ...), custom_call_target="tpu_custom_call" | custom-call | flops 1862270976 | bytes 4000000 | tf_op jit(solution)/shard_map/centre/pallas_call | solution.py:240
  62.9 10.1 %centre.3 = (bf16[2,128,512]{2,1,0:T(8,128)(2,1)S(1)}, f32[4,2,2,136,128]{4,3,2,1,0:T(8,128)S(1)}) custom-call(bf16[3,4,128,1024]{3,2,1,0:T(8,128)(2,1)S(1)} %bitcast.217, bf16[2,4,64,1024]{3,2,1,0:T(8,128)(2,1)} %bitcast.9.up_ref, bf16[2,4,64,1024]{3,2,1,0:T(8,128)(2,1)} %bitcast.10.down_ref, bf16[3,8,1024]{2,1,0:T(8,128)(2,1)S(1)} %copy-done.4, ...), custom_call_target="tpu_custom_call" | custom-call | flops 1862270976 | bytes 4000000 | tf_op jit(solution)/shard_map/centre/pallas_call | solution.py:240
  73.0 10.2 %edges.1 = bf16[16,32,1024]{2,1,0:T(8,128)(2,1)} custom-call(bf16[3,4,128,1024]{3,2,1,0:T(8,128)(2,1)S(1)} %bitcast.218, bf16[2,128,1024]{2,1,0:T(8,128)(2,1)} %bitcast.2.l_ref, bf16[2,128,1024]{2,1,0:T(8,128)(2,1)} %bitcast.3.r_ref, bf16[2,2,64,1024]{3,2,1,0:T(8,128)(2,1)S(1)} %copy.8.cu_ref, bf16[2,2,64,1024]{3,2,1,0:T(8,128)(2,1)S(1)} %collective-permute-done.3.cd_ref, ...), custom_call_target="tpu_custom_call" | custom-call | flops 500000000 | bytes 3000000 | tf_op jit(solution)/shard_map/edges/pallas_call | solution.py:335
  (30 shorter events, 0.3 us)
Async XLA Ops:
  0.6 1.9 %copy-start = (bf16[3,16,32,1024]{3,2,1,0:T(8,128)(2,1)S(1)}, bf16[3,16,32,1024]{3,2,1,0:T(8,128)(2,1)}, u32[]{:S(2)}) copy-start(bf16[3,16,32,1024]{3,2,1,0:T(8,128)(2,1)} %p_ref.3) | copy-start | bytes 9437188
  2.5 0.8 copy-start.3
  3.3 2.7 %copy-start.1 = (bf16[3,16,32,1024]{3,2,1,0:T(8,128)(2,1)S(1)}, bf16[3,16,32,1024]{3,2,1,0:T(8,128)(2,1)}, u32[]{:S(2)}) copy-start(bf16[3,16,32,1024]{3,2,1,0:T(8,128)(2,1)} %p_ref.3) | copy-start | bytes 9437188
  5.3 22.9 %copy-start.5 = (bf16[2,256,128]{2,1,0:T(8,128)(2,1)S(1)}, bf16[2,256,128]{2,1,0:T(8,128)(2,1)}, u32[]{:S(2)}) copy-start(bf16[2,256,128]{2,1,0:T(8,128)(2,1)} %constant.136) | copy-start | bytes 393220
  5.3 15.9 %collective-permute-start.6 = (f32[3,8,1024]{2,1,0:T(8,128)S(1)}, f32[3,8,1024]{2,1,0:T(8,128)S(1)}, u32[]{:S(2)}, u32[]{:S(2)}) collective-permute-start(f32[3,8,1024]{2,1,0:T(8,128)S(1)} %get-tuple-element.21), channel_id=1, source_target_pairs={{0,4},{4,0},{8,12},{12,8},{16,20},{20,16},{24,28},{28,24},{1,5},{5... | collective-permute-start | bytes 294920 | tf_op jit(solution)/shard_map/ppermute | solution.py:174
  8.4 44.4 %collective-permute-start.5 = (bf16[2,4,8,8,1024]{4,3,2,1,0:T(8,128)(2,1)}, bf16[2,4,8,8,1024]{4,3,2,1,0:T(8,128)(2,1)}, u32[]{:S(2)}, u32[]{:S(2)}) collective-permute-start(bf16[2,4,8,8,1024]{4,3,2,1,0:T(8,128)(2,1)} %get-tuple-element.16), channel_id=1, source_target_pairs={{4,0},{8,4},{12,8},{16,12},{20,16},{24,20},{28,24},{5,1},{9,5},{13... | collective-permute-start | bytes 3145736 | tf_op jit(solution)/shard_map/ppermute | solution.py:32
  10.4 42.4 %collective-permute-start.4 = (bf16[2,4,8,8,1024]{4,3,2,1,0:T(8,128)(2,1)}, bf16[2,4,8,8,1024]{4,3,2,1,0:T(8,128)(2,1)}, u32[]{:S(2)}, u32[]{:S(2)}) collective-permute-start(bf16[2,4,8,8,1024]{4,3,2,1,0:T(8,128)(2,1)} %get-tuple-element.15), channel_id=1, source_target_pairs={{0,4},{4,8},{8,12},{12,16},{16,20},{20,24},{24,28},{1,5},{5,9},{9,... | collective-permute-start | bytes 3145736 | tf_op jit(solution)/shard_map/ppermute | solution.py:32
  14.0 20.2 %collective-permute-start = (bf16[2,16,8,1024]{3,2,1,0:T(8,128)(2,1)}, bf16[2,16,8,1024]{3,2,1,0:T(8,128)(2,1)}, u32[]{:S(2)}, u32[]{:S(2)}) collective-permute-start(bf16[2,16,8,1024]{3,2,1,0:T(8,128)(2,1)} %get-tuple-element.13), channel_id=1, source_target_pairs={{0,1},{1,2},{2,3},{4,5},{5,6},{6,7},{8,9},{9,10},{10,11},{12,13},{... | collective-permute-start | bytes 1572872 | tf_op jit(solution)/shard_map/ppermute | solution.py:32
  17.1 24.9 %collective-permute-start.1 = (bf16[2,16,8,1024]{3,2,1,0:T(8,128)(2,1)}, bf16[2,16,8,1024]{3,2,1,0:T(8,128)(2,1)}, u32[]{:S(2)}, u32[]{:S(2)}) collective-permute-start(bf16[2,16,8,1024]{3,2,1,0:T(8,128)(2,1)} %get-tuple-element.14), channel_id=1, source_target_pairs={{1,0},{2,1},{3,2},{5,4},{6,5},{7,6},{9,8},{10,9},{11,10},{13,12},{... | collective-permute-start | bytes 1572872 | tf_op jit(solution)/shard_map/ppermute | solution.py:32
  21.3 6.7 %collective-permute-start.7 = (f32[3,8,1024]{2,1,0:T(8,128)S(1)}, f32[3,8,1024]{2,1,0:T(8,128)S(1)}, u32[]{:S(2)}, u32[]{:S(2)}) collective-permute-start(f32[3,8,1024]{2,1,0:T(8,128)S(1)} %pad_maximum_fusion.2), channel_id=1, source_target_pairs={{0,8},{4,12},{8,0},{12,4},{16,24},{20,28},{24,16},{28,20},{1,9},{5... | collective-permute-start | bytes 294920 | tf_op jit(solution)/shard_map/ppermute | solution.py:174
  28.1 5.9 %collective-permute-start.8 = (f32[3,8,1024]{2,1,0:T(8,128)S(1)}, f32[3,8,1024]{2,1,0:T(8,128)S(1)}, u32[]{:S(2)}, u32[]{:S(2)}) collective-permute-start(f32[3,8,1024]{2,1,0:T(8,128)S(1)} %pad_maximum_fusion.3), channel_id=1, source_target_pairs={{0,16},{4,20},{8,24},{12,28},{16,0},{20,4},{24,8},{28,12},{1,17},{... | collective-permute-start | bytes 294920 | tf_op jit(solution)/shard_map/ppermute | solution.py:174
  34.1 12.6 %collective-permute-start.9 = (f32[3,8,1024]{2,1,0:T(8,128)S(1)}, f32[3,8,1024]{2,1,0:T(8,128)S(1)}, u32[]{:S(2)}, u32[]{:S(2)}) collective-permute-start(f32[3,8,1024]{2,1,0:T(8,128)S(1)} %pad_maximum_fusion.4), channel_id=1, source_target_pairs={{0,1},{1,0},{2,3},{3,2},{4,5},{5,4},{6,7},{7,6},{8,9},{9,8},{10,11... | collective-permute-start | bytes 294920 | tf_op jit(solution)/shard_map/ppermute | solution.py:174
  34.2 18.6 %copy-start.2 = (bf16[4,128,128]{2,1,0:T(8,128)(2,1)S(1)}, bf16[4,128,128]{2,1,0:T(8,128)(2,1)}, u32[]{:S(2)}) copy-start(bf16[4,128,128]{2,1,0:T(8,128)(2,1)} %constant.39.clone.qf_ref) | copy-start | bytes 393220
  34.2 18.6 %copy-start.4 = (bf16[3,8,1024]{2,1,0:T(8,128)(2,1)S(1)}, bf16[3,8,1024]{2,1,0:T(8,128)(2,1)}, u32[]{:S(2)}) copy-start(bf16[3,8,1024]{2,1,0:T(8,128)(2,1)} %reg_ref.5) | copy-start | bytes 147460
  43.2 9.6 %collective-permute-start.2 = (bf16[2,2,64,1024]{3,2,0,1:T(8,128)(2,1)S(1)}, bf16[2,2,64,1024]{3,2,0,1:T(8,128)(2,1)S(1)}, u32[]{:S(2)}, u32[]{:S(2)}) collective-permute-start(bf16[2,2,64,1024]{3,2,0,1:T(8,128)(2,1)S(1)} %pad_maximum_fusion), channel_id=1, source_target_pairs={{0,4},{4,8},{8,12},{12,16},{16,20},{20,24},{24,28},{1,5},{5,9},{9,... | collective-permute-start | bytes 1572872 | tf_op jit(solution)/shard_map/ppermute | solution.py:32
  46.7 4.3 %collective-permute-start.10 = (f32[3,8,1024]{2,1,0:T(8,128)S(1)}, f32[3,8,1024]{2,1,0:T(8,128)S(1)}, u32[]{:S(2)}, u32[]{:S(2)}) collective-permute-start(f32[3,8,1024]{2,1,0:T(8,128)S(1)} %pad_maximum_fusion.5), channel_id=1, source_target_pairs={{0,2},{1,3},{2,0},{3,1},{4,6},{5,7},{6,4},{7,5},{8,10},{9,11},{10,... | collective-permute-start | bytes 294920 | tf_op jit(solution)/shard_map/ppermute | solution.py:174
  46.9 26.1 %collective-permute-start.3 = (bf16[2,2,64,1024]{3,2,1,0:T(8,128)(2,1)S(1)}, bf16[2,2,64,1024]{3,2,1,0:T(8,128)(2,1)S(1)}, u32[]{:S(2)}, u32[]{:S(2)}) collective-permute-start(bf16[2,2,64,1024]{3,2,1,0:T(8,128)(2,1)S(1)} %pad_maximum_fusion.1), channel_id=1, source_target_pairs={{4,0},{8,4},{12,8},{16,12},{20,16},{24,20},{28,24},{5,1},{9,5},{13... | collective-permute-start | bytes 1572872 | tf_op jit(solution)/shard_map/ppermute | solution.py:32

commit v3 on v2

--- a/solution.py
+++ b/solution.py
@@ -8,7 +8,9 @@
 from jax.experimental.pallas import tpu as pltpu
 from jax.sharding import PartitionSpec as P
 
+
 HEADS = 16
+PARTS = 4
 RADIUS = 8
 FAR = -30000.0
 LANES = 128
@@ -59,15 +61,21 @@
     return started
 
 
-def pack_kernel(p_ref, right_ref, left_ref, down_ref, up_ref, sems):
-    _, tr, tc, _ = p_ref.shape
-    groups = tc // RADIUS
+def pack_sides_kernel(p_ref, right_ref, left_ref, sems):
+    tc = p_ref.shape[2]
     copies = []
     for j in range(2):
         copies.append((p_ref.at[1 + j, :, pl.ds(tc - RADIUS, RADIUS)], right_ref.at[j]))
         copies.append((p_ref.at[1 + j, :, pl.ds(0, RADIUS)], left_ref.at[j]))
+    for c in copy_all(copies, sems):
+        c.wait()
+
+
+def pack_rows_kernel(p_ref, down_ref, up_ref, sems):
+    _, tr, tc, _ = p_ref.shape
+    copies = []
     for j in range(2):
-        for g in range(groups):
+        for g in range(tc // RADIUS):
             cols = pl.ds(g * RADIUS, RADIUS)
             copies.append((p_ref.at[1 + j, pl.ds(tr - RADIUS, RADIUS), cols], down_ref.at[j, g]))
             copies.append((p_ref.at[1 + j, pl.ds(0, RADIUS), cols], up_ref.at[j, g]))
@@ -75,19 +83,15 @@
         c.wait()
 
 
-def pack(patches):
-    _, tr, tc, width = patches.shape
-    groups = tc // RADIUS
-    side = pltpu.VMEM((2, tr, RADIUS, width), BF16)
-    rows = pltpu.VMEM((2, groups, RADIUS, RADIUS, width), BF16)
+def pack(kernel, patches, shape, copies):
+    payload = pltpu.VMEM(shape, BF16)
     return pl.pallas_call(
-        pack_kernel,
+        kernel,
         in_specs=[HBM],
-        out_specs=[VMEM] * 4,
-        out_shape=[side, side, rows, rows],
-        scratch_shapes=[pltpu.SemaphoreType.DMA((4 + 4 * groups,))],
+        out_specs=[VMEM] * 2,
+        out_shape=[payload] * 2,
+        scratch_shapes=[pltpu.SemaphoreType.DMA((copies,))],
         compiler_params=PARAMS,
-        name="pack",
     )(patches)
 
 
@@ -171,13 +175,14 @@
         return functools.reduce(merge, [every[i] for i in range(n)])
     step = 1
     while step < n:
-        part = merge(part, lax.ppermute(part, axis, [(i, i ^ step) for i in range(n)]))
+        other = lax.ppermute(part, axis, [(i, i ^ step) for i in range(n)])
+        part = merge(part, other)
         step *= 2
     return part
 
 
 def centre_kernel(scale, first, p_ref, up_ref, down_ref, reg_ref, qf_ref, kf_ref, in_ref, st_ref):
-    _, groups, cells, width = p_ref.shape
+    _, _, cells, width = p_ref.shape
     d = LANES
     head = width // HEADS
     edge = RADIUS * RADIUS
@@ -232,7 +237,7 @@
 
 
 def centre(pg, up, down, registers, qf, kf, scale, first, pairs):
-    _, groups, cells, width = pg.shape
+    _, _, cells, _ = pg.shape
     edge = RADIUS * RADIUS
     d = LANES
     keys = 3 * (cells + edge) + 2 * RADIUS
@@ -289,7 +294,7 @@
 
                     def keys(j):
                         own = halo[j, :, lanes]
-                        far = corner[j, side, :, lanes]
+                        far = corner[side, j, :, lanes]
                         return jnp.concatenate([far, own] if half == 0 else [own, far], axis=0)
 
                     f = kf_ref[side, half * edge : half * edge + span]
@@ -330,7 +335,7 @@
 
 
 def edges(pg, left, right, corner_up, corner_down, qf, kf, inner, states, scale, tr, tc):
-    _, groups, cells, width = pg.shape
+    _, _, _, width = pg.shape
     parts = len(states)
     return pl.pallas_call(
         functools.partial(edge_kernel, scale, parts),
@@ -359,14 +364,19 @@
     row_at, row_n = lax.axis_index("row"), lax.axis_size("row")
     col_at, col_n = lax.axis_index("col"), lax.axis_size("col")
 
-    to_right, to_left, to_down, to_up = pack(patches)
-    left = shift(to_right, "col", 1).reshape(2, cells, width)
-    right = shift(to_left, "col", -1).reshape(2, cells, width)
-    up = shift(to_down, "row", 1).reshape(2, groups, edge, width)
-    down = shift(to_up, "row", -1).reshape(2, groups, edge, width)
+    source = pltpu.with_memory_space_constraint(patches, pltpu.HBM)
+    to_right, to_left = pack(pack_sides_kernel, source, (2, tr, RADIUS, width), 4)
+    left = shift(to_right, "col", 1)
+    right = shift(to_left, "col", -1)
+    shape = (2, groups, RADIUS, RADIUS, width)
+    to_down, to_up = pack(pack_rows_kernel, source, shape, 4 * groups)
+    up = shift(to_down, "row", 1)
+    down = shift(to_up, "row", -1)
+    left, right = (x.reshape(2, cells, width) for x in (left, right))
+    up, down = (x.reshape(2, groups, edge, width) for x in (up, down))
 
     flag = jnp.where((row_at == 0) & (col_at == 0), 0.0, -1e30).astype(F32).reshape(1)
-    pg, part = prep(patches, registers, flag, scale)
+    pg, part = prep(source, registers, flag, scale)
     pg = pg.reshape(3, groups, cells, width)
     part = merge_over(merge_over(part, "row"), "col")
     register_out = (part[0] / part[2]).astype(BF16)
@@ -388,11 +398,17 @@
     qf = jnp.asarray(qf.astype(BF16))
 
     pairs = HEADS // 2
-    parts = 2
+    parts = PARTS
     per = pairs // parts
-    done = [centre(pg, up, down, registers, qf, kf, scale, n * per, per) for n in range(parts)]
-    corner_up = shift(jnp.stack([left[:, -edge:], right[:, -edge:]], axis=1), "row", 1)
-    corner_down = shift(jnp.stack([left[:, :edge], right[:, :edge]], axis=1), "row", -1)
+    done = []
+    for n in range(parts):
+        done.append(centre(pg, up, down, registers, qf, kf, scale, n * per, per))
+    near_l, near_r, first_state = lax.optimization_barrier((left, right, done[0][1]))
+    done[0] = (done[0][0], first_state)
+    bottom = jnp.stack([near_l[:, -edge:], near_r[:, -edge:]])
+    corner_up = shift(bottom, "row", 1)
+    top = jnp.stack([near_l[:, :edge], near_r[:, :edge]])
+    corner_down = shift(top, "row", -1)
     inner = [x[0].reshape(2, tr, RADIUS, per * LANES) for x in done]
     out = edges(
         pg, left, right, corner_up, corner_down, qf, kf_side, inner, [x[1] for x in done], scale, tr, tc

time: 84.3 us -> 92.9 us (1.10)
  the two profiles are of different devices: /device:TPU:19 before, /device:TPU:9 now
where the time goes in v3:
time: 92.9 us; the launch traced here: 92.1 us
  Pallas kernels  41.5 us (45%)
  starting transfers between devices  30.2 us (33%)
  waiting for transfers between devices  11.8 us (13%)
  other arithmetic  5.35 us (6%)
  local copies, waits for them, and re-layouts  2.19 us (2%)
  between operations  1.01 us (1%)
    ppermute x6, starting transfers between devices, shift(): lax.ppermute(x, axis, [(i, i + step) for i in range(n) if 0 <= i + step <...  23.4 us
    pallas_call x4, Pallas kernels, centre(): pl.pallas_call(functools.partial(centre_kernel, scale, first), in_specs=[...  23.2 us
    ppermute x5, waiting for transfers between devices, merge_over(): other = lax.ppermute(part, axis, [(i, i ^ step) for i in range(n)])  11.8 us
    pallas_call x1, Pallas kernels, edges(): pl.pallas_call(functools.partial(edge_kernel, scale, parts), in_specs=[VM...  10.3 us
    ppermute x5, starting transfers between devices, merge_over(): other = lax.ppermute(part, axis, [(i, i ^ step) for i in range(n)])  6.86 us
    pallas_call x2, Pallas kernels, pack(): pl.pallas_call(kernel, in_specs=[HBM], out_specs=[VMEM] * 2, out_shape=[p...  5.34 us
    pallas_call x1, Pallas kernels, prep(): pl.pallas_call(functools.partial(prep_kernel, scale), in_specs=[SMEM, VME...  2.72 us
  transfers between devices with their start and end apart: 11, of which 4 were waited for; matrix products, arithmetic and copies ran while one was open for 7% of the time, Pallas kernels for 31%

profile of v3, /device:TPU:9, one launch (start us, length us, event | category | flops | bytes accessed | tf_op | source)
XLA Modules:
  0.0 92.1 jit_solution(723033183731505791)
XLA Ops:
  0.6 2.3 %shard_map.68 = (bf16[2,16,8,1024]{3,2,1,0:T(8,128)(2,1)}, bf16[2,16,8,1024]{3,2,1,0:T(8,128)(2,1)}) custom-call(bf16[3,16,32,1024]{3,2,1,0:T(8,128)(2,1)} %p_ref.5), custom_call_target="tpu_custom_call" | custom-call | tf_op jit(solution)/shard_map/pallas_call | solution.py:88
  2.9 3.9 %collective-permute-start = (bf16[2,16,8,1024]{3,2,1,0:T(8,128)(2,1)}, bf16[2,16,8,1024]{3,2,1,0:T(8,128)(2,1)}, u32[]{:S(2)}, u32[]{:S(2)}) collective-permute-start(bf16[2,16,8,1024]{3,2,1,0:T(8,128)(2,1)} %get-tuple-element.20), channel_id=1, source_target_pairs={{0,1},{1,2},{2,3},{4,5},{5,6},{6,7},{8,9},{9,10},{10,11},{12,13},{... | collective-permute-start | bytes 1572872 | tf_op jit(solution)/shard_map/ppermute | solution.py:34
  6.8 1.3 %collective-permute-start.1 = (bf16[2,16,8,1024]{3,2,1,0:T(8,128)(2,1)}, bf16[2,16,8,1024]{3,2,1,0:T(8,128)(2,1)}, u32[]{:S(2)}, u32[]{:S(2)}) collective-permute-start(bf16[2,16,8,1024]{3,2,1,0:T(8,128)(2,1)} %get-tuple-element.21), channel_id=1, source_target_pairs={{1,0},{2,1},{3,2},{5,4},{6,5},{7,6},{9,8},{10,9},{11,10},{13,12},{... | collective-permute-start | bytes 1572872 | tf_op jit(solution)/shard_map/ppermute | solution.py:34
  8.1 3.1 %shard_map.69 = (bf16[2,4,8,8,1024]{4,3,2,1,0:T(8,128)(2,1)}, bf16[2,4,8,8,1024]{4,3,2,1,0:T(8,128)(2,1)}) custom-call(bf16[3,16,32,1024]{3,2,1,0:T(8,128)(2,1)} %p_ref.5), custom_call_target="tpu_custom_call" | custom-call | tf_op jit(solution)/shard_map/pallas_call | solution.py:88
  11.2 4.2 %collective-permute-start.2 = (bf16[2,4,8,8,1024]{4,3,2,1,0:T(8,128)(2,1)}, bf16[2,4,8,8,1024]{4,3,2,1,0:T(8,128)(2,1)}, u32[]{:S(2)}, u32[]{:S(2)}) collective-permute-start(bf16[2,4,8,8,1024]{4,3,2,1,0:T(8,128)(2,1)} %get-tuple-element.22), channel_id=1, source_target_pairs={{0,4},{4,8},{8,12},{12,16},{16,20},{20,24},{24,28},{1,5},{5,9},{9,... | collective-permute-start | bytes 3145736 | tf_op jit(solution)/shard_map/ppermute | solution.py:34
  15.4 1.9 %collective-permute-start.3 = (bf16[2,4,8,8,1024]{4,3,2,1,0:T(8,128)(2,1)}, bf16[2,4,8,8,1024]{4,3,2,1,0:T(8,128)(2,1)}, u32[]{:S(2)}, u32[]{:S(2)}) collective-permute-start(bf16[2,4,8,8,1024]{4,3,2,1,0:T(8,128)(2,1)} %get-tuple-element.23), channel_id=1, source_target_pairs={{4,0},{8,4},{12,8},{16,12},{20,16},{24,20},{28,24},{5,1},{9,5},{13... | collective-permute-start | bytes 3145736 | tf_op jit(solution)/shard_map/ppermute | solution.py:34
  17.4 2.7 %prep.1 = (bf16[3,4,16,8,1024]{4,3,2,1,0:T(8,128)(2,1)S(1)}, f32[3,8,1024]{2,1,0:T(8,128)S(1)}) custom-call(f32[1]{0:T(128)} %bitcast.flag_ref, bf16[3,8,1024]{2,1,0:T(8,128)(2,1)S(1)} %copy-done.1, bf16[3,16,32,1024]{3,2,1,0:T(8,128)(2,1)} %p_ref.5), custom_call_target="tpu_custom_call" | custom-call | flops 300000000 | bytes 4000000 | tf_op jit(solution)/shard_map/prep/pallas_call | solution.py:147
  20.1 0.6 collective-permute-start.6
  20.7 0.9 %collective-permute-done.6 = f32[3,8,1024]{2,1,0:T(8,128)S(1)} collective-permute-done((f32[3,8,1024]{2,1,0:T(8,128)S(1)}, f32[3,8,1024]{2,1,0:T(8,128)S(1)}, u32[]{:S(2)}, u32[]{:S(2)}) %collective-permute-start.6) | collective-permute-done | bytes 98336 | tf_op jit(solution)/shard_map/ppermute | solution.py:178
  21.7 0.7 pad_maximum_fusion.2
  22.4 0.1 collective-permute-start.7
  22.5 1.1 %select_convert_fusion.kf_ref = bf16[4,256,128]{2,1,0:T(8,128)(2,1)S(1)} fusion(bf16[4,256,128]{2,1,0:T(8,128)(2,1)} %constant.136, pred[128]{0:T(512)(128)(4,1)S(1)} %iota_compare_fusion, pred[256]{0:T(512)(128)(4,1)S(1)} %and_or_fusion.1), kind=kLoop, calls=%fused_computation.2 | loop fusion | flops 262144 | bytes 524672 | tf_op jit(solution)/shard_map/convert_element_type | solution.py:52
  23.6 6.8 %collective-permute-done.7 = f32[3,8,1024]{2,1,0:T(8,128)} collective-permute-done((f32[3,8,1024]{2,1,0:T(8,128)}, f32[3,8,1024]{2,1,0:T(8,128)}, u32[]{:S(2)}, u32[]{:S(2)}) %collective-permute-start.7) | collective-permute-done | bytes 98336 | tf_op jit(solution)/shard_map/ppermute | solution.py:178
  30.5 0.8 multiply_add_fusion.5
  31.3 0.8 multiply_add_fusion.4
  32.1 2.4 %collective-permute-start.8 = (f32[3,8,1024]{2,1,0:T(8,128)S(1)}, f32[3,8,1024]{2,1,0:T(8,128)S(1)}, u32[]{:S(2)}, u32[]{:S(2)}) collective-permute-start(f32[3,8,1024]{2,1,0:T(8,128)S(1)} %pad_maximum_fusion.3), channel_id=1, source_target_pairs={{0,16},{4,20},{8,24},{12,28},{16,0},{20,4},{24,8},{28,12},{1,17},{... | collective-permute-start | bytes 294920 | tf_op jit(solution)/shard_map/ppermute | solution.py:178
  34.5 2.0 %collective-permute-done.8 = f32[3,8,1024]{2,1,0:T(8,128)S(1)} collective-permute-done((f32[3,8,1024]{2,1,0:T(8,128)S(1)}, f32[3,8,1024]{2,1,0:T(8,128)S(1)}, u32[]{:S(2)}, u32[]{:S(2)}) %collective-permute-start.8) | collective-permute-done | bytes 98336 | tf_op jit(solution)/shard_map/ppermute | solution.py:178
  36.6 2.1 %collective-permute-start.9 = (f32[3,8,1024]{2,1,0:T(8,128)S(1)}, f32[3,8,1024]{2,1,0:T(8,128)S(1)}, u32[]{:S(2)}, u32[]{:S(2)}) collective-permute-start(f32[3,8,1024]{2,1,0:T(8,128)S(1)} %pad_maximum_fusion.4), channel_id=1, source_target_pairs={{0,1},{1,0},{2,3},{3,2},{4,5},{5,4},{6,7},{7,6},{8,9},{9,8},{10,11... | collective-permute-start | bytes 294920 | tf_op jit(solution)/shard_map/ppermute | solution.py:178
  38.8 0.1 broadcast_or_fusion
  38.8 1.9 %collective-permute-done.9 = f32[3,8,1024]{2,1,0:T(8,128)S(1)} collective-permute-done((f32[3,8,1024]{2,1,0:T(8,128)S(1)}, f32[3,8,1024]{2,1,0:T(8,128)S(1)}, u32[]{:S(2)}, u32[]{:S(2)}) %collective-permute-start.9) | collective-permute-done | bytes 98336 | tf_op jit(solution)/shard_map/ppermute | solution.py:178
  40.8 1.7 %collective-permute-start.10 = (f32[3,8,1024]{2,1,0:T(8,128)S(1)}, f32[3,8,1024]{2,1,0:T(8,128)S(1)}, u32[]{:S(2)}, u32[]{:S(2)}) collective-permute-start(f32[3,8,1024]{2,1,0:T(8,128)S(1)} %pad_maximum_fusion.5), channel_id=1, source_target_pairs={{0,2},{1,3},{2,0},{3,1},{4,6},{5,7},{6,4},{7,5},{8,10},{9,11},{10,... | collective-permute-start | bytes 294920 | tf_op jit(solution)/shard_map/ppermute | solution.py:178
  42.5 0.8 copy-done.2
  43.3 5.7 %centre.4 = (bf16[2,128,256]{2,1,0:T(8,128)(2,1)S(1)}, f32[2,2,2,136,128]{4,3,2,1,0:T(8,128)S(1)}) custom-call(bf16[3,4,128,1024]{3,2,1,0:T(8,128)(2,1)S(1)} %bitcast.216, bf16[2,4,64,1024]{3,2,1,0:T(8,128)(2,1)} %bitcast.4.up_ref, bf16[2,4,64,1024]{3,2,1,0:T(8,128)(2,1)} %bitcast.5.down_ref, bf16[3,8,1024]{2,1,0:T(8,128)(2,1)S(1)} %copy-done.2, ...), custom_call_target="tpu_custom_call" | custom-call | flops 931135488 | bytes 4000000 | tf_op jit(solution)/shard_map/centre/pallas_call | solution.py:245
  49.1 1.3 %slice_bitcast_fusion = (bf16[1,2,64,1024]{3,2,1,0:T(8,128)(2,1)S(1)}, bf16[1,2,64,1024]{3,2,1,0:T(8,128)(2,1)S(1)}, bf16[1,2,64,1024]{3,2,1,0:T(8,128)(2,1)S(1)}, bf16[1,2,64,1024]{3,2,1,0:T(8,128)(2,1)S(1)}) fusion(bf16[2,128,1024]{2,1,0:T(8,128)(2,1)} %bitcast.3.r_ref, bf16[2,128,1024]{2,1,0:T(8,128)(2,1)} %bitcast.2.l_ref), kind=kLoop, calls=%fused_computation.4 | loop fusion | bytes 2097152 | tf_op jit(solution)/shard_map/stack | solution.py:410
  50.5 10.1 %collective-permute-start.4 = (bf16[2,2,64,1024]{3,2,1,0:T(8,128)(2,1)S(1)}, bf16[2,2,64,1024]{3,2,1,0:T(8,128)(2,1)S(1)}, u32[]{:S(2)}, u32[]{:S(2)}) collective-permute-start(bf16[2,2,64,1024]{3,2,1,0:T(8,128)(2,1)S(1)} %pad_maximum_fusion), channel_id=1, source_target_pairs={{0,4},{4,8},{8,12},{12,16},{16,20},{20,24},{24,28},{1,5},{5,9},{9,... | collective-permute-start | bytes 1572872 | tf_op jit(solution)/shard_map/ppermute | solution.py:34
  60.7 1.9 %collective-permute-start.5 = (bf16[2,2,64,1024]{3,2,1,0:T(8,128)(2,1)S(1)}, bf16[2,2,64,1024]{3,2,1,0:T(8,128)(2,1)S(1)}, u32[]{:S(2)}, u32[]{:S(2)}) collective-permute-start(bf16[2,2,64,1024]{3,2,1,0:T(8,128)(2,1)S(1)} %pad_maximum_fusion.1), channel_id=1, source_target_pairs={{4,0},{8,4},{12,8},{16,12},{20,16},{24,20},{28,24},{5,1},{9,5},{13... | collective-permute-start | bytes 1572872 | tf_op jit(solution)/shard_map/ppermute | solution.py:34
  62.7 0.1 select_convert_fusion.1.kf_ref
  62.8 1.5 %fusion.36 = bf16[8,1024]{1,0:T(8,128)(2,1)} fusion(f32[3,8,1024]{2,1,0:T(8,128)S(1)} %collective-permute-done.10, f32[3,8,1024]{2,1,0:T(8,128)S(1)} %collective-permute-done.9, f32[3,8,1024]{2,1,0:T(8,128)S(1)} %collective-permute-done.8, f32[3,8,1024]{2,1,0:T(8,128)} %collective-permute-done.7, f32[3,8,1024]{2,1,0:T(8,128)S(1)} %copy-done.7, ...), kind=kLoop, calls=%fused_computation.86 | loop fusion | flops 385024 | bytes 606208 | tf_op jit(solution)/shard_map/convert_element_type | solution.py:382
  64.3 5.8 %centre.7 = (bf16[2,128,256]{2,1,0:T(8,128)(2,1)S(1)}, f32[2,2,2,136,128]{4,3,2,1,0:T(8,128)S(1)}) custom-call(bf16[3,4,128,1024]{3,2,1,0:T(8,128)(2,1)S(1)} %bitcast.217, bf16[2,4,64,1024]{3,2,1,0:T(8,128)(2,1)} %bitcast.4.up_ref, bf16[2,4,64,1024]{3,2,1,0:T(8,128)(2,1)} %bitcast.5.down_ref, bf16[3,8,1024]{2,1,0:T(8,128)(2,1)S(1)} %copy-done.2, ...), custom_call_target="tpu_custom_call" | custom-call | flops 931135488 | bytes 4000000 | tf_op jit(solution)/shard_map/centre/pallas_call | solution.py:245
  70.1 5.8 %centre.6 = (bf16[2,128,256]{2,1,0:T(8,128)(2,1)S(1)}, f32[2,2,2,136,128]{4,3,2,1,0:T(8,128)S(1)}) custom-call(bf16[3,4,128,1024]{3,2,1,0:T(8,128)(2,1)S(1)} %bitcast.218, bf16[2,4,64,1024]{3,2,1,0:T(8,128)(2,1)} %bitcast.4.up_ref, bf16[2,4,64,1024]{3,2,1,0:T(8,128)(2,1)} %bitcast.5.down_ref, bf16[3,8,1024]{2,1,0:T(8,128)(2,1)S(1)} %copy-done.2, ...), custom_call_target="tpu_custom_call" | custom-call | flops 931135488 | bytes 4000000 | tf_op jit(solution)/shard_map/centre/pallas_call | solution.py:245
  76.0 5.8 %centre.5 = (bf16[2,128,256]{2,1,0:T(8,128)(2,1)S(1)}, f32[2,2,2,136,128]{4,3,2,1,0:T(8,128)S(1)}) custom-call(bf16[3,4,128,1024]{3,2,1,0:T(8,128)(2,1)S(1)} %bitcast.219, bf16[2,4,64,1024]{3,2,1,0:T(8,128)(2,1)} %bitcast.4.up_ref, bf16[2,4,64,1024]{3,2,1,0:T(8,128)(2,1)} %bitcast.5.down_ref, bf16[3,8,1024]{2,1,0:T(8,128)(2,1)S(1)} %copy-done.2, ...), custom_call_target="tpu_custom_call" | custom-call | flops 931135488 | bytes 4000000 | tf_op jit(solution)/shard_map/centre/pallas_call | solution.py:245
  81.8 10.3 %edges.1 = bf16[16,32,1024]{2,1,0:T(8,128)(2,1)} custom-call(bf16[3,4,128,1024]{3,2,1,0:T(8,128)(2,1)S(1)} %bitcast.220, bf16[2,128,1024]{2,1,0:T(8,128)(2,1)} %bitcast.2.l_ref, bf16[2,128,1024]{2,1,0:T(8,128)(2,1)} %bitcast.3.r_ref, bf16[2,2,64,1024]{3,2,1,0:T(8,128)(2,1)S(1)} %collective-permute-done.4.cu_ref, ...), custom_call_target="tpu_custom_call" | custom-call | flops 500000000 | bytes 3000000 | tf_op jit(solution)/shard_map/edges/pallas_call | solution.py:340
  (41 shorter events, 0.3 us)
Async XLA Ops:
  0.6 16.7 %copy-start.1 = (bf16[3,8,1024]{2,1,0:T(8,128)(2,1)S(1)}, bf16[3,8,1024]{2,1,0:T(8,128)(2,1)}, u32[]{:S(2)}) copy-start(bf16[3,8,1024]{2,1,0:T(8,128)(2,1)} %reg_ref.9) | copy-start | bytes 147460
  2.9 46.2 %collective-permute-start = (bf16[2,16,8,1024]{3,2,1,0:T(8,128)(2,1)}, bf16[2,16,8,1024]{3,2,1,0:T(8,128)(2,1)}, u32[]{:S(2)}, u32[]{:S(2)}) collective-permute-start(bf16[2,16,8,1024]{3,2,1,0:T(8,128)(2,1)} %get-tuple-element.20), channel_id=1, source_target_pairs={{0,1},{1,2},{2,3},{4,5},{5,6},{6,7},{8,9},{9,10},{10,11},{12,13},{... | collective-permute-start | bytes 1572872 | tf_op jit(solution)/shard_map/ppermute | solution.py:34
  6.8 42.3 %collective-permute-start.1 = (bf16[2,16,8,1024]{3,2,1,0:T(8,128)(2,1)}, bf16[2,16,8,1024]{3,2,1,0:T(8,128)(2,1)}, u32[]{:S(2)}, u32[]{:S(2)}) collective-permute-start(bf16[2,16,8,1024]{3,2,1,0:T(8,128)(2,1)} %get-tuple-element.21), channel_id=1, source_target_pairs={{1,0},{2,1},{3,2},{5,4},{6,5},{7,6},{9,8},{10,9},{11,10},{13,12},{... | collective-permute-start | bytes 1572872 | tf_op jit(solution)/shard_map/ppermute | solution.py:34
  11.2 31.3 %copy-start = (bf16[4,128,128]{2,1,0:T(8,128)(2,1)S(1)}, bf16[4,128,128]{2,1,0:T(8,128)(2,1)}, u32[]{:S(2)}) copy-start(bf16[4,128,128]{2,1,0:T(8,128)(2,1)} %constant.39.clone.qf_ref) | copy-start | bytes 393220
  11.2 31.3 %collective-permute-start.2 = (bf16[2,4,8,8,1024]{4,3,2,1,0:T(8,128)(2,1)}, bf16[2,4,8,8,1024]{4,3,2,1,0:T(8,128)(2,1)}, u32[]{:S(2)}, u32[]{:S(2)}) collective-permute-start(bf16[2,4,8,8,1024]{4,3,2,1,0:T(8,128)(2,1)} %get-tuple-element.22), channel_id=1, source_target_pairs={{0,4},{4,8},{8,12},{12,16},{16,20},{20,24},{24,28},{1,5},{5,9},{9,... | collective-permute-start | bytes 3145736 | tf_op jit(solution)/shard_map/ppermute | solution.py:34
  15.4 27.1 %collective-permute-start.3 = (bf16[2,4,8,8,1024]{4,3,2,1,0:T(8,128)(2,1)}, bf16[2,4,8,8,1024]{4,3,2,1,0:T(8,128)(2,1)}, u32[]{:S(2)}, u32[]{:S(2)}) collective-permute-start(bf16[2,4,8,8,1024]{4,3,2,1,0:T(8,128)(2,1)} %get-tuple-element.23), channel_id=1, source_target_pairs={{4,0},{8,4},{12,8},{16,12},{20,16},{24,20},{28,24},{5,1},{9,5},{13... | collective-permute-start | bytes 3145736 | tf_op jit(solution)/shard_map/ppermute | solution.py:34
  20.1 2.3 %copy-start.3 = (f32[3,8,1024]{2,1,0:T(8,128)}, f32[3,8,1024]{2,1,0:T(8,128)S(1)}, u32[]{:S(2)}) copy-start(f32[3,8,1024]{2,1,0:T(8,128)S(1)} %get-tuple-element.35) | copy-start | bytes 294916
  20.1 1.6 %collective-permute-start.6 = (f32[3,8,1024]{2,1,0:T(8,128)S(1)}, f32[3,8,1024]{2,1,0:T(8,128)S(1)}, u32[]{:S(2)}, u32[]{:S(2)}) collective-permute-start(f32[3,8,1024]{2,1,0:T(8,128)S(1)} %get-tuple-element.35), channel_id=1, source_target_pairs={{0,4},{4,0},{8,12},{12,8},{16,20},{20,16},{24,28},{28,24},{1,5},{5... | collective-permute-start | bytes 294920 | tf_op jit(solution)/shard_map/ppermute | solution.py:178
  21.7 0.8 copy-start.6
  21.7 0.7 copy-start.5
  21.7 0.7 copy-start.9
  21.7 0.7 copy-start.8
  22.4 8.0 %collective-permute-start.7 = (f32[3,8,1024]{2,1,0:T(8,128)}, f32[3,8,1024]{2,1,0:T(8,128)}, u32[]{:S(2)}, u32[]{:S(2)}) collective-permute-start(f32[3,8,1024]{2,1,0:T(8,128)} %pad_maximum_fusion.2), channel_id=1, source_target_pairs={{0,8},{4,12},{8,0},{12,4},{16,24},{20,28},{24,16},{28,20},{1,9},{5... | collective-permute-start | bytes 294920 | tf_op jit(solution)/shard_map/ppermute | solution.py:178
  32.1 4.4 %collective-permute-start.8 = (f32[3,8,1024]{2,1,0:T(8,128)S(1)}, f32[3,8,1024]{2,1,0:T(8,128)S(1)}, u32[]{:S(2)}, u32[]{:S(2)}) collective-permute-start(f32[3,8,1024]{2,1,0:T(8,128)S(1)} %pad_maximum_fusion.3), channel_id=1, source_target_pairs={{0,16},{4,20},{8,24},{12,28},{16,0},{20,4},{24,8},{28,12},{1,17},{... | collective-permute-start | bytes 294920 | tf_op jit(solution)/shard_map/ppermute | solution.py:178
  36.6 4.1 %collective-permute-start.9 = (f32[3,8,1024]{2,1,0:T(8,128)S(1)}, f32[3,8,1024]{2,1,0:T(8,128)S(1)}, u32[]{:S(2)}, u32[]{:S(2)}) collective-permute-start(f32[3,8,1024]{2,1,0:T(8,128)S(1)} %pad_maximum_fusion.4), channel_id=1, source_target_pairs={{0,1},{1,0},{2,3},{3,2},{4,5},{5,4},{6,7},{7,6},{8,9},{9,8},{10,11... | collective-permute-start | bytes 294920 | tf_op jit(solution)/shard_map/ppermute | solution.py:178
  40.8 22.0 %collective-permute-start.10 = (f32[3,8,1024]{2,1,0:T(8,128)S(1)}, f32[3,8,1024]{2,1,0:T(8,128)S(1)}, u32[]{:S(2)}, u32[]{:S(2)}) collective-permute-start(f32[3,8,1024]{2,1,0:T(8,128)S(1)} %pad_maximum_fusion.5), channel_id=1, source_target_pairs={{0,2},{1,3},{2,0},{3,1},{4,6},{5,7},{6,4},{7,5},{8,10},{9,11},{10,... | collective-permute-start | bytes 294920 | tf_op jit(solution)/shard_map/ppermute | solution.py:178
  42.5 0.8 copy-start.2
  49.0 13.6 %copy-start.10 = (bf16[2,256,128]{2,1,0:T(8,128)(2,1)S(1)}, bf16[2,256,128]{2,1,0:T(8,128)(2,1)}, u32[]{:S(2)}) copy-start(bf16[2,256,128]{2,1,0:T(8,128)(2,1)} %constant.137) | copy-start | bytes 393220
  49.1 13.8 %copy-start.4 = (f32[3,8,1024]{2,1,0:T(8,128)S(1)}, f32[3,8,1024]{2,1,0:T(8,128)}, u32[]{:S(2)}) copy-start(f32[3,8,1024]{2,1,0:T(8,128)} %copy-done.3) | copy-start | bytes 294916
  49.1 13.8 %copy-start.7 = (f32[3,8,1024]{2,1,0:T(8,128)S(1)}, f32[3,8,1024]{2,1,0:T(8,128)}, u32[]{:S(2)}) copy-start(f32[3,8,1024]{2,1,0:T(8,128)} %copy-done.6) | copy-start | bytes 294916
  50.5 31.3 %collective-permute-start.4 = (bf16[2,2,64,1024]{3,2,1,0:T(8,128)(2,1)S(1)}, bf16[2,2,64,1024]{3,2,1,0:T(8,128)(2,1)S(1)}, u32[]{:S(2)}, u32[]{:S(2)}) collective-permute-start(bf16[2,2,64,1024]{3,2,1,0:T(8,128)(2,1)S(1)} %pad_maximum_fusion), channel_id=1, source_target_pairs={{0,4},{4,8},{8,12},{12,16},{16,20},{20,24},{24,28},{1,5},{5,9},{9,... | collective-permute-start | bytes 1572872 | tf_op jit(solution)/shard_map/ppermute | solution.py:34
  60.7 21.1 %collective-permute-start.5 = (bf16[2,2,64,1024]{3,2,1,0:T(8,128)(2,1)S(1)}, bf16[2,2,64,1024]{3,2,1,0:T(8,128)(2,1)S(1)}, u32[]{:S(2)}, u32[]{:S(2)}) collective-permute-start(bf16[2,2,64,1024]{3,2,1,0:T(8,128)(2,1)S(1)} %pad_maximum_fusion.1), channel_id=1, source_target_pairs={{4,0},{8,4},{12,8},{16,12},{20,16},{24,20},{28,24},{5,1},{9,5},{13... | collective-permute-start | bytes 1572872 | tf_op jit(solution)/shard_map/ppermute | solution.py:34

commit v4 on v3

--- a/solution.py
+++ b/solution.py
@@ -13,6 +13,7 @@
 PARTS = 4
 RADIUS = 8
 FAR = -30000.0
+LEAST, MOST = 1e-20, 1e30
 LANES = 128
 F32 = jnp.float32
 BF16 = jnp.bfloat16
@@ -61,38 +62,32 @@
     return started
 
 
-def pack_sides_kernel(p_ref, right_ref, left_ref, sems):
-    tc = p_ref.shape[2]
-    copies = []
-    for j in range(2):
-        copies.append((p_ref.at[1 + j, :, pl.ds(tc - RADIUS, RADIUS)], right_ref.at[j]))
-        copies.append((p_ref.at[1 + j, :, pl.ds(0, RADIUS)], left_ref.at[j]))
+def stage_kernel(copies_of, a_ref, b_ref, a_out, b_out, sems):
+    copies = copies_of(a_ref, a_out) + copies_of(b_ref, b_out)
     for c in copy_all(copies, sems):
         c.wait()
 
 
-def pack_rows_kernel(p_ref, down_ref, up_ref, sems):
-    _, tr, tc, _ = p_ref.shape
-    copies = []
-    for j in range(2):
-        for g in range(tc // RADIUS):
-            cols = pl.ds(g * RADIUS, RADIUS)
-            copies.append((p_ref.at[1 + j, pl.ds(tr - RADIUS, RADIUS), cols], down_ref.at[j, g]))
-            copies.append((p_ref.at[1 + j, pl.ds(0, RADIUS), cols], up_ref.at[j, g]))
-    for c in copy_all(copies, sems):
-        c.wait()
-
-
-def pack(kernel, patches, shape, copies):
-    payload = pltpu.VMEM(shape, BF16)
+def whole(src, dst):
+    return [(src.at[j], dst.at[j]) for j in range(2)]
+
+
+def grouped(src, dst):
+    cut = lambda g: pl.ds(g * RADIUS, RADIUS)
+    return [(src.at[j, :, cut(g)], dst.at[j, g]) for j in range(2) for g in range(dst.shape[1])]
+
+
+def stage(copies_of, count, a, b, shape):
+    a, b = (pltpu.with_memory_space_constraint(x, pltpu.HBM) for x in (a, b))
     return pl.pallas_call(
-        kernel,
-        in_specs=[HBM],
-        out_specs=[VMEM] * 2,
-        out_shape=[payload] * 2,
-        scratch_shapes=[pltpu.SemaphoreType.DMA((copies,))],
+        functools.partial(stage_kernel, copies_of),
+        in_specs=[HBM, HBM],
+        out_specs=[VMEM, VMEM],
+        out_shape=[pltpu.VMEM(shape, BF16)] * 2,
+        scratch_shapes=[pltpu.SemaphoreType.DMA((2 * count,))],
+        cost_estimate=pl.CostEstimate(flops=1_000_000, bytes_accessed=4_000_000, transcendentals=0),
         compiler_params=PARAMS,
-    )(patches)
+    )(a, b)
 
 
 def prep_kernel(scale, flag_ref, reg_ref, p_ref, out_ref, part_ref, sems):
@@ -182,7 +177,7 @@
 
 
 def centre_kernel(scale, first, p_ref, up_ref, down_ref, reg_ref, qf_ref, kf_ref, in_ref, st_ref):
-    _, _, cells, width = p_ref.shape
+    _, groups, cells, width = p_ref.shape
     d = LANES
     head = width // HEADS
     edge = RADIUS * RADIUS
@@ -192,48 +187,75 @@
     reg_f = jnp.where(pad & off, FAR, 0.0).astype(BF16)
     zero = jnp.zeros((RADIUS, d), BF16)
 
-    @pl.loop(0, st_ref.shape[0])
-    def _(i):
+    def unit(i, half, part, exact):
         lanes = pl.ds(pl.multiple_of((i + first) * d, d), d)
         lanes_out = pl.ds(pl.multiple_of(i * d, d), d)
-        reg_k = jnp.concatenate([reg_ref[1, :, lanes], zero], axis=0)
-        reg_v = jnp.concatenate([reg_ref[2, :, lanes], zero], axis=0)
-        for half in range(2):
-            for part in range(2):
-                near = range(part, part + 3)
-
-                def piece(j, g):
-                    own = p_ref[1 + j, g, :, lanes]
-                    if half == 0:
-                        return [up_ref[j, g, :, lanes], own]
-                    return [own, down_ref[j, g, :, lanes]]
-
-                span = cells + edge
-                k = jnp.concatenate(sum([piece(0, g) for g in near], []) + [reg_k], axis=0)
-                v = jnp.concatenate(sum([piece(1, g) for g in near], []) + [reg_v], axis=0)
-                f = jnp.concatenate(
-                    [kf_ref[g, half * edge : half * edge + span] for g in near] + [reg_f], axis=0
-                )
-                kc = jnp.concatenate([k, f], axis=1)
-                qs = []
-                for g in (0, 1) if part == 0 else (3, 2):
-                    rows = slice(half * edge, (half + 1) * edge)
-                    q = p_ref[0, g, rows, lanes].astype(F32) * scale
-                    qf = qf_ref[g, rows]
-                    for x in (jnp.where(low, q, 0.0), jnp.where(low, 0.0, q)):
-                        qs.append(jnp.concatenate([x.astype(BF16), qf], axis=1))
-                s = dot(kc, jnp.concatenate(qs, axis=0), NT)
-                high = jnp.max(s, axis=0, keepdims=True)
-                w = jnp.exp(s - high)
-                total = jnp.sum(w, axis=0, keepdims=True)
-                o = dot(v, w.astype(BF16), TN)
-                st_ref[i, half, part, :d] = o[:, :d]
-                st_ref[i, half, part, d : d + 8] = jnp.concatenate(
-                    [high[:, :d], total[:, :d], jnp.zeros((6, d), F32)], axis=0
-                )
-                t = jnp.transpose(o[:, d:] / total[:, d:])
-                t = jnp.where(low, t[:edge], t[edge:])
-                in_ref[part, half * edge : (half + 1) * edge, lanes_out] = t.astype(BF16)
+        rows = slice(half * edge, (half + 1) * edge)
+        near = range(part, part + 3)
+        span = cells + edge
+
+        def stacked(j):
+            pieces = []
+            for g in near:
+                own = p_ref[j, g, :, lanes]
+                if half == 0:
+                    pieces += [up_ref[j - 1, g, :, lanes], own]
+                else:
+                    pieces += [own, down_ref[j - 1, g, :, lanes]]
+            return jnp.concatenate(pieces + [reg_ref[j, :, lanes], zero], axis=0)
+
+        f = jnp.concatenate(
+            [kf_ref[g, half * edge : half * edge + span] for g in near] + [reg_f], axis=0
+        )
+        kc = jnp.concatenate([stacked(1), f], axis=1)
+        qs = []
+        for g in (0, 1) if part == 0 else (groups - 1, groups - 2):
+            q = p_ref[0, g, rows, lanes].astype(F32) * scale
+            qf = qf_ref[g, rows]
+            for x in (jnp.where(low, q, 0.0), jnp.where(low, 0.0, q)):
+                qs.append(jnp.concatenate([x.astype(BF16), qf], axis=1))
+        s = dot(kc, jnp.concatenate(qs, axis=0), NT)
+        if exact:
+            high = jnp.max(s, axis=0, keepdims=True)
+            s = s - high
+        else:
+            high = jnp.zeros((1, s.shape[1]), F32)
+        w = jnp.exp(s)
+        total = jnp.sum(w, axis=0, keepdims=True)
+        o = dot(stacked(2), w.astype(BF16), TN)
+        st_ref[i, half, part, :d] = o[:, :d]
+        st_ref[i, half, part, d : d + 8] = jnp.concatenate(
+            [high[:, :d], total[:, :d], jnp.zeros((6, d), F32)], axis=0
+        )
+        t = jnp.transpose(o[:, d:] / total[:, d:])
+        t = jnp.where(low, t[:edge], t[edge:])
+        in_ref[part, rows, lanes_out] = t.astype(BF16)
+        return total
+
+    run_guarded(unit, st_ref.shape[0], 4 * edge)
+
+
+def run_guarded(unit, count, lanes):
+    units = [(half, part) for half in range(2) for part in range(2)]
+
+    def fast(i, seen):
+        least, most = seen
+        for half, part in units:
+            total = unit(i, half, part, False)
+            least = jnp.where(total >= least, least, total)
+            most = jnp.where(total <= most, most, total)
+        return least, most
+
+    one = jnp.ones((1, lanes), F32)
+    least, most = lax.fori_loop(0, count, fast, (one, one))
+    fine = jnp.where((least > LEAST) & (most < MOST), 1.0, 0.0)
+
+    @pl.when(jnp.min(fine) < 0.5)
+    def _():
+        @pl.loop(0, count)
+        def _(i):
+            for half, part in units:
+                unit(i, half, part, True)
 
 
 def centre(pg, up, down, registers, qf, kf, scale, first, pairs):
@@ -281,47 +303,50 @@
                 )
             )
     started = copy_all(copies, sems)
+
+    def unit_of(n, i, half, side, exact):
+        st = states[n]
+        lanes = pl.ds(pl.multiple_of((i + n * per) * d, d), d)
+        cells_of = slice(half * edge, (half + 1) * edge)
+        halo = l_ref if side == 0 else r_ref
+        corner = cu_ref if half == 0 else cd_ref
+
+        def keys(j):
+            own = halo[j, :, lanes]
+            far = corner[side, j, :, lanes]
+            return jnp.concatenate([far, own] if half == 0 else [own, far], axis=0)
+
+        f = kf_ref[side, half * edge : half * edge + span]
+        kc = jnp.concatenate([keys(0), f], axis=1)
+        g = 0 if side == 0 else groups - 1
+        q = p_ref[0, g, cells_of, lanes].astype(F32) * scale
+        qf = qf_ref[g, cells_of]
+        qc = jnp.concatenate(
+            [
+                jnp.concatenate([x.astype(BF16), qf], axis=1)
+                for x in (jnp.where(low, q, 0.0), jnp.where(low, 0.0, q))
+            ],
+            axis=0,
+        )
+        s = dot(kc, qc, NT)
+        acc = st[i, half, side, :d]
+        high = st[i, half, side, d : d + 1]
+        total = st[i, half, side, d + 1 : d + 2]
+        if exact:
+            new = jnp.maximum(high, jnp.max(s, axis=0, keepdims=True))
+            fade = jnp.exp(high - new)
+            acc, total, high = acc * fade, total * fade, new
+        w = jnp.exp(s - high)
+        total = total + jnp.sum(w, axis=0, keepdims=True)
+        acc = acc + dot(keys(1), w.astype(BF16), TN)
+        t = jnp.transpose(acc / total)
+        t = jnp.where(low, t[:edge], t[edge:])
+        rows_of = slice(half * RADIUS, (half + 1) * RADIUS)
+        edge_ref[side, rows_of, :, lanes] = t.reshape(RADIUS, RADIUS, d).astype(BF16)
+        return total
+
     for n in range(parts):
-
-        @pl.loop(0, per)
-        def _(i):
-            lanes = pl.ds(pl.multiple_of((i + n * per) * d, d), d)
-            for half in range(2):
-                cells_of = slice(half * edge, (half + 1) * edge)
-                for side in range(2):
-                    halo = l_ref if side == 0 else r_ref
-                    corner = cu_ref if half == 0 else cd_ref
-
-                    def keys(j):
-                        own = halo[j, :, lanes]
-                        far = corner[side, j, :, lanes]
-                        return jnp.concatenate([far, own] if half == 0 else [own, far], axis=0)
-
-                    f = kf_ref[side, half * edge : half * edge + span]
-                    kc = jnp.concatenate([keys(0), f], axis=1)
-                    g = 0 if side == 0 else groups - 1
-                    q = p_ref[0, g, cells_of, lanes].astype(F32) * scale
-                    qf = qf_ref[g, cells_of]
-                    qc = jnp.concatenate(
-                        [
-                            jnp.concatenate([x.astype(BF16), qf], axis=1)
-                            for x in (jnp.where(low, q, 0.0), jnp.where(low, 0.0, q))
-                        ],
-                        axis=0,
-                    )
-                    s = dot(kc, qc, NT)
-                    st = states[n]
-                    high1 = st[i, half, side, d : d + 1]
-                    total1 = st[i, half, side, d + 1 : d + 2]
-                    high = jnp.maximum(high1, jnp.max(s, axis=0, keepdims=True))
-                    fade = jnp.exp(high1 - high)
-                    w = jnp.exp(s - high)
-                    total = total1 * fade + jnp.sum(w, axis=0, keepdims=True)
-                    acc = st[i, half, side, :d] * fade + dot(keys(1), w.astype(BF16), TN)
-                    t = jnp.transpose(acc / total)
-                    t = jnp.where(low, t[:edge], t[edge:])
-                    rows_of = slice(half * RADIUS, (half + 1) * RADIUS)
-                    edge_ref[side, rows_of, :, lanes] = t.reshape(RADIUS, RADIUS, d).astype(BF16)
+        run_guarded(functools.partial(unit_of, n), per, 2 * edge)
 
     copies = []
     for side in range(2):
@@ -364,15 +389,15 @@
     row_at, row_n = lax.axis_index("row"), lax.axis_size("row")
     col_at, col_n = lax.axis_index("col"), lax.axis_size("col")
 
+    in_vmem = lambda x: pltpu.with_memory_space_constraint(x, pltpu.VMEM)
     source = pltpu.with_memory_space_constraint(patches, pltpu.HBM)
-    to_right, to_left = pack(pack_sides_kernel, source, (2, tr, RADIUS, width), 4)
-    left = shift(to_right, "col", 1)
-    right = shift(to_left, "col", -1)
-    shape = (2, groups, RADIUS, RADIUS, width)
-    to_down, to_up = pack(pack_rows_kernel, source, shape, 4 * groups)
-    up = shift(to_down, "row", 1)
-    down = shift(to_up, "row", -1)
+    left = shift(patches[1:3, :, tc - RADIUS :], "col", 1)
+    right = shift(patches[1:3, :, :RADIUS], "col", -1)
+    up = shift(patches[1:3, tr - RADIUS :], "row", 1)
+    down = shift(patches[1:3, :RADIUS], "row", -1)
     left, right = (x.reshape(2, cells, width) for x in (left, right))
+    rows_shape = (2, groups, RADIUS, RADIUS, width)
+    up, down = stage(grouped, 2 * groups, up, down, rows_shape)
     up, down = (x.reshape(2, groups, edge, width) for x in (up, down))
 
     flag = jnp.where((row_at == 0) & (col_at == 0), 0.0, -1e30).astype(F32).reshape(1)
@@ -406,9 +431,10 @@
     near_l, near_r, first_state = lax.optimization_barrier((left, right, done[0][1]))
     done[0] = (done[0][0], first_state)
     bottom = jnp.stack([near_l[:, -edge:], near_r[:, -edge:]])
-    corner_up = shift(bottom, "row", 1)
+    corner_up = in_vmem(shift(bottom, "row", 1))
     top = jnp.stack([near_l[:, :edge], near_r[:, :edge]])
-    corner_down = shift(top, "row", -1)
+    corner_down = in_vmem(shift(top, "row", -1))
+    left, right = stage(whole, 2, near_l, near_r, left.shape)
     inner = [x[0].reshape(2, tr, RADIUS, per * LANES) for x in done]
     out = edges(
         pg, left, right, corner_up, corner_down, qf, kf_side, inner, [x[1] for x in done], scale, tr, tc

time: 92.9 us -> 97.1 us (1.045)
  the two profiles are of different devices: /device:TPU:9 before, /device:TPU:16 now
where the time goes in v4:
time: 97.1 us; the launch traced here: 96.5 us
  Pallas kernels  43.9 us (45%)
  starting transfers between devices  23.2 us (24%)
  waiting for transfers between devices  16 us (16%)
  local copies, waits for them, and re-layouts  6.89 us (7%)
  other arithmetic  5.33 us (5%)
  between operations  1.18 us (1%)
    pallas_call x4, Pallas kernels, centre(): pl.pallas_call(functools.partial(centre_kernel, scale, first), in_specs=[...  29.6 us
    ppermute x6, starting transfers between devices, shift(): lax.ppermute(x, axis, [(i, i + step) for i in range(n) if 0 <= i + step <...  16.5 us
    ppermute x5, waiting for transfers between devices, merge_over(): other = lax.ppermute(part, axis, [(i, i ^ step) for i in range(n)])  16 us
    pallas_call x1, Pallas kernels, edges(): pl.pallas_call(functools.partial(edge_kernel, scale, parts), in_specs=[VM...  8.62 us
    ppermute x5, starting transfers between devices, merge_over(): other = lax.ppermute(part, axis, [(i, i ^ step) for i in range(n)])  6.72 us
    slice x1, local copies, waits for them, and re-layouts, local(): down = shift(patches[1:3, :RADIUS], 'row', -1)  3.14 us
    pallas_call x2, Pallas kernels, stage(): pl.pallas_call(functools.partial(stage_kernel, copies_of), in_specs=[HBM,...  2.96 us
    pallas_call x1, Pallas kernels, prep(): pl.pallas_call(functools.partial(prep_kernel, scale), in_specs=[SMEM, VME...  2.72 us
  transfers between devices with their start and end apart: 11, of which 4 were waited for; matrix products, arithmetic and copies ran while one was open for 10% of the time, Pallas kernels for 37%

profile of v4, /device:TPU:16, one launch (start us, length us, event | category | flops | bytes accessed | tf_op | source)
XLA Modules:
  0.0 96.5 jit_solution(6448752409579646238)
XLA Ops:
  0.6 2.3 %fusion.38 = (bf16[2,16,8,1024]{3,2,1,0:T(8,128)(2,1)}, bf16[2,16,8,1024]{3,2,1,0:T(8,128)(2,1)}) fusion(bf16[3,16,32,1024]{3,2,1,0:T(8,128)(2,1)} %p_ref.1), kind=kLoop, calls=%fused_computation.96 | loop fusion | bytes 2097152 | tf_op jit(solution)/shard_map/slice | solution.py:395
  3.0 1.3 %collective-permute-start.1 = (bf16[2,16,8,1024]{3,2,1,0:T(8,128)(2,1)}, bf16[2,16,8,1024]{3,2,1,0:T(8,128)(2,1)}, u32[]{:S(2)}, u32[]{:S(2)}) collective-permute-start(bf16[2,16,8,1024]{3,2,1,0:T(8,128)(2,1)} %get-tuple-element.44), channel_id=1, source_target_pairs={{1,0},{2,1},{3,2},{5,4},{6,5},{7,6},{9,8},{10,9},{11,10},{13,12},{... | collective-permute-start | bytes 1572872 | tf_op jit(solution)/shard_map/ppermute | solution.py:35
  4.2 5.3 %collective-permute-start = (bf16[2,16,8,1024]{3,2,1,0:T(8,128)(2,1)}, bf16[2,16,8,1024]{3,2,1,0:T(8,128)(2,1)}, u32[]{:S(2)}, u32[]{:S(2)}) collective-permute-start(bf16[2,16,8,1024]{3,2,1,0:T(8,128)(2,1)} %get-tuple-element.45), channel_id=1, source_target_pairs={{0,1},{1,2},{2,3},{4,5},{5,6},{6,7},{8,9},{9,10},{10,11},{12,13},{... | collective-permute-start | bytes 1572872 | tf_op jit(solution)/shard_map/ppermute | solution.py:35
  9.6 3.1 %fusion.37 = (bf16[2,8,32,1024]{3,2,1,0:T(8,128)(2,1)}, bf16[2,8,32,1024]{3,2,1,0:T(8,128)(2,1)}) fusion(bf16[3,16,32,1024]{3,2,1,0:T(8,128)(2,1)} %p_ref.1), kind=kLoop, calls=%fused_computation.95 | loop fusion | bytes 4194304 | tf_op jit(solution)/shard_map/slice | solution.py:397
  12.7 1.9 %collective-permute-start.3 = (bf16[2,8,32,1024]{3,2,1,0:T(8,128)(2,1)}, bf16[2,8,32,1024]{3,2,1,0:T(8,128)(2,1)}, u32[]{:S(2)}, u32[]{:S(2)}) collective-permute-start(bf16[2,8,32,1024]{3,2,1,0:T(8,128)(2,1)} %get-tuple-element.42), channel_id=1, source_target_pairs={{4,0},{8,4},{12,8},{16,12},{20,16},{24,20},{28,24},{5,1},{9,5},{13... | collective-permute-start | bytes 3145736 | tf_op jit(solution)/shard_map/ppermute | solution.py:35
  14.7 2.4 %collective-permute-start.2 = (bf16[2,8,32,1024]{3,2,1,0:T(8,128)(2,1)}, bf16[2,8,32,1024]{3,2,1,0:T(8,128)(2,1)}, u32[]{:S(2)}, u32[]{:S(2)}) collective-permute-start(bf16[2,8,32,1024]{3,2,1,0:T(8,128)(2,1)} %get-tuple-element.43), channel_id=1, source_target_pairs={{0,4},{4,8},{8,12},{12,16},{16,20},{20,24},{24,28},{1,5},{5,9},{9,... | collective-permute-start | bytes 3145736 | tf_op jit(solution)/shard_map/ppermute | solution.py:35
  17.1 2.7 %prep.1 = (bf16[3,4,16,8,1024]{4,3,2,1,0:T(8,128)(2,1)S(1)}, f32[3,8,1024]{2,1,0:T(8,128)S(1)}) custom-call(f32[1]{0:T(128)} %bitcast.flag_ref, bf16[3,8,1024]{2,1,0:T(8,128)(2,1)S(1)} %copy-done.1, bf16[3,16,32,1024]{3,2,1,0:T(8,128)(2,1)} %p_ref.1), custom_call_target="tpu_custom_call" | custom-call | flops 300000000 | bytes 4000000 | tf_op jit(solution)/shard_map/prep/pallas_call | solution.py:142
  19.8 1.3 %collective-permute-start.6 = (f32[3,8,1024]{2,1,0:T(8,128)S(1)}, f32[3,8,1024]{2,1,0:T(8,128)S(1)}, u32[]{:S(2)}, u32[]{:S(2)}) collective-permute-start(f32[3,8,1024]{2,1,0:T(8,128)S(1)} %get-tuple-element.35), channel_id=1, source_target_pairs={{0,4},{4,0},{8,12},{12,8},{16,20},{20,16},{24,28},{28,24},{1,5},{5... | collective-permute-start | bytes 294920 | tf_op jit(solution)/shard_map/ppermute | solution.py:173
  21.1 0.9 collective-permute-done.6
  22.1 0.6 pad_maximum_fusion.2
  22.8 1.8 %collective-permute-start.7 = (f32[3,8,1024]{2,1,0:T(8,128)}, f32[3,8,1024]{2,1,0:T(8,128)}, u32[]{:S(2)}, u32[]{:S(2)}) collective-permute-start(f32[3,8,1024]{2,1,0:T(8,128)} %pad_maximum_fusion.2), channel_id=1, source_target_pairs={{0,8},{4,12},{8,0},{12,4},{16,24},{20,28},{24,16},{28,20},{1,9},{5... | collective-permute-start | bytes 294920 | tf_op jit(solution)/shard_map/ppermute | solution.py:173
  24.6 1.1 %select_convert_fusion.kf_ref = bf16[4,256,128]{2,1,0:T(8,128)(2,1)S(1)} fusion(bf16[4,256,128]{2,1,0:T(8,128)(2,1)} %constant.136, pred[128]{0:T(512)(128)(4,1)S(1)} %iota_compare_fusion, pred[256]{0:T(512)(128)(4,1)S(1)} %and_or_fusion.1), kind=kLoop, calls=%fused_computation.2 | loop fusion | flops 262144 | bytes 524672 | tf_op jit(solution)/shard_map/convert_element_type | solution.py:53
  25.7 5.7 %collective-permute-done.7 = f32[3,8,1024]{2,1,0:T(8,128)} collective-permute-done((f32[3,8,1024]{2,1,0:T(8,128)}, f32[3,8,1024]{2,1,0:T(8,128)}, u32[]{:S(2)}, u32[]{:S(2)}) %collective-permute-start.7) | collective-permute-done | bytes 98336 | tf_op jit(solution)/shard_map/ppermute | solution.py:173
  31.4 0.8 multiply_add_fusion.5
  32.2 0.8 multiply_add_fusion.4
  33.1 0.4 collective-permute-start.8
  33.5 6.3 %collective-permute-done.8 = f32[3,8,1024]{2,1,0:T(8,128)S(1)} collective-permute-done((f32[3,8,1024]{2,1,0:T(8,128)S(1)}, f32[3,8,1024]{2,1,0:T(8,128)S(1)}, u32[]{:S(2)}, u32[]{:S(2)}) %collective-permute-start.8) | collective-permute-done | bytes 98336 | tf_op jit(solution)/shard_map/ppermute | solution.py:173
  39.8 1.7 %collective-permute-start.9 = (f32[3,8,1024]{2,1,0:T(8,128)S(1)}, f32[3,8,1024]{2,1,0:T(8,128)S(1)}, u32[]{:S(2)}, u32[]{:S(2)}) collective-permute-start(f32[3,8,1024]{2,1,0:T(8,128)S(1)} %pad_maximum_fusion.4), channel_id=1, source_target_pairs={{0,1},{1,0},{2,3},{3,2},{4,5},{5,4},{6,7},{7,6},{8,9},{9,8},{10,11... | collective-permute-start | bytes 294920 | tf_op jit(solution)/shard_map/ppermute | solution.py:173
  41.6 3.0 %collective-permute-done.9 = f32[3,8,1024]{2,1,0:T(8,128)S(1)} collective-permute-done((f32[3,8,1024]{2,1,0:T(8,128)S(1)}, f32[3,8,1024]{2,1,0:T(8,128)S(1)}, u32[]{:S(2)}, u32[]{:S(2)}) %collective-permute-start.9) | collective-permute-done | bytes 98336 | tf_op jit(solution)/shard_map/ppermute | solution.py:173
  44.7 1.6 %collective-permute-start.10 = (f32[3,8,1024]{2,1,0:T(8,128)S(1)}, f32[3,8,1024]{2,1,0:T(8,128)S(1)}, u32[]{:S(2)}, u32[]{:S(2)}) collective-permute-start(f32[3,8,1024]{2,1,0:T(8,128)S(1)} %pad_maximum_fusion.5), channel_id=1, source_target_pairs={{0,2},{1,3},{2,0},{3,1},{4,6},{5,7},{6,4},{7,5},{8,10},{9,11},{10,... | collective-permute-start | bytes 294920 | tf_op jit(solution)/shard_map/ppermute | solution.py:173
  46.3 1.7 %shard_map.68 = (bf16[2,4,8,8,1024]{4,3,2,1,0:T(8,128)(2,1)S(1)}, bf16[2,4,8,8,1024]{4,3,2,1,0:T(8,128)(2,1)S(1)}) custom-call(bf16[2,8,32,1024]{3,2,1,0:T(8,128)(2,1)} %collective-permute-done.2.a_ref, bf16[2,8,32,1024]{3,2,1,0:T(8,128)(2,1)} %collective-permute-done.3.b_ref), custom_call_target="tpu_custom_call" | custom-call | flops 1000000 | bytes 4000000 | tf_op jit(solution)/shard_map/pallas_call | solution.py:82
  48.0 7.3 %centre.4 = (bf16[2,128,256]{2,1,0:T(8,128)(2,1)S(1)}, f32[2,2,2,136,128]{4,3,2,1,0:T(8,128)S(1)}) custom-call(bf16[3,4,128,1024]{3,2,1,0:T(8,128)(2,1)S(1)} %bitcast.216, bf16[2,4,64,1024]{3,2,1,0:T(8,128)(2,1)S(1)} %bitcast.221, bf16[2,4,64,1024]{3,2,1,0:T(8,128)(2,1)S(1)} %bitcast.225, bf16[3,8,1024]{2,1,0:T(8,128)(2,1)S(1)} %copy-done.2, ...), custom_call_target="tpu_custom_call" | custom-call | flops 931135488 | bytes 4000000 | tf_op jit(solution)/shard_map/centre/pallas_call | solution.py:267
  55.4 1.4 %slice_bitcast_fusion = (bf16[1,2,64,1024]{3,2,1,0:T(8,128)(2,1)S(1)}, bf16[1,2,64,1024]{3,2,1,0:T(8,128)(2,1)S(1)}, bf16[1,2,64,1024]{3,2,1,0:T(8,128)(2,1)S(1)}, bf16[1,2,64,1024]{3,2,1,0:T(8,128)(2,1)S(1)}) fusion(bf16[2,128,1024]{2,1,0:T(8,128)(2,1)} %bitcast.3.b_ref, bf16[2,128,1024]{2,1,0:T(8,128)(2,1)} %bitcast.2.a_ref), kind=kLoop, calls=%fused_computation.4 | loop fusion | bytes 2097152 | tf_op jit(solution)/shard_map/stack | solution.py:435
  56.8 1.9 %collective-permute-start.4 = (bf16[2,2,64,1024]{3,2,1,0:T(8,128)(2,1)S(1)}, bf16[2,2,64,1024]{3,2,1,0:T(8,128)(2,1)S(1)}, u32[]{:S(2)}, u32[]{:S(2)}) collective-permute-start(bf16[2,2,64,1024]{3,2,1,0:T(8,128)(2,1)S(1)} %pad_maximum_fusion), channel_id=1, source_target_pairs={{0,4},{4,8},{8,12},{12,16},{16,20},{20,24},{24,28},{1,5},{5,9},{9,... | collective-permute-start | bytes 1572872 | tf_op jit(solution)/shard_map/ppermute | solution.py:35
  58.8 3.6 %collective-permute-start.5 = (bf16[2,2,64,1024]{3,2,1,0:T(8,128)(2,1)S(1)}, bf16[2,2,64,1024]{3,2,1,0:T(8,128)(2,1)S(1)}, u32[]{:S(2)}, u32[]{:S(2)}) collective-permute-start(bf16[2,2,64,1024]{3,2,1,0:T(8,128)(2,1)S(1)} %pad_maximum_fusion.1), channel_id=1, source_target_pairs={{4,0},{8,4},{12,8},{16,12},{20,16},{24,20},{28,24},{5,1},{9,5},{13... | collective-permute-start | bytes 1572872 | tf_op jit(solution)/shard_map/ppermute | solution.py:35
  62.5 0.1 select_convert_fusion.1.kf_ref
  62.6 1.5 %fusion.36 = bf16[8,1024]{1,0:T(8,128)(2,1)} fusion(f32[3,8,1024]{2,1,0:T(8,128)S(1)} %collective-permute-done.10, f32[3,8,1024]{2,1,0:T(8,128)S(1)} %collective-permute-done.9, f32[3,8,1024]{2,1,0:T(8,128)S(1)} %collective-permute-done.8, f32[3,8,1024]{2,1,0:T(8,128)} %collective-permute-done.7, f32[3,8,1024]{2,1,0:T(8,128)S(1)} %copy-done.7, ...), kind=kLoop, calls=%fused_computation.86 | loop fusion | flops 385024 | bytes 606208 | tf_op jit(solution)/shard_map/convert_element_type | solution.py:407
  64.1 1.2 %shard_map.69 = (bf16[2,128,1024]{2,1,0:T(8,128)(2,1)S(1)}, bf16[2,128,1024]{2,1,0:T(8,128)(2,1)S(1)}) custom-call(bf16[2,128,1024]{2,1,0:T(8,128)(2,1)} %bitcast.2.a_ref, bf16[2,128,1024]{2,1,0:T(8,128)(2,1)} %bitcast.3.b_ref), custom_call_target="tpu_custom_call" | custom-call | flops 1000000 | bytes 4000000 | tf_op jit(solution)/shard_map/pallas_call | solution.py:82
  65.4 7.4 %centre.7 = (bf16[2,128,256]{2,1,0:T(8,128)(2,1)S(1)}, f32[2,2,2,136,128]{4,3,2,1,0:T(8,128)S(1)}) custom-call(bf16[3,4,128,1024]{3,2,1,0:T(8,128)(2,1)S(1)} %bitcast.217, bf16[2,4,64,1024]{3,2,1,0:T(8,128)(2,1)S(1)} %bitcast.222, bf16[2,4,64,1024]{3,2,1,0:T(8,128)(2,1)S(1)} %bitcast.226, bf16[3,8,1024]{2,1,0:T(8,128)(2,1)S(1)} %copy-done.2, ...), custom_call_target="tpu_custom_call" | custom-call | flops 931135488 | bytes 4000000 | tf_op jit(solution)/shard_map/centre/pallas_call | solution.py:267
  72.7 7.5 %centre.6 = (bf16[2,128,256]{2,1,0:T(8,128)(2,1)S(1)}, f32[2,2,2,136,128]{4,3,2,1,0:T(8,128)S(1)}) custom-call(bf16[3,4,128,1024]{3,2,1,0:T(8,128)(2,1)S(1)} %bitcast.218, bf16[2,4,64,1024]{3,2,1,0:T(8,128)(2,1)S(1)} %bitcast.223, bf16[2,4,64,1024]{3,2,1,0:T(8,128)(2,1)S(1)} %bitcast.227, bf16[3,8,1024]{2,1,0:T(8,128)(2,1)S(1)} %copy-done.2, ...), custom_call_target="tpu_custom_call" | custom-call | flops 931135488 | bytes 4000000 | tf_op jit(solution)/shard_map/centre/pallas_call | solution.py:267
  80.3 7.4 %centre.5 = (bf16[2,128,256]{2,1,0:T(8,128)(2,1)S(1)}, f32[2,2,2,136,128]{4,3,2,1,0:T(8,128)S(1)}) custom-call(bf16[3,4,128,1024]{3,2,1,0:T(8,128)(2,1)S(1)} %bitcast.219, bf16[2,4,64,1024]{3,2,1,0:T(8,128)(2,1)S(1)} %bitcast.224, bf16[2,4,64,1024]{3,2,1,0:T(8,128)(2,1)S(1)} %bitcast.228, bf16[3,8,1024]{2,1,0:T(8,128)(2,1)S(1)} %copy-done.2, ...), custom_call_target="tpu_custom_call" | custom-call | flops 931135488 | bytes 4000000 | tf_op jit(solution)/shard_map/centre/pallas_call | solution.py:267
  87.7 8.6 %edges.1 = bf16[16,32,1024]{2,1,0:T(8,128)(2,1)} custom-call(bf16[3,4,128,1024]{3,2,1,0:T(8,128)(2,1)S(1)} %bitcast.220, bf16[2,128,1024]{2,1,0:T(8,128)(2,1)S(1)} %get-tuple-element.25.l_ref, bf16[2,128,1024]{2,1,0:T(8,128)(2,1)S(1)} %get-tuple-element.26.r_ref, bf16[2,2,64,1024]{3,2,1,0:T(8,128)(2,1)S(1)} %collective-permute-done.4.cu_ref, ...), custom_call_target="tpu_custom_call" | custom-call | flops 500000000 | bytes 3000000 | tf_op jit(solution)/shard_map/edges/pallas_call | solution.py:365
  (43 shorter events, 0.4 us)
Async XLA Ops:
  0.6 16.5 %copy-start.1 = (bf16[3,8,1024]{2,1,0:T(8,128)(2,1)S(1)}, bf16[3,8,1024]{2,1,0:T(8,128)(2,1)}, u32[]{:S(2)}) copy-start(bf16[3,8,1024]{2,1,0:T(8,128)(2,1)} %reg_ref.9) | copy-start | bytes 147460
  3.0 52.4 %collective-permute-start.1 = (bf16[2,16,8,1024]{3,2,1,0:T(8,128)(2,1)}, bf16[2,16,8,1024]{3,2,1,0:T(8,128)(2,1)}, u32[]{:S(2)}, u32[]{:S(2)}) collective-permute-start(bf16[2,16,8,1024]{3,2,1,0:T(8,128)(2,1)} %get-tuple-element.44), channel_id=1, source_target_pairs={{1,0},{2,1},{3,2},{5,4},{6,5},{7,6},{9,8},{10,9},{11,10},{13,12},{... | collective-permute-start | bytes 1572872 | tf_op jit(solution)/shard_map/ppermute | solution.py:35
  4.2 51.1 %collective-permute-start = (bf16[2,16,8,1024]{3,2,1,0:T(8,128)(2,1)}, bf16[2,16,8,1024]{3,2,1,0:T(8,128)(2,1)}, u32[]{:S(2)}, u32[]{:S(2)}) collective-permute-start(bf16[2,16,8,1024]{3,2,1,0:T(8,128)(2,1)} %get-tuple-element.45), channel_id=1, source_target_pairs={{0,1},{1,2},{2,3},{4,5},{5,6},{6,7},{8,9},{9,10},{10,11},{12,13},{... | collective-permute-start | bytes 1572872 | tf_op jit(solution)/shard_map/ppermute | solution.py:35
  12.7 33.5 %collective-permute-start.3 = (bf16[2,8,32,1024]{3,2,1,0:T(8,128)(2,1)}, bf16[2,8,32,1024]{3,2,1,0:T(8,128)(2,1)}, u32[]{:S(2)}, u32[]{:S(2)}) collective-permute-start(bf16[2,8,32,1024]{3,2,1,0:T(8,128)(2,1)} %get-tuple-element.42), channel_id=1, source_target_pairs={{4,0},{8,4},{12,8},{16,12},{20,16},{24,20},{28,24},{5,1},{9,5},{13... | collective-permute-start | bytes 3145736 | tf_op jit(solution)/shard_map/ppermute | solution.py:35
  14.7 31.6 %collective-permute-start.2 = (bf16[2,8,32,1024]{3,2,1,0:T(8,128)(2,1)}, bf16[2,8,32,1024]{3,2,1,0:T(8,128)(2,1)}, u32[]{:S(2)}, u32[]{:S(2)}) collective-permute-start(bf16[2,8,32,1024]{3,2,1,0:T(8,128)(2,1)} %get-tuple-element.43), channel_id=1, source_target_pairs={{0,4},{4,8},{8,12},{12,16},{16,20},{20,24},{24,28},{1,5},{5,9},{9,... | collective-permute-start | bytes 3145736 | tf_op jit(solution)/shard_map/ppermute | solution.py:35
  19.8 3.0 %copy-start.3 = (f32[3,8,1024]{2,1,0:T(8,128)}, f32[3,8,1024]{2,1,0:T(8,128)S(1)}, u32[]{:S(2)}) copy-start(f32[3,8,1024]{2,1,0:T(8,128)S(1)} %get-tuple-element.35) | copy-start | bytes 294916
  19.8 28.2 %copy-start = (bf16[4,128,128]{2,1,0:T(8,128)(2,1)S(1)}, bf16[4,128,128]{2,1,0:T(8,128)(2,1)}, u32[]{:S(2)}) copy-start(bf16[4,128,128]{2,1,0:T(8,128)(2,1)} %constant.39.clone.qf_ref) | copy-start | bytes 393220
  19.8 2.2 %collective-permute-start.6 = (f32[3,8,1024]{2,1,0:T(8,128)S(1)}, f32[3,8,1024]{2,1,0:T(8,128)S(1)}, u32[]{:S(2)}, u32[]{:S(2)}) collective-permute-start(f32[3,8,1024]{2,1,0:T(8,128)S(1)} %get-tuple-element.35), channel_id=1, source_target_pairs={{0,4},{4,0},{8,12},{12,8},{16,20},{20,16},{24,28},{28,24},{1,5},{5... | collective-permute-start | bytes 294920 | tf_op jit(solution)/shard_map/ppermute | solution.py:173
  22.1 0.7 copy-start.6
  22.1 0.7 copy-start.5
  22.1 0.7 copy-start.9
  22.1 0.7 copy-start.8
  22.8 8.6 %collective-permute-start.7 = (f32[3,8,1024]{2,1,0:T(8,128)}, f32[3,8,1024]{2,1,0:T(8,128)}, u32[]{:S(2)}, u32[]{:S(2)}) collective-permute-start(f32[3,8,1024]{2,1,0:T(8,128)} %pad_maximum_fusion.2), channel_id=1, source_target_pairs={{0,8},{4,12},{8,0},{12,4},{16,24},{20,28},{24,16},{28,20},{1,9},{5... | collective-permute-start | bytes 294920 | tf_op jit(solution)/shard_map/ppermute | solution.py:173
  25.7 22.4 %copy-start.2 = (bf16[3,8,1024]{2,1,0:T(8,128)(2,1)S(1)}, bf16[3,8,1024]{2,1,0:T(8,128)(2,1)}, u32[]{:S(2)}) copy-start(bf16[3,8,1024]{2,1,0:T(8,128)(2,1)} %reg_ref.9) | copy-start | bytes 147460
  33.1 6.7 %collective-permute-start.8 = (f32[3,8,1024]{2,1,0:T(8,128)S(1)}, f32[3,8,1024]{2,1,0:T(8,128)S(1)}, u32[]{:S(2)}, u32[]{:S(2)}) collective-permute-start(f32[3,8,1024]{2,1,0:T(8,128)S(1)} %pad_maximum_fusion.3), channel_id=1, source_target_pairs={{0,16},{4,20},{8,24},{12,28},{16,0},{20,4},{24,8},{28,12},{1,17},{... | collective-permute-start | bytes 294920 | tf_op jit(solution)/shard_map/ppermute | solution.py:173
  39.8 4.8 %collective-permute-start.9 = (f32[3,8,1024]{2,1,0:T(8,128)S(1)}, f32[3,8,1024]{2,1,0:T(8,128)S(1)}, u32[]{:S(2)}, u32[]{:S(2)}) collective-permute-start(f32[3,8,1024]{2,1,0:T(8,128)S(1)} %pad_maximum_fusion.4), channel_id=1, source_target_pairs={{0,1},{1,0},{2,3},{3,2},{4,5},{5,4},{6,7},{7,6},{8,9},{9,8},{10,11... | collective-permute-start | bytes 294920 | tf_op jit(solution)/shard_map/ppermute | solution.py:173
  44.7 17.9 %collective-permute-start.10 = (f32[3,8,1024]{2,1,0:T(8,128)S(1)}, f32[3,8,1024]{2,1,0:T(8,128)S(1)}, u32[]{:S(2)}, u32[]{:S(2)}) collective-permute-start(f32[3,8,1024]{2,1,0:T(8,128)S(1)} %pad_maximum_fusion.5), channel_id=1, source_target_pairs={{0,2},{1,3},{2,0},{3,1},{4,6},{5,7},{6,4},{7,5},{8,10},{9,11},{10,... | collective-permute-start | bytes 294920 | tf_op jit(solution)/shard_map/ppermute | solution.py:173
  55.3 7.1 %copy-start.10 = (bf16[2,256,128]{2,1,0:T(8,128)(2,1)S(1)}, bf16[2,256,128]{2,1,0:T(8,128)(2,1)}, u32[]{:S(2)}) copy-start(bf16[2,256,128]{2,1,0:T(8,128)(2,1)} %constant.137) | copy-start | bytes 393220
  55.3 7.3 %copy-start.4 = (f32[3,8,1024]{2,1,0:T(8,128)S(1)}, f32[3,8,1024]{2,1,0:T(8,128)}, u32[]{:S(2)}) copy-start(f32[3,8,1024]{2,1,0:T(8,128)} %copy-done.3) | copy-start | bytes 294916
  55.3 7.3 %copy-start.7 = (f32[3,8,1024]{2,1,0:T(8,128)S(1)}, f32[3,8,1024]{2,1,0:T(8,128)}, u32[]{:S(2)}) copy-start(f32[3,8,1024]{2,1,0:T(8,128)} %copy-done.6) | copy-start | bytes 294916
  56.8 30.8 %collective-permute-start.4 = (bf16[2,2,64,1024]{3,2,1,0:T(8,128)(2,1)S(1)}, bf16[2,2,64,1024]{3,2,1,0:T(8,128)(2,1)S(1)}, u32[]{:S(2)}, u32[]{:S(2)}) collective-permute-start(bf16[2,2,64,1024]{3,2,1,0:T(8,128)(2,1)S(1)} %pad_maximum_fusion), channel_id=1, source_target_pairs={{0,4},{4,8},{8,12},{12,16},{16,20},{20,24},{24,28},{1,5},{5,9},{9,... | collective-permute-start | bytes 1572872 | tf_op jit(solution)/shard_map/ppermute | solution.py:35
  58.8 28.9 %collective-permute-start.5 = (bf16[2,2,64,1024]{3,2,1,0:T(8,128)(2,1)S(1)}, bf16[2,2,64,1024]{3,2,1,0:T(8,128)(2,1)S(1)}, u32[]{:S(2)}, u32[]{:S(2)}) collective-permute-start(bf16[2,2,64,1024]{3,2,1,0:T(8,128)(2,1)S(1)} %pad_maximum_fusion.1), channel_id=1, source_target_pairs={{4,0},{8,4},{12,8},{16,12},{20,16},{24,20},{28,24},{5,1},{9,5},{13... | collective-permute-start | bytes 1572872 | tf_op jit(solution)/shard_map/ppermute | solution.py:35

commit v5 on v4

--- a/solution.py
+++ b/solution.py
@@ -11,6 +11,8 @@
 
 HEADS = 16
 PARTS = 4
+TOGETHER_C = 2
+TOGETHER_E = 2
 RADIUS = 8
 FAR = -30000.0
 LEAST, MOST = 1e-20, 1e30
@@ -220,9 +222,10 @@
             s = s - high
         else:
             high = jnp.zeros((1, s.shape[1]), F32)
-        w = jnp.exp(s)
-        total = jnp.sum(w, axis=0, keepdims=True)
-        o = dot(stacked(2), w.astype(BF16), TN)
+        w = jnp.exp(s).astype(BF16)
+        total = jnp.sum(w.astype(F32), axis=0, keepdims=True)
+        yield total
+        o = dot(stacked(2), w, TN)
         st_ref[i, half, part, :d] = o[:, :d]
         st_ref[i, half, part, d : d + 8] = jnp.concatenate(
             [high[:, :d], total[:, :d], jnp.zeros((6, d), F32)], axis=0
@@ -230,32 +233,39 @@
         t = jnp.transpose(o[:, d:] / total[:, d:])
         t = jnp.where(low, t[:edge], t[edge:])
         in_ref[part, rows, lanes_out] = t.astype(BF16)
-        return total
-
-    run_guarded(unit, st_ref.shape[0], 4 * edge)
-
-
-def run_guarded(unit, count, lanes):
+
+    run_guarded(unit, st_ref.shape[0], 4 * edge, TOGETHER_C)
+
+
+def run_guarded(unit, count, lanes, together=1):
     units = [(half, part) for half in range(2) for part in range(2)]
+
+    def both(i, exact):
+        step = 1 if exact else together
+        running = [
+            unit(i * step + k, half, part, exact) for k in range(step) for half, part in units
+        ]
+        totals = [next(r) for r in running]
+        for r in running:
+            next(r, None)
+        return totals
 
     def fast(i, seen):
         least, most = seen
-        for half, part in units:
-            total = unit(i, half, part, False)
+        for total in both(i, False):
             least = jnp.where(total >= least, least, total)
             most = jnp.where(total <= most, most, total)
         return least, most
 
     one = jnp.ones((1, lanes), F32)
-    least, most = lax.fori_loop(0, count, fast, (one, one))
+    least, most = lax.fori_loop(0, count // together, fast, (one, one))
     fine = jnp.where((least > LEAST) & (most < MOST), 1.0, 0.0)
 
     @pl.when(jnp.min(fine) < 0.5)
     def _():
         @pl.loop(0, count)
         def _(i):
-            for half, part in units:
-                unit(i, half, part, True)
+            both(i, True)
 
 
 def centre(pg, up, down, registers, qf, kf, scale, first, pairs):
@@ -336,17 +346,17 @@
             new = jnp.maximum(high, jnp.max(s, axis=0, keepdims=True))
             fade = jnp.exp(high - new)
             acc, total, high = acc * fade, total * fade, new
-        w = jnp.exp(s - high)
-        total = total + jnp.sum(w, axis=0, keepdims=True)
-        acc = acc + dot(keys(1), w.astype(BF16), TN)
+        w = jnp.exp(s - high).astype(BF16)
+        total = total + jnp.sum(w.astype(F32), axis=0, keepdims=True)
+        yield total
+        acc = acc + dot(keys(1), w, TN)
         t = jnp.transpose(acc / total)
         t = jnp.where(low, t[:edge], t[edge:])
         rows_of = slice(half * RADIUS, (half + 1) * RADIUS)
         edge_ref[side, rows_of, :, lanes] = t.reshape(RADIUS, RADIUS, d).astype(BF16)
-        return total
 
     for n in range(parts):
-        run_guarded(functools.partial(unit_of, n), per, 2 * edge)
+        run_guarded(functools.partial(unit_of, n), per, 2 * edge, TOGETHER_E)
 
     copies = []
     for side in range(2):

time: 97.1 us -> 79.2 us (0.82)
  Pallas kernels: 43.9 us -> 26 us
    pallas_call x4, Pallas kernels: 29.6 us -> 16.9 us  [centre(): pl.pallas_call(functools.partial(centre_kernel, scale, first), in_specs=[...]
    pallas_call x1, Pallas kernels: 8.62 us -> 3.4 us  [edges(): pl.pallas_call(functools.partial(edge_kernel, scale, parts), in_specs=[VM...]
  transfers between devices with their start and end apart: 11 -> 11, of which waited for: 4 -> 4; matrix products, arithmetic and copies ran while one was open for 10% -> 13% of each run, Pallas kernels for 37% -> 29%
where the time goes in v5:
time: 79.2 us; the launch traced here: 78.6 us
  Pallas kernels  26 us (33%)
  starting transfers between devices  23.2 us (29%)
  waiting for transfers between devices  16 us (20%)
  local copies, waits for them, and re-layouts  6.89 us (9%)
  other arithmetic  5.33 us (7%)
  between operations  1.18 us (1%)
    pallas_call x4, Pallas kernels, centre(): pl.pallas_call(functools.partial(centre_kernel, scale, first), in_specs=[...  16.9 us
    ppermute x6, starting transfers between devices, shift(): lax.ppermute(x, axis, [(i, i + step) for i in range(n) if 0 <= i + step <...  16.5 us
    ppermute x5, waiting for transfers between devices, merge_over(): other = lax.ppermute(part, axis, [(i, i ^ step) for i in range(n)])  16 us
    ppermute x5, starting transfers between devices, merge_over(): other = lax.ppermute(part, axis, [(i, i ^ step) for i in range(n)])  6.72 us
    pallas_call x1, Pallas kernels, edges(): pl.pallas_call(functools.partial(edge_kernel, scale, parts), in_specs=[VM...  3.4 us
    slice x1, local copies, waits for them, and re-layouts, local(): down = shift(patches[1:3, :RADIUS], 'row', -1)  3.14 us
    pallas_call x2, Pallas kernels, stage(): pl.pallas_call(functools.partial(stage_kernel, copies_of), in_specs=[HBM,...  2.96 us
    pallas_call x1, Pallas kernels, prep(): pl.pallas_call(functools.partial(prep_kernel, scale), in_specs=[SMEM, VME...  2.72 us
  transfers between devices with their start and end apart: 11, of which 4 were waited for; matrix products, arithmetic and copies ran while one was open for 13% of the time, Pallas kernels for 29%

profile of v5, /device:TPU:16, one launch (start us, length us, event | category | flops | bytes accessed | tf_op | source)
XLA Modules:
  0.0 78.6 jit_solution(17896644001562292035)
XLA Ops:
  0.6 2.3 %fusion.38 = (bf16[2,16,8,1024]{3,2,1,0:T(8,128)(2,1)}, bf16[2,16,8,1024]{3,2,1,0:T(8,128)(2,1)}) fusion(bf16[3,16,32,1024]{3,2,1,0:T(8,128)(2,1)} %p_ref.1), kind=kLoop, calls=%fused_computation.96 | loop fusion | bytes 2097152 | tf_op jit(solution)/shard_map/slice | solution.py:405
  3.0 1.3 %collective-permute-start.1 = (bf16[2,16,8,1024]{3,2,1,0:T(8,128)(2,1)}, bf16[2,16,8,1024]{3,2,1,0:T(8,128)(2,1)}, u32[]{:S(2)}, u32[]{:S(2)}) collective-permute-start(bf16[2,16,8,1024]{3,2,1,0:T(8,128)(2,1)} %get-tuple-element.44), channel_id=1, source_target_pairs={{1,0},{2,1},{3,2},{5,4},{6,5},{7,6},{9,8},{10,9},{11,10},{13,12},{... | collective-permute-start | bytes 1572872 | tf_op jit(solution)/shard_map/ppermute | solution.py:37
  4.2 5.3 %collective-permute-start = (bf16[2,16,8,1024]{3,2,1,0:T(8,128)(2,1)}, bf16[2,16,8,1024]{3,2,1,0:T(8,128)(2,1)}, u32[]{:S(2)}, u32[]{:S(2)}) collective-permute-start(bf16[2,16,8,1024]{3,2,1,0:T(8,128)(2,1)} %get-tuple-element.45), channel_id=1, source_target_pairs={{0,1},{1,2},{2,3},{4,5},{5,6},{6,7},{8,9},{9,10},{10,11},{12,13},{... | collective-permute-start | bytes 1572872 | tf_op jit(solution)/shard_map/ppermute | solution.py:37
  9.6 3.1 %fusion.37 = (bf16[2,8,32,1024]{3,2,1,0:T(8,128)(2,1)}, bf16[2,8,32,1024]{3,2,1,0:T(8,128)(2,1)}) fusion(bf16[3,16,32,1024]{3,2,1,0:T(8,128)(2,1)} %p_ref.1), kind=kLoop, calls=%fused_computation.95 | loop fusion | bytes 4194304 | tf_op jit(solution)/shard_map/slice | solution.py:407
  12.7 1.9 %collective-permute-start.3 = (bf16[2,8,32,1024]{3,2,1,0:T(8,128)(2,1)}, bf16[2,8,32,1024]{3,2,1,0:T(8,128)(2,1)}, u32[]{:S(2)}, u32[]{:S(2)}) collective-permute-start(bf16[2,8,32,1024]{3,2,1,0:T(8,128)(2,1)} %get-tuple-element.42), channel_id=1, source_target_pairs={{4,0},{8,4},{12,8},{16,12},{20,16},{24,20},{28,24},{5,1},{9,5},{13... | collective-permute-start | bytes 3145736 | tf_op jit(solution)/shard_map/ppermute | solution.py:37
  14.7 2.4 %collective-permute-start.2 = (bf16[2,8,32,1024]{3,2,1,0:T(8,128)(2,1)}, bf16[2,8,32,1024]{3,2,1,0:T(8,128)(2,1)}, u32[]{:S(2)}, u32[]{:S(2)}) collective-permute-start(bf16[2,8,32,1024]{3,2,1,0:T(8,128)(2,1)} %get-tuple-element.43), channel_id=1, source_target_pairs={{0,4},{4,8},{8,12},{12,16},{16,20},{20,24},{24,28},{1,5},{5,9},{9,... | collective-permute-start | bytes 3145736 | tf_op jit(solution)/shard_map/ppermute | solution.py:37
  17.1 2.7 %prep.1 = (bf16[3,4,16,8,1024]{4,3,2,1,0:T(8,128)(2,1)S(1)}, f32[3,8,1024]{2,1,0:T(8,128)S(1)}) custom-call(f32[1]{0:T(128)} %bitcast.flag_ref, bf16[3,8,1024]{2,1,0:T(8,128)(2,1)S(1)} %copy-done.1, bf16[3,16,32,1024]{3,2,1,0:T(8,128)(2,1)} %p_ref.1), custom_call_target="tpu_custom_call" | custom-call | flops 300000000 | bytes 4000000 | tf_op jit(solution)/shard_map/prep/pallas_call | solution.py:144
  19.8 1.3 %collective-permute-start.6 = (f32[3,8,1024]{2,1,0:T(8,128)S(1)}, f32[3,8,1024]{2,1,0:T(8,128)S(1)}, u32[]{:S(2)}, u32[]{:S(2)}) collective-permute-start(f32[3,8,1024]{2,1,0:T(8,128)S(1)} %get-tuple-element.35), channel_id=1, source_target_pairs={{0,4},{4,0},{8,12},{12,8},{16,20},{20,16},{24,28},{28,24},{1,5},{5... | collective-permute-start | bytes 294920 | tf_op jit(solution)/shard_map/ppermute | solution.py:175
  21.1 0.9 %collective-permute-done.6 = f32[3,8,1024]{2,1,0:T(8,128)S(1)} collective-permute-done((f32[3,8,1024]{2,1,0:T(8,128)S(1)}, f32[3,8,1024]{2,1,0:T(8,128)S(1)}, u32[]{:S(2)}, u32[]{:S(2)}) %collective-permute-start.6) | collective-permute-done | bytes 98336 | tf_op jit(solution)/shard_map/ppermute | solution.py:175
  22.1 0.6 pad_maximum_fusion.2
  22.8 1.8 %collective-permute-start.7 = (f32[3,8,1024]{2,1,0:T(8,128)}, f32[3,8,1024]{2,1,0:T(8,128)}, u32[]{:S(2)}, u32[]{:S(2)}) collective-permute-start(f32[3,8,1024]{2,1,0:T(8,128)} %pad_maximum_fusion.2), channel_id=1, source_target_pairs={{0,8},{4,12},{8,0},{12,4},{16,24},{20,28},{24,16},{28,20},{1,9},{5... | collective-permute-start | bytes 294920 | tf_op jit(solution)/shard_map/ppermute | solution.py:175
  24.6 1.1 %select_convert_fusion.kf_ref = bf16[4,256,128]{2,1,0:T(8,128)(2,1)S(1)} fusion(bf16[4,256,128]{2,1,0:T(8,128)(2,1)} %constant.136, pred[128]{0:T(512)(128)(4,1)S(1)} %iota_compare_fusion, pred[256]{0:T(512)(128)(4,1)S(1)} %and_or_fusion.1), kind=kLoop, calls=%fused_computation.2 | loop fusion | flops 262144 | bytes 524672 | tf_op jit(solution)/shard_map/convert_element_type | solution.py:55
  25.7 5.7 %collective-permute-done.7 = f32[3,8,1024]{2,1,0:T(8,128)} collective-permute-done((f32[3,8,1024]{2,1,0:T(8,128)}, f32[3,8,1024]{2,1,0:T(8,128)}, u32[]{:S(2)}, u32[]{:S(2)}) %collective-permute-start.7) | collective-permute-done | bytes 98336 | tf_op jit(solution)/shard_map/ppermute | solution.py:175
  31.4 0.8 %multiply_add_fusion.5 = (f32[1,8,1024]{2,1,0:T(8,128)S(1)}, f32[1,8,1024]{2,1,0:T(8,128)S(1)}) fusion(f32[1,8,1024]{2,1,0:T(8,128)} %copy-done.9, f32[3,8,1024]{2,1,0:T(8,128)} %collective-permute-done.7, f32[1,8,1024]{2,1,0:T(8,128)} %copy-done.5), kind=kLoop, calls=%fused_computation.79 | loop fusion | flops 49152 | bytes 196608 | tf_op jit(solution)/shard_map/add | solution.py:165
  32.2 0.8 %multiply_add_fusion.4 = f32[1,8,1024]{2,1,0:T(8,128)S(1)} fusion(f32[1,8,1024]{2,1,0:T(8,128)} %copy-done.8, f32[3,8,1024]{2,1,0:T(8,128)} %collective-permute-done.7, f32[1,8,1024]{2,1,0:T(8,128)} %copy-done.5, f32[1,8,1024]{2,1,0:T(8,128)S(1)} %get-tuple-element.39), kind=kLoop, calls=%fused_computation.78 | loop fusion | flops 40960 | bytes 196608 | tf_op jit(solution)/shard_map/add | solution.py:165
  33.1 0.4 collective-permute-start.8
  33.5 6.3 %collective-permute-done.8 = f32[3,8,1024]{2,1,0:T(8,128)S(1)} collective-permute-done((f32[3,8,1024]{2,1,0:T(8,128)S(1)}, f32[3,8,1024]{2,1,0:T(8,128)S(1)}, u32[]{:S(2)}, u32[]{:S(2)}) %collective-permute-start.8) | collective-permute-done | bytes 98336 | tf_op jit(solution)/shard_map/ppermute | solution.py:175
  39.8 1.7 %collective-permute-start.9 = (f32[3,8,1024]{2,1,0:T(8,128)S(1)}, f32[3,8,1024]{2,1,0:T(8,128)S(1)}, u32[]{:S(2)}, u32[]{:S(2)}) collective-permute-start(f32[3,8,1024]{2,1,0:T(8,128)S(1)} %pad_maximum_fusion.4), channel_id=1, source_target_pairs={{0,1},{1,0},{2,3},{3,2},{4,5},{5,4},{6,7},{7,6},{8,9},{9,8},{10,11... | collective-permute-start | bytes 294920 | tf_op jit(solution)/shard_map/ppermute | solution.py:175
  41.6 3.0 %collective-permute-done.9 = f32[3,8,1024]{2,1,0:T(8,128)S(1)} collective-permute-done((f32[3,8,1024]{2,1,0:T(8,128)S(1)}, f32[3,8,1024]{2,1,0:T(8,128)S(1)}, u32[]{:S(2)}, u32[]{:S(2)}) %collective-permute-start.9) | collective-permute-done | bytes 98336 | tf_op jit(solution)/shard_map/ppermute | solution.py:175
  44.7 1.6 %collective-permute-start.10 = (f32[3,8,1024]{2,1,0:T(8,128)S(1)}, f32[3,8,1024]{2,1,0:T(8,128)S(1)}, u32[]{:S(2)}, u32[]{:S(2)}) collective-permute-start(f32[3,8,1024]{2,1,0:T(8,128)S(1)} %pad_maximum_fusion.5), channel_id=1, source_target_pairs={{0,2},{1,3},{2,0},{3,1},{4,6},{5,7},{6,4},{7,5},{8,10},{9,11},{10,... | collective-permute-start | bytes 294920 | tf_op jit(solution)/shard_map/ppermute | solution.py:175
  46.3 1.7 %shard_map.68 = (bf16[2,4,8,8,1024]{4,3,2,1,0:T(8,128)(2,1)S(1)}, bf16[2,4,8,8,1024]{4,3,2,1,0:T(8,128)(2,1)S(1)}) custom-call(bf16[2,8,32,1024]{3,2,1,0:T(8,128)(2,1)} %collective-permute-done.2.a_ref, bf16[2,8,32,1024]{3,2,1,0:T(8,128)(2,1)} %collective-permute-done.3.b_ref), custom_call_target="tpu_custom_call" | custom-call | flops 1000000 | bytes 4000000 | tf_op jit(solution)/shard_map/pallas_call | solution.py:84
  48.0 4.1 %centre.4 = (bf16[2,128,256]{2,1,0:T(8,128)(2,1)S(1)}, f32[2,2,2,136,128]{4,3,2,1,0:T(8,128)S(1)}) custom-call(bf16[3,4,128,1024]{3,2,1,0:T(8,128)(2,1)S(1)} %bitcast.216, bf16[2,4,64,1024]{3,2,1,0:T(8,128)(2,1)S(1)} %bitcast.221, bf16[2,4,64,1024]{3,2,1,0:T(8,128)(2,1)S(1)} %bitcast.225, bf16[3,8,1024]{2,1,0:T(8,128)(2,1)S(1)} %copy-done.2, ...), custom_call_target="tpu_custom_call" | custom-call | flops 931135488 | bytes 4000000 | tf_op jit(solution)/shard_map/centre/pallas_call | solution.py:277
  52.2 1.4 %slice_bitcast_fusion = (bf16[1,2,64,1024]{3,2,1,0:T(8,128)(2,1)S(1)}, bf16[1,2,64,1024]{3,2,1,0:T(8,128)(2,1)S(1)}, bf16[1,2,64,1024]{3,2,1,0:T(8,128)(2,1)S(1)}, bf16[1,2,64,1024]{3,2,1,0:T(8,128)(2,1)S(1)}) fusion(bf16[2,128,1024]{2,1,0:T(8,128)(2,1)} %bitcast.3.b_ref, bf16[2,128,1024]{2,1,0:T(8,128)(2,1)} %bitcast.2.a_ref), kind=kLoop, calls=%fused_computation.4 | loop fusion | bytes 2097152 | tf_op jit(solution)/shard_map/stack | solution.py:445
  53.7 1.9 %collective-permute-start.4 = (bf16[2,2,64,1024]{3,2,1,0:T(8,128)(2,1)S(1)}, bf16[2,2,64,1024]{3,2,1,0:T(8,128)(2,1)S(1)}, u32[]{:S(2)}, u32[]{:S(2)}) collective-permute-start(bf16[2,2,64,1024]{3,2,1,0:T(8,128)(2,1)S(1)} %pad_maximum_fusion), channel_id=1, source_target_pairs={{0,4},{4,8},{8,12},{12,16},{16,20},{20,24},{24,28},{1,5},{5,9},{9,... | collective-permute-start | bytes 1572872 | tf_op jit(solution)/shard_map/ppermute | solution.py:37
  55.7 3.6 %collective-permute-start.5 = (bf16[2,2,64,1024]{3,2,1,0:T(8,128)(2,1)S(1)}, bf16[2,2,64,1024]{3,2,1,0:T(8,128)(2,1)S(1)}, u32[]{:S(2)}, u32[]{:S(2)}) collective-permute-start(bf16[2,2,64,1024]{3,2,1,0:T(8,128)(2,1)S(1)} %pad_maximum_fusion.1), channel_id=1, source_target_pairs={{4,0},{8,4},{12,8},{16,12},{20,16},{24,20},{28,24},{5,1},{9,5},{13... | collective-permute-start | bytes 1572872 | tf_op jit(solution)/shard_map/ppermute | solution.py:37
  59.3 0.1 select_convert_fusion.1.kf_ref
  59.5 1.5 %fusion.36 = bf16[8,1024]{1,0:T(8,128)(2,1)} fusion(f32[3,8,1024]{2,1,0:T(8,128)S(1)} %collective-permute-done.10, f32[3,8,1024]{2,1,0:T(8,128)S(1)} %collective-permute-done.9, f32[3,8,1024]{2,1,0:T(8,128)S(1)} %collective-permute-done.8, f32[3,8,1024]{2,1,0:T(8,128)} %collective-permute-done.7, f32[3,8,1024]{2,1,0:T(8,128)S(1)} %copy-done.7, ...), kind=kLoop, calls=%fused_computation.86 | loop fusion | flops 385024 | bytes 606208 | tf_op jit(solution)/shard_map/convert_element_type | solution.py:417
  61.0 1.2 %shard_map.69 = (bf16[2,128,1024]{2,1,0:T(8,128)(2,1)S(1)}, bf16[2,128,1024]{2,1,0:T(8,128)(2,1)S(1)}) custom-call(bf16[2,128,1024]{2,1,0:T(8,128)(2,1)} %bitcast.2.a_ref, bf16[2,128,1024]{2,1,0:T(8,128)(2,1)} %bitcast.3.b_ref), custom_call_target="tpu_custom_call" | custom-call | flops 1000000 | bytes 4000000 | tf_op jit(solution)/shard_map/pallas_call | solution.py:84
  62.2 4.2 %centre.7 = (bf16[2,128,256]{2,1,0:T(8,128)(2,1)S(1)}, f32[2,2,2,136,128]{4,3,2,1,0:T(8,128)S(1)}) custom-call(bf16[3,4,128,1024]{3,2,1,0:T(8,128)(2,1)S(1)} %bitcast.217, bf16[2,4,64,1024]{3,2,1,0:T(8,128)(2,1)S(1)} %bitcast.222, bf16[2,4,64,1024]{3,2,1,0:T(8,128)(2,1)S(1)} %bitcast.226, bf16[3,8,1024]{2,1,0:T(8,128)(2,1)S(1)} %copy-done.2, ...), custom_call_target="tpu_custom_call" | custom-call | flops 931135488 | bytes 4000000 | tf_op jit(solution)/shard_map/centre/pallas_call | solution.py:277
  66.4 4.4 %centre.6 = (bf16[2,128,256]{2,1,0:T(8,128)(2,1)S(1)}, f32[2,2,2,136,128]{4,3,2,1,0:T(8,128)S(1)}) custom-call(bf16[3,4,128,1024]{3,2,1,0:T(8,128)(2,1)S(1)} %bitcast.218, bf16[2,4,64,1024]{3,2,1,0:T(8,128)(2,1)S(1)} %bitcast.223, bf16[2,4,64,1024]{3,2,1,0:T(8,128)(2,1)S(1)} %bitcast.227, bf16[3,8,1024]{2,1,0:T(8,128)(2,1)S(1)} %copy-done.2, ...), custom_call_target="tpu_custom_call" | custom-call | flops 931135488 | bytes 4000000 | tf_op jit(solution)/shard_map/centre/pallas_call | solution.py:277
  70.8 4.2 %centre.5 = (bf16[2,128,256]{2,1,0:T(8,128)(2,1)S(1)}, f32[2,2,2,136,128]{4,3,2,1,0:T(8,128)S(1)}) custom-call(bf16[3,4,128,1024]{3,2,1,0:T(8,128)(2,1)S(1)} %bitcast.219, bf16[2,4,64,1024]{3,2,1,0:T(8,128)(2,1)S(1)} %bitcast.224, bf16[2,4,64,1024]{3,2,1,0:T(8,128)(2,1)S(1)} %bitcast.228, bf16[3,8,1024]{2,1,0:T(8,128)(2,1)S(1)} %copy-done.2, ...), custom_call_target="tpu_custom_call" | custom-call | flops 931135488 | bytes 4000000 | tf_op jit(solution)/shard_map/centre/pallas_call | solution.py:277
  75.0 3.4 %edges.1 = bf16[16,32,1024]{2,1,0:T(8,128)(2,1)} custom-call(bf16[3,4,128,1024]{3,2,1,0:T(8,128)(2,1)S(1)} %bitcast.220, bf16[2,128,1024]{2,1,0:T(8,128)(2,1)S(1)} %get-tuple-element.25.l_ref, bf16[2,128,1024]{2,1,0:T(8,128)(2,1)S(1)} %get-tuple-element.26.r_ref, bf16[2,2,64,1024]{3,2,1,0:T(8,128)(2,1)S(1)} %collective-permute-done.4.cu_ref, ...), custom_call_target="tpu_custom_call" | custom-call | flops 500000000 | bytes 3000000 | tf_op jit(solution)/shard_map/edges/pallas_call | solution.py:375
  (43 shorter events, 0.4 us)
Async XLA Ops:
  0.6 16.5 %copy-start.1 = (bf16[3,8,1024]{2,1,0:T(8,128)(2,1)S(1)}, bf16[3,8,1024]{2,1,0:T(8,128)(2,1)}, u32[]{:S(2)}) copy-start(bf16[3,8,1024]{2,1,0:T(8,128)(2,1)} %reg_ref.9) | copy-start | bytes 147460
  3.0 49.3 %collective-permute-start.1 = (bf16[2,16,8,1024]{3,2,1,0:T(8,128)(2,1)}, bf16[2,16,8,1024]{3,2,1,0:T(8,128)(2,1)}, u32[]{:S(2)}, u32[]{:S(2)}) collective-permute-start(bf16[2,16,8,1024]{3,2,1,0:T(8,128)(2,1)} %get-tuple-element.44), channel_id=1, source_target_pairs={{1,0},{2,1},{3,2},{5,4},{6,5},{7,6},{9,8},{10,9},{11,10},{13,12},{... | collective-permute-start | bytes 1572872 | tf_op jit(solution)/shard_map/ppermute | solution.py:37
  4.2 48.0 %collective-permute-start = (bf16[2,16,8,1024]{3,2,1,0:T(8,128)(2,1)}, bf16[2,16,8,1024]{3,2,1,0:T(8,128)(2,1)}, u32[]{:S(2)}, u32[]{:S(2)}) collective-permute-start(bf16[2,16,8,1024]{3,2,1,0:T(8,128)(2,1)} %get-tuple-element.45), channel_id=1, source_target_pairs={{0,1},{1,2},{2,3},{4,5},{5,6},{6,7},{8,9},{9,10},{10,11},{12,13},{... | collective-permute-start | bytes 1572872 | tf_op jit(solution)/shard_map/ppermute | solution.py:37
  12.7 33.5 %collective-permute-start.3 = (bf16[2,8,32,1024]{3,2,1,0:T(8,128)(2,1)}, bf16[2,8,32,1024]{3,2,1,0:T(8,128)(2,1)}, u32[]{:S(2)}, u32[]{:S(2)}) collective-permute-start(bf16[2,8,32,1024]{3,2,1,0:T(8,128)(2,1)} %get-tuple-element.42), channel_id=1, source_target_pairs={{4,0},{8,4},{12,8},{16,12},{20,16},{24,20},{28,24},{5,1},{9,5},{13... | collective-permute-start | bytes 3145736 | tf_op jit(solution)/shard_map/ppermute | solution.py:37
  14.7 31.6 %collective-permute-start.2 = (bf16[2,8,32,1024]{3,2,1,0:T(8,128)(2,1)}, bf16[2,8,32,1024]{3,2,1,0:T(8,128)(2,1)}, u32[]{:S(2)}, u32[]{:S(2)}) collective-permute-start(bf16[2,8,32,1024]{3,2,1,0:T(8,128)(2,1)} %get-tuple-element.43), channel_id=1, source_target_pairs={{0,4},{4,8},{8,12},{12,16},{16,20},{20,24},{24,28},{1,5},{5,9},{9,... | collective-permute-start | bytes 3145736 | tf_op jit(solution)/shard_map/ppermute | solution.py:37
  19.8 3.0 %copy-start.3 = (f32[3,8,1024]{2,1,0:T(8,128)}, f32[3,8,1024]{2,1,0:T(8,128)S(1)}, u32[]{:S(2)}) copy-start(f32[3,8,1024]{2,1,0:T(8,128)S(1)} %get-tuple-element.35) | copy-start | bytes 294916
  19.8 28.2 %copy-start = (bf16[4,128,128]{2,1,0:T(8,128)(2,1)S(1)}, bf16[4,128,128]{2,1,0:T(8,128)(2,1)}, u32[]{:S(2)}) copy-start(bf16[4,128,128]{2,1,0:T(8,128)(2,1)} %constant.39.clone.qf_ref) | copy-start | bytes 393220
  19.8 2.2 %collective-permute-start.6 = (f32[3,8,1024]{2,1,0:T(8,128)S(1)}, f32[3,8,1024]{2,1,0:T(8,128)S(1)}, u32[]{:S(2)}, u32[]{:S(2)}) collective-permute-start(f32[3,8,1024]{2,1,0:T(8,128)S(1)} %get-tuple-element.35), channel_id=1, source_target_pairs={{0,4},{4,0},{8,12},{12,8},{16,20},{20,16},{24,28},{28,24},{1,5},{5... | collective-permute-start | bytes 294920 | tf_op jit(solution)/shard_map/ppermute | solution.py:175
  22.1 0.7 copy-start.6
  22.1 0.7 copy-start.5
  22.1 0.7 copy-start.9
  22.1 0.7 copy-start.8
  22.8 8.6 %collective-permute-start.7 = (f32[3,8,1024]{2,1,0:T(8,128)}, f32[3,8,1024]{2,1,0:T(8,128)}, u32[]{:S(2)}, u32[]{:S(2)}) collective-permute-start(f32[3,8,1024]{2,1,0:T(8,128)} %pad_maximum_fusion.2), channel_id=1, source_target_pairs={{0,8},{4,12},{8,0},{12,4},{16,24},{20,28},{24,16},{28,20},{1,9},{5... | collective-permute-start | bytes 294920 | tf_op jit(solution)/shard_map/ppermute | solution.py:175
  25.7 22.4 %copy-start.2 = (bf16[3,8,1024]{2,1,0:T(8,128)(2,1)S(1)}, bf16[3,8,1024]{2,1,0:T(8,128)(2,1)}, u32[]{:S(2)}) copy-start(bf16[3,8,1024]{2,1,0:T(8,128)(2,1)} %reg_ref.9) | copy-start | bytes 147460
  33.1 6.7 %collective-permute-start.8 = (f32[3,8,1024]{2,1,0:T(8,128)S(1)}, f32[3,8,1024]{2,1,0:T(8,128)S(1)}, u32[]{:S(2)}, u32[]{:S(2)}) collective-permute-start(f32[3,8,1024]{2,1,0:T(8,128)S(1)} %pad_maximum_fusion.3), channel_id=1, source_target_pairs={{0,16},{4,20},{8,24},{12,28},{16,0},{20,4},{24,8},{28,12},{1,17},{... | collective-permute-start | bytes 294920 | tf_op jit(solution)/shard_map/ppermute | solution.py:175
  39.8 4.8 %collective-permute-start.9 = (f32[3,8,1024]{2,1,0:T(8,128)S(1)}, f32[3,8,1024]{2,1,0:T(8,128)S(1)}, u32[]{:S(2)}, u32[]{:S(2)}) collective-permute-start(f32[3,8,1024]{2,1,0:T(8,128)S(1)} %pad_maximum_fusion.4), channel_id=1, source_target_pairs={{0,1},{1,0},{2,3},{3,2},{4,5},{5,4},{6,7},{7,6},{8,9},{9,8},{10,11... | collective-permute-start | bytes 294920 | tf_op jit(solution)/shard_map/ppermute | solution.py:175
  44.7 14.8 %collective-permute-start.10 = (f32[3,8,1024]{2,1,0:T(8,128)S(1)}, f32[3,8,1024]{2,1,0:T(8,128)S(1)}, u32[]{:S(2)}, u32[]{:S(2)}) collective-permute-start(f32[3,8,1024]{2,1,0:T(8,128)S(1)} %pad_maximum_fusion.5), channel_id=1, source_target_pairs={{0,2},{1,3},{2,0},{3,1},{4,6},{5,7},{6,4},{7,5},{8,10},{9,11},{10,... | collective-permute-start | bytes 294920 | tf_op jit(solution)/shard_map/ppermute | solution.py:175
  52.2 7.1 %copy-start.10 = (bf16[2,256,128]{2,1,0:T(8,128)(2,1)S(1)}, bf16[2,256,128]{2,1,0:T(8,128)(2,1)}, u32[]{:S(2)}) copy-start(bf16[2,256,128]{2,1,0:T(8,128)(2,1)} %constant.137) | copy-start | bytes 393220
  52.2 7.3 %copy-start.4 = (f32[3,8,1024]{2,1,0:T(8,128)S(1)}, f32[3,8,1024]{2,1,0:T(8,128)}, u32[]{:S(2)}) copy-start(f32[3,8,1024]{2,1,0:T(8,128)} %copy-done.3) | copy-start | bytes 294916
  52.2 7.3 %copy-start.7 = (f32[3,8,1024]{2,1,0:T(8,128)S(1)}, f32[3,8,1024]{2,1,0:T(8,128)}, u32[]{:S(2)}) copy-start(f32[3,8,1024]{2,1,0:T(8,128)} %copy-done.6) | copy-start | bytes 294916
  53.7 21.3 %collective-permute-start.4 = (bf16[2,2,64,1024]{3,2,1,0:T(8,128)(2,1)S(1)}, bf16[2,2,64,1024]{3,2,1,0:T(8,128)(2,1)S(1)}, u32[]{:S(2)}, u32[]{:S(2)}) collective-permute-start(bf16[2,2,64,1024]{3,2,1,0:T(8,128)(2,1)S(1)} %pad_maximum_fusion), channel_id=1, source_target_pairs={{0,4},{4,8},{8,12},{12,16},{16,20},{20,24},{24,28},{1,5},{5,9},{9,... | collective-permute-start | bytes 1572872 | tf_op jit(solution)/shard_map/ppermute | solution.py:37
  55.7 19.3 %collective-permute-start.5 = (bf16[2,2,64,1024]{3,2,1,0:T(8,128)(2,1)S(1)}, bf16[2,2,64,1024]{3,2,1,0:T(8,128)(2,1)S(1)}, u32[]{:S(2)}, u32[]{:S(2)}) collective-permute-start(bf16[2,2,64,1024]{3,2,1,0:T(8,128)(2,1)S(1)} %pad_maximum_fusion.1), channel_id=1, source_target_pairs={{4,0},{8,4},{12,8},{16,12},{20,16},{24,20},{28,24},{5,1},{9,5},{13... | collective-permute-start | bytes 1572872 | tf_op jit(solution)/shard_map/ppermute | solution.py:37
